TPU v7x, 512 devices: a whole 4x8x8 slice. The times are simulated.
512 devices in a mesh: dp: 32 (over x, z), heads: 16 (over y, core).
Axes of the slice: x: 4, y: 8, z: 8, core: 2. Of those that a mesh axis runs over, the one named last changes fastest.
Arguments:
- queries: bfloat16 [8, 8192, 4096], P(None, ('dp', 'heads')), may hold values from -6 to 6
- keys: bfloat16 [8, 8192, 2048], P(None, ('dp', 'heads')), may hold values from -6 to 6
- values: bfloat16 [8, 8192, 2048], P(None, ('dp', 'heads')), may hold values from -6 to 6
- lengths: int32 [8, 32], replicated, may hold values from 1 to 1024, 8192 in all within a row
Outputs:
- attended: bfloat16 [8, 8192, 4096], P(None, ('dp', 'heads'))
- log_norm: float32 [32, 8, 8192], P('heads', None, 'dp')
Inputs may be any that keep to these rules, and one draw needn't show every extreme that they name: In each row the 32 lengths sum to 8192, and the longest is exactly 1024.
All inputs are finite; a program needn't handle non-finite values.
Results may differ from a plain program's by a relative error of at most 0.0034.
Values may be sent and summed in bfloat16 or wider, within the bound.
No kernel may reach another device: no remote copies, remote signals or barrier semaphores. Data moves between devices by JAX's collectives and lax.ppermute only.
A program may use at most 64 MiB of HBM per device.

v0:
```python
import jax
import jax.numpy as jnp
from jax import lax
from jax.sharding import Mesh
from jax.sharding import PartitionSpec as P

HEAD_SIZE = 128
HEADS = ("heads_0", "heads_1")
DP_HEADS = ("dp", "heads_0", "heads_1")


def in_blocks(value, dim, devices):
    before, after = (value.shape[:dim], value.shape[dim + 1 :])
    return jnp.moveaxis(value.reshape(*before, devices, -1, *after), dim, 0)


def laid_out(parts, dim):
    shape = list(parts.shape[1:])
    shape[dim] *= parts.shape[0]
    return jnp.moveaxis(parts, 0, dim).reshape(shape)


def turned_blocks(parts, axes, order):
    inside = parts.shape[1:]
    out = parts.reshape(*(lax.axis_size(a) for a in axes), *inside)
    for k in order:
        out = lax.all_to_all(out, axes[k], k, k, tiled=True)
    return out.reshape(-1, *inside)


def two_step_exchange(value, groups, order, split_dim, concat_dim):
    devices = lax.axis_size(groups[0]) * lax.axis_size(groups[1])
    parts = in_blocks(value, split_dim, devices)
    return laid_out(turned_blocks(parts, groups, order), concat_dim)


def from_behind(value, axis, steps):
    count = lax.axis_size(axis)
    leading, last = (max(0, -steps), min(count, count - steps))
    return lax.ppermute(value, axis, [(source, source + steps) for source in range(leading, last)])


def doc_numbers(doc_ends, positions):
    return jnp.sum((doc_ends[:, None, :] <= positions[None, :, None]).astype(jnp.int32), axis=-1)


def per_device(queries, keys, values, lengths):
    local_q, local_k, local_v = (
        two_step_exchange(queries, ("heads_0", "heads_1"), (1, 0), 2, 1),
        two_step_exchange(keys, ("heads_0", "heads_1"), (1, 0), 2, 1),
        two_step_exchange(values, ("heads_0", "heads_1"), (1, 0), 2, 1),
    )
    row_count, tok_row, q_width = local_q.shape
    kv_heads = local_k.shape[2] // HEAD_SIZE
    per_group = q_width // (kv_heads * HEAD_SIZE)
    shards = lax.axis_size("dp")
    reach_blocks = shards // 8
    dp_index = lax.axis_index("dp")
    doc_ends = jnp.cumsum(lengths, axis=1)
    query_pos = dp_index * tok_row + jnp.arange(tok_row, dtype=jnp.int32)
    query_doc = doc_numbers(doc_ends, query_pos)
    doc_starts = jnp.max(
        jnp.where(doc_ends[:, None, :] <= query_pos[None, :, None], doc_ends[:, None, :], 0),
        axis=-1,
    )
    lowest = jnp.min(doc_starts)
    query_last = dp_index * tok_row + tok_row - 1
    query_heads = local_q.reshape(row_count, tok_row, kv_heads, per_group, HEAD_SIZE)
    score_scale = HEAD_SIZE ** (-0.5)

    def attend(state_now, key_block, value_block, anchor):
        run_max, run_sum, run_acc = state_now
        span_keys = key_block.shape[1]
        key_pos = anchor + jnp.arange(span_keys, dtype=jnp.int32)
        key_doc = doc_numbers(doc_ends, key_pos)
        visible = (
            (key_doc[:, None, :] == query_doc[:, :, None])
            & (key_pos[None, None, :] <= query_pos[None, :, None])
            & (key_pos[None, None, :] >= 0)
        )
        key_heads = key_block.reshape(row_count, span_keys, kv_heads, HEAD_SIZE)
        value_heads = value_block.reshape(row_count, span_keys, kv_heads, HEAD_SIZE)
        scores = (
            jnp.einsum(
                "rtkgd,rskd->kgrts", query_heads, key_heads, preferred_element_type=jnp.float32
            )
            * score_scale
        )
        masked = jnp.where(visible[None, None], scores, -1e30)
        new_max = jnp.maximum(run_max, jnp.max(masked, axis=-1))
        weights = jnp.where(visible[None, None], jnp.exp(masked - new_max[..., None]), 0.0)
        shrink = jnp.exp(run_max - new_max)
        run_sum = run_sum * shrink + jnp.sum(weights, axis=-1)
        partial_value = jnp.einsum(
            "kgrts,rskd->rtkgd",
            weights.astype(jnp.bfloat16),
            value_heads,
            preferred_element_type=jnp.float32,
        )
        run_acc = run_acc * jnp.transpose(shrink, (2, 3, 0, 1))[..., None] + partial_value
        return (new_max, run_sum, run_acc)

    def visit(state_now, key_block, value_block, anchor):
        key_end = anchor + key_block.shape[1] - 1
        needed = (anchor <= query_last) & (key_end >= lowest) & (key_end >= 0)
        result = lax.cond(
            needed,
            lambda carried: attend(carried, key_block, value_block, anchor),
            lambda carried: carried,
            state_now,
        )
        return result

    own_block = jnp.stack((local_k, local_v))
    shift_plan = []
    held_blocks = 1
    while 2 * held_blocks <= reach_blocks + 1:
        shift_plan.append((held_blocks, held_blocks))
        held_blocks = 2 * held_blocks
    shift_plan.append((held_blocks, reach_blocks + 1 - held_blocks))
    window = own_block
    for distance, block_total in shift_plan:
        newest = window[:, :, window.shape[2] - block_total * tok_row :]
        earlier = from_behind(newest, "dp", distance)
        window = jnp.concatenate((earlier, window), axis=2)
    anchor_first = (dp_index - reach_blocks) * tok_row
    key_window = window[0]
    value_window = window[1]

    def advance(block_index, carried):
        key_block = lax.dynamic_slice_in_dim(key_window, block_index * tok_row, tok_row, 1)
        value_block = lax.dynamic_slice_in_dim(value_window, block_index * tok_row, tok_row, 1)
        return visit(carried, key_block, value_block, anchor_first + block_index * tok_row)

    initial = (
        jnp.full((kv_heads, per_group, row_count, tok_row), -1e30, jnp.float32),
        jnp.zeros((kv_heads, per_group, row_count, tok_row), jnp.float32),
        jnp.zeros((row_count, tok_row, kv_heads, per_group, HEAD_SIZE), jnp.float32),
    )
    folded = lax.fori_loop(0, reach_blocks + 1, advance, initial)
    run_max, run_sum, run_acc = folded
    scaled = run_acc / jnp.transpose(run_sum, (2, 3, 0, 1))[..., None]
    attended = scaled.astype(jnp.bfloat16).reshape(row_count, tok_row, q_width)
    spread = lax.all_to_all(attended, HEADS, split_axis=1, concat_axis=2, tiled=True)
    log_norm = (run_max + jnp.log(run_sum)).reshape(kv_heads * per_group, row_count, tok_row)
    return (spread, log_norm)


def solution(mesh):
    split = Mesh(mesh.devices.reshape(mesh.shape["dp"], 8, 2), ("dp", "heads_0", "heads_1"))
    in_specs = (P(None, DP_HEADS, None), P(None, DP_HEADS, None), P(None, DP_HEADS, None), P())
    out_specs = (P(None, DP_HEADS, None), P(HEADS, None, "dp"))
    return jax.shard_map(
        per_device, mesh=split, in_specs=in_specs, out_specs=out_specs, check_vma=False
    )
```

profile of v0, /device:TPU:131, one launch (start us, length us, event | category | flops | bytes accessed | tf_op | source)
XLA Modules:
  0.0 317.5 jit_solution(8536956070249744335)
XLA Ops:
  2.7 4.2 %all-to-all-start = ((bf16[8,2,8,16,128]{4,3,0,2,1:T(8,128)(2,1)}), bf16[8,2,8,16,128]{4,3,0,2,1:T(8,128)(2,1)S(1)}, u32[]{:S(2)}, u32[]{:S(2)}) async-start(bf16[8,2,8,16,128]{4,3,0,2,1:T(8,128)(2,1)} %copy.84), calls=%async_computation | async-start | bytes 1048576 | tf_op jit(solution)/shard_map/all_to_all | solution.py:27
  9.0 3.5 %all-to-all-start.2 = ((bf16[8,2,8,16,128]{4,3,0,2,1:T(8,128)(2,1)}), bf16[8,2,8,16,128]{4,3,0,2,1:T(8,128)(2,1)S(1)}, u32[]{:S(2)}, u32[]{:S(2)}) async-start(bf16[8,2,8,16,128]{4,3,0,2,1:T(8,128)(2,1)} %copy.88), calls=%async_computation.2 | async-start | bytes 1048576 | tf_op jit(solution)/shard_map/all_to_all | solution.py:27
  13.8 6.8 %all-to-all-start.1 = ((bf16[8,2,8,16,128]{4,3,1,2,0:T(8,128)(2,1)}), bf16[8,2,8,16,128]{4,3,1,2,0:T(8,128)(2,1)S(1)}, u32[]{:S(2)}, u32[]{:S(2)}) async-start(bf16[8,2,8,16,128]{4,3,1,2,0:T(8,128)(2,1)} %copy.85), calls=%async_computation.1 | async-start | bytes 1048576 | tf_op jit(solution)/shard_map/all_to_all | solution.py:27
  21.5 17.1 %all-to-all-done.1 = bf16[8,2,8,16,128]{4,3,1,2,0:T(8,128)(2,1)S(1)} async-done(((bf16[8,2,8,16,128]{4,3,1,2,0:T(8,128)(2,1)}), bf16[8,2,8,16,128]{4,3,1,2,0:T(8,128)(2,1)S(1)}, u32[]{:S(2)}, u32[]{:S(2)}) %all-to-all-start.1) | async-done | bytes 524320 | tf_op jit(solution)/shard_map/all_to_all | solution.py:27
  38.6 3.5 %all-to-all-start.3 = ((bf16[8,2,8,16,128]{4,3,1,2,0:T(8,128)(2,1)}), bf16[8,2,8,16,128]{4,3,1,2,0:T(8,128)(2,1)S(1)}, u32[]{:S(2)}, u32[]{:S(2)}) async-start(bf16[8,2,8,16,128]{4,3,1,2,0:T(8,128)(2,1)} %copy.89), calls=%async_computation.3 | async-start | bytes 1048576 | tf_op jit(solution)/shard_map/all_to_all | solution.py:27
  42.2 17.8 %all-to-all-done.3 = bf16[8,2,8,16,128]{4,3,1,2,0:T(8,128)(2,1)S(1)} async-done(((bf16[8,2,8,16,128]{4,3,1,2,0:T(8,128)(2,1)}), bf16[8,2,8,16,128]{4,3,1,2,0:T(8,128)(2,1)S(1)}, u32[]{:S(2)}, u32[]{:S(2)}) %all-to-all-start.3) | async-done | bytes 524320 | tf_op jit(solution)/shard_map/all_to_all | solution.py:27
  60.1 4.0 %collective-permute-start.1 = (bf16[2,8,256,128]{3,2,1,0:T(8,128)(2,1)S(1)}, bf16[2,8,256,128]{3,2,1,0:T(8,128)(2,1)S(1)}, u32[]{:S(2)}, u32[]{:S(2)}) collective-permute-start(bf16[2,8,256,128]{3,2,1,0:T(8,128)(2,1)S(1)} %pad_maximum_fusion), channel_id=1, source_target_pairs={{0,16},{16,32},{32,48},{48,64},{64,80},{80,96},{96,112},{112,128},... | collective-permute-start | bytes 3145736 | tf_op jit(solution)/shard_map/ppermute | solution.py:40
  65.6 20.6 %collective-permute-done.1 = bf16[2,8,256,128]{3,2,1,0:T(8,128)(2,1)S(1)} collective-permute-done((bf16[2,8,256,128]{3,2,1,0:T(8,128)(2,1)S(1)}, bf16[2,8,256,128]{3,2,1,0:T(8,128)(2,1)S(1)}, u32[]{:S(2)}, u32[]{:S(2)}) %collective-permute-start.1) | collective-permute-done | bytes 1048608 | tf_op jit(solution)/shard_map/ppermute | solution.py:40
  87.8 8.2 %collective-permute-start.2 = (bf16[2,8,512,128]{3,2,1,0:T(8,128)(2,1)}, bf16[2,8,512,128]{3,2,1,0:T(8,128)(2,1)}, u32[]{:S(2)}, u32[]{:S(2)}) collective-permute-start(bf16[2,8,512,128]{3,2,1,0:T(8,128)(2,1)} %maximum_maximum_fusion.1), channel_id=1, source_target_pairs={{0,32},{16,48},{32,64},{48,80},{64,96},{80,112},{96,128},{112,144}... | collective-permute-start | bytes 6291464 | tf_op jit(solution)/shard_map/ppermute | solution.py:40
  96.5 5.8 %all_to_all.48 = bf16[8,2,8,16,256]{4,3,0,2,1:T(8,128)(2,1)S(1)} all-to-all(bf16[8,2,8,16,256]{4,3,0,2,1:T(8,128)(2,1)S(1)} %copy.92), channel_id=1, replica_groups=mesh['dp'=32,'heads_0'=8,'heads_1'=2] {'heads_1'}, dimensions={1} | all-to-all | bytes 2097152 | tf_op jit(solution)/shard_map/all_to_all | solution.py:27
  103.5 3.6 %all-to-all-start.5 = ((bf16[8,2,8,16,256]{4,3,1,2,0:T(8,128)(2,1)}), bf16[8,2,8,16,256]{4,3,1,2,0:T(8,128)(2,1)S(1)}, u32[]{:S(2)}, u32[]{:S(2)}) async-start(bf16[8,2,8,16,256]{4,3,1,2,0:T(8,128)(2,1)} %copy.93), calls=%async_computation.5 | async-start | bytes 2097152 | tf_op jit(solution)/shard_map/all_to_all | solution.py:27
  107.1 5.5 %collective-permute-start = (bf16[2,8,256,128]{3,2,1,0:T(8,128)(2,1)}, bf16[2,8,256,128]{3,2,1,0:T(8,128)(2,1)}, u32[]{:S(2)}, u32[]{:S(2)}) collective-permute-start(bf16[2,8,256,128]{3,2,1,0:T(8,128)(2,1)} %copy-done), channel_id=1, source_target_pairs={{0,64},{16,80},{32,96},{48,112},{64,128},{80,144},{96,160},{112,17... | collective-permute-start | bytes 3145736 | tf_op jit(solution)/shard_map/ppermute | solution.py:40
  113.7 22.6 %all-to-all-done.5 = bf16[8,2,8,16,256]{4,3,1,2,0:T(8,128)(2,1)S(1)} async-done(((bf16[8,2,8,16,256]{4,3,1,2,0:T(8,128)(2,1)}), bf16[8,2,8,16,256]{4,3,1,2,0:T(8,128)(2,1)S(1)}, u32[]{:S(2)}, u32[]{:S(2)}) %all-to-all-start.5) | async-done | bytes 1048608 | tf_op jit(solution)/shard_map/all_to_all | solution.py:27
  139.1 96.8 %collective-permute-done = bf16[2,8,256,128]{3,2,1,0:T(8,128)(2,1)} collective-permute-done((bf16[2,8,256,128]{3,2,1,0:T(8,128)(2,1)}, bf16[2,8,256,128]{3,2,1,0:T(8,128)(2,1)}, u32[]{:S(2)}, u32[]{:S(2)}) %collective-permute-start) | collective-permute-done | bytes 1048608 | tf_op jit(solution)/shard_map/ppermute | solution.py:40
  235.9 2.7 maximum_maximum_fusion
  241.3 4.4 %copy.97 = bf16[8,1280,128]{1,2,0:T(8,128)(2,1)} copy(bf16[8,1280,128]{2,1,0:T(8,128)(2,1)} %get-tuple-element.710) | data formatting | bytes 5242880
  245.9 35.6 %while.22 = (s32[]{:T(128)}, f32[1,2,8,256]{3,1,2,0:T(2,128)S(1)}, f32[1,2,8,256]{3,1,2,0:T(2,128)S(1)}, f32[8,256,1,2,128]{1,4,3,0,2:T(8,128)S(1)}, s32[]{:T(12...) while((s32[]{:T(128)}, f32[1,2,8,256]{3,1,2,0:T(2,128)S(1)}, ...), condition=%wide.region_10.11_spmd.clone, body=%wide.region_4.10_spmd.clone.sunk | while | flops 553397248 | bytes 21398452 | solution.py:140
  246.6 6.4 %conditional.3 = ((f32[1,2,8,256]{3,1,2,0:T(2,128)S(1)}, f32[1,2,8,256]{3,1,2,0:T(2,128)S(1)}, f32[8,256,1,2,128]{1,4,3,0,2:T(8,128)S(1)})) conditional(s32[]{:T(128)} %convert_element_type.46, (f32[1,2,8,256]{3,1,2,0:T(2,128)S(1)}, f32[1,2,8,256]{3,1,2,0:T(2,128)S(1)}, f32[8,256,1,2,128]{1,4,3,0,2:T(8,128)S(1)}) %tuple.85, (s32[8,32]{1,0:T(8,128)S(1)}, ...), branch_computations={%region_5.5_spmd, %region_6.9_spmd} | conditional | flops 553397248 | bytes 21397078 | solution.py:106
  253.8 6.4 %conditional.3 = ((f32[1,2,8,256]{3,1,2,0:T(2,128)S(1)}, f32[1,2,8,256]{3,1,2,0:T(2,128)S(1)}, f32[8,256,1,2,128]{1,4,3,0,2:T(8,128)S(1)})) conditional(s32[]{:T(128)} %convert_element_type.46, (f32[1,2,8,256]{3,1,2,0:T(2,128)S(1)}, f32[1,2,8,256]{3,1,2,0:T(2,128)S(1)}, f32[8,256,1,2,128]{1,4,3,0,2:T(8,128)S(1)}) %tuple.85, (s32[8,32]{1,0:T(8,128)S(1)}, ...), branch_computations={%region_5.5_spmd, %region_6.9_spmd} | conditional | flops 553397248 | bytes 21397078 | solution.py:106
  260.9 6.4 %conditional.3 = ((f32[1,2,8,256]{3,1,2,0:T(2,128)S(1)}, f32[1,2,8,256]{3,1,2,0:T(2,128)S(1)}, f32[8,256,1,2,128]{1,4,3,0,2:T(8,128)S(1)})) conditional(s32[]{:T(128)} %convert_element_type.46, (f32[1,2,8,256]{3,1,2,0:T(2,128)S(1)}, f32[1,2,8,256]{3,1,2,0:T(2,128)S(1)}, f32[8,256,1,2,128]{1,4,3,0,2:T(8,128)S(1)}) %tuple.85, (s32[8,32]{1,0:T(8,128)S(1)}, ...), branch_computations={%region_5.5_spmd, %region_6.9_spmd} | conditional | flops 553397248 | bytes 21397078 | solution.py:106
  268.0 6.4 %conditional.3 = ((f32[1,2,8,256]{3,1,2,0:T(2,128)S(1)}, f32[1,2,8,256]{3,1,2,0:T(2,128)S(1)}, f32[8,256,1,2,128]{1,4,3,0,2:T(8,128)S(1)})) conditional(s32[]{:T(128)} %convert_element_type.46, (f32[1,2,8,256]{3,1,2,0:T(2,128)S(1)}, f32[1,2,8,256]{3,1,2,0:T(2,128)S(1)}, f32[8,256,1,2,128]{1,4,3,0,2:T(8,128)S(1)}) %tuple.85, (s32[8,32]{1,0:T(8,128)S(1)}, ...), branch_computations={%region_5.5_spmd, %region_6.9_spmd} | conditional | flops 553397248 | bytes 21397078 | solution.py:106
  275.1 6.4 %conditional.3 = ((f32[1,2,8,256]{3,1,2,0:T(2,128)S(1)}, f32[1,2,8,256]{3,1,2,0:T(2,128)S(1)}, f32[8,256,1,2,128]{1,4,3,0,2:T(8,128)S(1)})) conditional(s32[]{:T(128)} %convert_element_type.46, (f32[1,2,8,256]{3,1,2,0:T(2,128)S(1)}, f32[1,2,8,256]{3,1,2,0:T(2,128)S(1)}, f32[8,256,1,2,128]{1,4,3,0,2:T(8,128)S(1)}) %tuple.85, (s32[8,32]{1,0:T(8,128)S(1)}, ...), branch_computations={%region_5.5_spmd, %region_6.9_spmd} | conditional | flops 553397248 | bytes 21397078 | solution.py:106
  283.5 4.1 %all-to-all-start.6 = ((bf16[8,256,256]{2,0,1:T(8,128)(2,1)}), bf16[8,256,256]{2,0,1:T(8,128)(2,1)S(1)}, u32[]{:S(2)}, u32[]{:S(2)}) async-start(bf16[8,256,256]{2,0,1:T(8,128)(2,1)} %bitcast.33), calls=%async_computation.6 | async-start | bytes 2097152 | tf_op jit(solution)/shard_map/all_to_all | solution.py:144
  288.2 27.4 %all-to-all-done.6 = bf16[8,256,256]{2,0,1:T(8,128)(2,1)S(1)} async-done(((bf16[8,256,256]{2,0,1:T(8,128)(2,1)}), bf16[8,256,256]{2,0,1:T(8,128)(2,1)S(1)}, u32[]{:S(2)}, u32[]{:S(2)}) %all-to-all-start.6) | async-done | bytes 1048608 | tf_op jit(solution)/shard_map/all_to_all | solution.py:144
  (99 shorter events, 53.9 us)
Async XLA Ops:
  2.7 6.2 %all-to-all-start = ((bf16[8,2,8,16,128]{4,3,0,2,1:T(8,128)(2,1)}), bf16[8,2,8,16,128]{4,3,0,2,1:T(8,128)(2,1)S(1)}, u32[]{:S(2)}, u32[]{:S(2)}) async-start(bf16[8,2,8,16,128]{4,3,0,2,1:T(8,128)(2,1)} %copy.84), calls=%async_computation | async-start | bytes 1048576 | tf_op jit(solution)/shard_map/all_to_all | solution.py:27
  9.0 4.9 %all-to-all-start.2 = ((bf16[8,2,8,16,128]{4,3,0,2,1:T(8,128)(2,1)}), bf16[8,2,8,16,128]{4,3,0,2,1:T(8,128)(2,1)S(1)}, u32[]{:S(2)}, u32[]{:S(2)}) async-start(bf16[8,2,8,16,128]{4,3,0,2,1:T(8,128)(2,1)} %copy.88), calls=%async_computation.2 | async-start | bytes 1048576 | tf_op jit(solution)/shard_map/all_to_all | solution.py:27
  13.8 24.8 %all-to-all-start.1 = ((bf16[8,2,8,16,128]{4,3,1,2,0:T(8,128)(2,1)}), bf16[8,2,8,16,128]{4,3,1,2,0:T(8,128)(2,1)S(1)}, u32[]{:S(2)}, u32[]{:S(2)}) async-start(bf16[8,2,8,16,128]{4,3,1,2,0:T(8,128)(2,1)} %copy.85), calls=%async_computation.1 | async-start | bytes 1048576 | tf_op jit(solution)/shard_map/all_to_all | solution.py:27
  38.6 21.4 %all-to-all-start.3 = ((bf16[8,2,8,16,128]{4,3,1,2,0:T(8,128)(2,1)}), bf16[8,2,8,16,128]{4,3,1,2,0:T(8,128)(2,1)S(1)}, u32[]{:S(2)}, u32[]{:S(2)}) async-start(bf16[8,2,8,16,128]{4,3,1,2,0:T(8,128)(2,1)} %copy.89), calls=%async_computation.3 | async-start | bytes 1048576 | tf_op jit(solution)/shard_map/all_to_all | solution.py:27
  60.1 4.0 %copy-start = (bf16[2,8,256,128]{3,2,1,0:T(8,128)(2,1)}, bf16[2,8,256,128]{3,2,1,0:T(8,128)(2,1)S(1)}, u32[]{:S(2)}) copy-start(bf16[2,8,256,128]{3,2,1,0:T(8,128)(2,1)S(1)} %pad_maximum_fusion) | copy-start | bytes 3145732
  60.1 26.1 %collective-permute-start.1 = (bf16[2,8,256,128]{3,2,1,0:T(8,128)(2,1)S(1)}, bf16[2,8,256,128]{3,2,1,0:T(8,128)(2,1)S(1)}, u32[]{:S(2)}, u32[]{:S(2)}) collective-permute-start(bf16[2,8,256,128]{3,2,1,0:T(8,128)(2,1)S(1)} %pad_maximum_fusion), channel_id=1, source_target_pairs={{0,16},{16,32},{32,48},{48,64},{64,80},{80,96},{96,112},{112,128},... | collective-permute-start | bytes 3145736 | tf_op jit(solution)/shard_map/ppermute | solution.py:40
  87.8 148.1 %collective-permute-start.2 = (bf16[2,8,512,128]{3,2,1,0:T(8,128)(2,1)}, bf16[2,8,512,128]{3,2,1,0:T(8,128)(2,1)}, u32[]{:S(2)}, u32[]{:S(2)}) collective-permute-start(bf16[2,8,512,128]{3,2,1,0:T(8,128)(2,1)} %maximum_maximum_fusion.1), channel_id=1, source_target_pairs={{0,32},{16,48},{32,64},{48,80},{64,96},{80,112},{96,128},{112,144}... | collective-permute-start | bytes 6291464 | tf_op jit(solution)/shard_map/ppermute | solution.py:40
  96.4 16.2 %copy-start.1 = (s32[8,32]{1,0:T(8,128)S(1)}, s32[8,32]{1,0:T(8,128)}, u32[]{:S(2)}) copy-start(s32[8,32]{1,0:T(8,128)} %param.11) | copy-start | bytes 3076
  103.5 32.8 %all-to-all-start.5 = ((bf16[8,2,8,16,256]{4,3,1,2,0:T(8,128)(2,1)}), bf16[8,2,8,16,256]{4,3,1,2,0:T(8,128)(2,1)S(1)}, u32[]{:S(2)}, u32[]{:S(2)}) async-start(bf16[8,2,8,16,256]{4,3,1,2,0:T(8,128)(2,1)} %copy.93), calls=%async_computation.5 | async-start | bytes 2097152 | tf_op jit(solution)/shard_map/all_to_all | solution.py:27
  107.1 128.8 %collective-permute-start = (bf16[2,8,256,128]{3,2,1,0:T(8,128)(2,1)}, bf16[2,8,256,128]{3,2,1,0:T(8,128)(2,1)}, u32[]{:S(2)}, u32[]{:S(2)}) collective-permute-start(bf16[2,8,256,128]{3,2,1,0:T(8,128)(2,1)} %copy-done), channel_id=1, source_target_pairs={{0,64},{16,80},{32,96},{48,112},{64,128},{80,144},{96,160},{112,17... | collective-permute-start | bytes 3145736 | tf_op jit(solution)/shard_map/ppermute | solution.py:40
  283.5 32.1 %all-to-all-start.6 = ((bf16[8,256,256]{2,0,1:T(8,128)(2,1)}), bf16[8,256,256]{2,0,1:T(8,128)(2,1)S(1)}, u32[]{:S(2)}, u32[]{:S(2)}) async-start(bf16[8,256,256]{2,0,1:T(8,128)(2,1)} %bitcast.33), calls=%async_computation.6 | async-start | bytes 2097152 | tf_op jit(solution)/shard_map/all_to_all | solution.py:144
where the time goes:
time: 319 us; the launch traced here: 318 us
  waiting for transfers between devices  203 us (64%)
  starting transfers between devices  43.4 us (14%)
  local copies, waits for them, and re-layouts  22.9 us (7%)
  matrix products  21.2 us (7%)
  other arithmetic  16.3 us (5%)
  blocking collectives  5.83 us (2%)
  loops' own time  4.17 us (1%)
    ppermute x3, waiting for transfers between devices, from_behind(): lax.ppermute(value, axis, [(source, source + steps) for source in range(l...  117 us
    all_to_all x5, waiting for transfers between devices, turned_blocks(): out = lax.all_to_all(out, axes[k], k, k, tiled=True)  58.1 us
    all_to_all x1, waiting for transfers between devices, per_device(): lax.all_to_all(attended, HEADS, split_axis=1, concat_axis=2, tiled=True)  27.4 us
    all_to_all x5, starting transfers between devices, turned_blocks(): out = lax.all_to_all(out, axes[k], k, k, tiled=True)  21.5 us
    ppermute x3, starting transfers between devices, from_behind(): lax.ppermute(value, axis, [(source, source + steps) for source in range(l...  17.8 us
    dot_general x5, matrix products, attend(): jnp.einsum('kgrts,rskd->rtkgd', weights.astype(jnp.bfloat16), value_heads...  12.1 us
    unnamed x9, local copies, waits for them, and re-layouts  9.6 us
    dot_general x5, matrix products, attend(): jnp.einsum('rtkgd,rskd->kgrts', query_heads, key_heads, preferred_element...  9.11 us
  transfers between devices with their start and end apart: 9, of which 7 were waited for; matrix products, arithmetic and copies ran while one was open for 4% of the time, Pallas kernels for 0%

commit v1 on v0

v1 whole, which is shorter than its diff:
```python
import jax
import jax.numpy as jnp
from jax import lax
from jax.experimental import pallas as pl
from jax.experimental.pallas import tpu as pltpu
from jax.sharding import Mesh
from jax.sharding import PartitionSpec as P

HEAD = 128
ROWS = 8
KV_HEADS = 16
HALO = 1024
SPAN = 2048
TQ = 128
TK = 256
MOST_BLOCKS = 6
LOG2E = 1.4426950408889634
SCALE = HEAD ** (-0.5)
ALL = ("x", "z", "y", "c")
PLANE = ("z", "y", "c")


def pack_body(q_ref, k_ref, v_ref, out_ref):
    for h in range(KV_HEADS):
        out_ref[h, :, 0:256] = q_ref[0, :, h * 256 : (h + 1) * 256]
        out_ref[h, :, 256:384] = k_ref[0, :, h * 128 : (h + 1) * 128]
        out_ref[h, :, 384:512] = v_ref[0, :, h * 128 : (h + 1) * 128]


def pack(queries, keys, values):
    wide = lambda width: pl.BlockSpec((1, 16, width), lambda r: (r, 0, 0))
    return pl.pallas_call(
        pack_body,
        grid=(ROWS,),
        in_specs=[wide(4096), wide(2048), wide(2048)],
        out_specs=pl.BlockSpec((KV_HEADS, 16, 512), lambda r: (r, 0, 0)),
        out_shape=jax.ShapeDtypeStruct((ROWS * KV_HEADS, 16, 512), jnp.bfloat16),
        name="pack",
    )(queries, keys, values)


def unpack_body(in_ref, out_ref):
    for h in range(KV_HEADS):
        out_ref[0, :, h * 256 : (h + 1) * 256] = in_ref[h]


def unpack(parts):
    return pl.pallas_call(
        unpack_body,
        grid=(ROWS,),
        in_specs=[pl.BlockSpec((KV_HEADS, 16, 256), lambda r: (r, 0, 0))],
        out_specs=pl.BlockSpec((1, 16, 4096), lambda r: (r, 0, 0)),
        out_shape=jax.ShapeDtypeStruct((ROWS, 16, 4096), jnp.bfloat16),
        name="unpack",
    )(parts)


def attend_body(low_ref, start_ref, qkv_ref, halo_ref, out_ref, norm_ref, kv_ref, s_ref, norm_acc):
    kv_ref[0:HALO] = halo_ref[...]
    kv_ref[HALO : HALO + SPAN] = qkv_ref[:, 256:512]
    lanes = lax.broadcasted_iota(jnp.int32, (TQ, 128), 1)
    key_lane = lax.broadcasted_iota(jnp.int32, (TQ, TK), 1)
    key_row = lax.broadcasted_iota(jnp.int32, (TQ, TK), 0)
    norm_acc[...] = jnp.zeros((TQ, 128), jnp.float32)

    def block(i, carry):
        first = pl.multiple_of(i * TQ, TQ)
        q0 = qkv_ref[pl.ds(first, TQ), 0:128]
        q1 = qkv_ref[pl.ds(first, TQ), 128:256]
        both = jnp.concatenate((q0, q1), axis=0)
        start = start_ref[pl.ds(first, TQ), :]
        start = jnp.concatenate((start, start), axis=1)
        j_low = low_ref[i] // TK
        j_high = (HALO + first + TQ - 1) // TK + 1

        def scores(j, top):
            at = pl.multiple_of(j * TK, TK)
            k = kv_ref[pl.ds(at, TK), 0:128]
            s = lax.dot_general(
                both, k, (((1,), (1,)), ((), ())), preferred_element_type=jnp.float32
            )
            key = key_lane + at
            seen = (key >= start) & (key <= key_row + (HALO + first))
            seen = jnp.concatenate((seen, seen), axis=0)
            s = jnp.where(seen, s, -1e30)
            s_ref[j - j_low] = s
            return jnp.maximum(top, jnp.maximum(s[:, 0:128], s[:, 128:256]))

        top = lax.fori_loop(j_low, j_high, scores, jnp.full((2 * TQ, 128), -1e30, jnp.float32))
        top = jnp.max(top, axis=1, keepdims=True)

        def gather(j, state):
            total, acc = state
            at = pl.multiple_of(j * TK, TK)
            v = kv_ref[pl.ds(at, TK), 128:256]
            w = jnp.exp2((s_ref[j - j_low] - top) * (SCALE * LOG2E))
            total = total + (w[:, 0:128] + w[:, 128:256])
            acc = acc + jnp.dot(w.astype(jnp.bfloat16), v, preferred_element_type=jnp.float32)
            return total, acc

        zero = jnp.zeros((2 * TQ, 128), jnp.float32)
        total, acc = lax.fori_loop(j_low, j_high, gather, (zero, zero))
        total = jnp.sum(total, axis=1, keepdims=True)
        result = (acc / total).astype(jnp.bfloat16)
        out_ref[pl.ds(first, TQ), 0:128] = result[0:TQ]
        out_ref[pl.ds(first, TQ), 128:256] = result[TQ : 2 * TQ]
        norm = top * SCALE + jnp.log(total)
        slot = (i // 2) * 4 + i % 2
        held = norm_acc[...]
        held = jnp.where(lanes == slot, norm[0:TQ], held)
        held = jnp.where(lanes == slot + 2, norm[TQ : 2 * TQ], held)
        norm_acc[...] = held
        return carry

    lax.fori_loop(0, SPAN // TQ, block, 0)
    norm_ref[...] = jnp.transpose(norm_acc[...])[0:32]


def attend(low, start, qkv, halo):
    return pl.pallas_call(
        attend_body,
        in_specs=[
            pl.BlockSpec(memory_space=pltpu.SMEM),
            pl.BlockSpec(memory_space=pltpu.VMEM),
            pl.BlockSpec(memory_space=pltpu.VMEM),
            pl.BlockSpec(memory_space=pltpu.VMEM),
        ],
        out_specs=[
            pl.BlockSpec(memory_space=pltpu.VMEM),
            pl.BlockSpec(memory_space=pltpu.VMEM),
        ],
        out_shape=[
            jax.ShapeDtypeStruct((SPAN, 256), jnp.bfloat16),
            jax.ShapeDtypeStruct((32, 128), jnp.float32),
        ],
        scratch_shapes=[
            pltpu.VMEM((HALO + SPAN, 256), jnp.bfloat16),
            pltpu.VMEM((MOST_BLOCKS, 2 * TQ, TK), jnp.float32),
            pltpu.VMEM((TQ, 128), jnp.float32),
        ],
        name="attend",
    )(low, start, qkv, halo)


def per_device(queries, keys, values, lengths):
    row = lax.axis_index("z")
    base = lax.axis_index("x") * SPAN
    ends = jnp.cumsum(lax.dynamic_index_in_dim(lengths, row, 0, keepdims=False))
    pos = base + jnp.arange(SPAN, dtype=jnp.int32)
    doc_start = jnp.max(jnp.where(ends[None, :] <= pos[:, None], ends[None, :], 0), axis=1)
    start = doc_start - base + HALO
    low = start[:: TQ]
    start = jnp.broadcast_to(start[:, None], (SPAN, 128))

    packed = pack(queries, keys, values)
    moved = lax.all_to_all(packed, PLANE, 0, 0, tiled=True)
    qkv = moved.reshape(SPAN, 512)
    halo = lax.ppermute(qkv[SPAN - HALO :, 256:512], "x", [(i, i + 1) for i in range(3)])
    out, norm = attend(low, start, qkv, halo)
    back = lax.all_to_all(out.reshape(128, 16, 256), PLANE, 0, 0, tiled=True)
    attended = unpack(back)
    norm = lax.all_to_all(norm.reshape(8, 2, 256), "z", 0, 0, tiled=True)
    return attended, jnp.transpose(norm, (1, 0, 2))


def solution(mesh):
    split = Mesh(mesh.devices.reshape(4, 8, 8, 2), ALL)
    wide = P(None, ALL, None)
    return jax.shard_map(
        per_device,
        mesh=split,
        in_specs=(wide, wide, wide, P()),
        out_specs=(wide, P(("y", "c"), None, ("x", "z"))),
        check_vma=False,
    )
```

time: 319 us -> 176 us (0.55)
  the two profiles are of different devices: /device:TPU:131 before, /device:TPU:12 now
where the time goes in v1:
time: 176 us; the launch traced here: 175 us
  waiting for transfers between devices  95.5 us (54%)
  Pallas kernels  35.2 us (20%)
  starting transfers between devices  26 us (15%)
  blocking collectives  12.5 us (7%)
  local copies, waits for them, and re-layouts  4.44 us (3%)
    all_to_all x1, waiting for transfers between devices, per_device(): moved = lax.all_to_all(packed, PLANE, 0, 0, tiled=True)  54 us
    all_to_all x1, waiting for transfers between devices, per_device(): back = lax.all_to_all(out.reshape(128, 16, 256), PLANE, 0, 0, tiled=True)  30.8 us
    pallas_call x1, Pallas kernels, attend(): pl.pallas_call(attend_body, in_specs=[pl.BlockSpec(memory_space=pltpu.SME...  24.3 us
    all_to_all x1, starting transfers between devices, per_device(): moved = lax.all_to_all(packed, PLANE, 0, 0, tiled=True)  17.4 us
    all_to_all x1, blocking collectives, per_device(): norm = lax.all_to_all(norm.reshape(8, 2, 256), 'z', 0, 0, tiled=True)  12.5 us
    ppermute x1, waiting for transfers between devices, per_device(): lax.ppermute(qkv[SPAN - HALO:, 256:512], 'x', [(i, i + 1) for i in range(...  10.6 us
    pallas_call x1, Pallas kernels, pack(): pl.pallas_call(pack_body, grid=(ROWS,), in_specs=[wide(4096), wide(2048),...  5.7 us
    all_to_all x1, starting transfers between devices, per_device(): back = lax.all_to_all(out.reshape(128, 16, 256), PLANE, 0, 0, tiled=True)  5.54 us
  transfers between devices with their start and end apart: 3, of which 3 were waited for; matrix products, arithmetic and copies ran while one was open for 1% of the time, Pallas kernels for 0%

profile of v1, /device:TPU:12, one launch (start us, length us, event | category | flops | bytes accessed | tf_op | source)
XLA Modules:
  0.0 174.6 jit_solution(12677292901113761957)
XLA Ops:
  0.6 0.0 copy-start
  0.6 5.7 %pack.1 = bf16[128,16,512]{2,1,0:T(8,128)(2,1)} custom-call(bf16[8,16,4096]{2,1,0:T(8,128)(2,1)} %q_ref.1, bf16[8,16,2048]{2,1,0:T(8,128)(2,1)} %k_ref.1, bf16[8,16,2048]{2,1,0:T(8,128)(2,1)} %v_ref.1), custom_call_target="tpu_custom_call" | custom-call | tf_op jit(solution)/shard_map/pack/pallas_call | solution.py:32
  6.3 17.4 %all-to-all-start = ((bf16[128,16,512]{2,1,0:T(8,128)(2,1)}), bf16[128,16,512]{2,1,0:T(8,128)(2,1)S(1)}, u32[]{:S(2)}, u32[]{:S(2)}) async-start(bf16[128,16,512]{2,1,0:T(8,128)(2,1)} %pack.1), calls=%async_computation | async-start | bytes 4194304 | tf_op jit(solution)/shard_map/all_to_all | solution.py:156
  23.7 54.0 %all-to-all-done = bf16[128,16,512]{2,1,0:T(8,128)(2,1)S(1)} async-done(((bf16[128,16,512]{2,1,0:T(8,128)(2,1)}), bf16[128,16,512]{2,1,0:T(8,128)(2,1)S(1)}, u32[]{:S(2)}, u32[]{:S(2)}) %all-to-all-start) | async-done | bytes 2097184 | tf_op jit(solution)/shard_map/all_to_all | solution.py:156
  77.7 0.0 copy-start.1
  77.8 3.1 %collective-permute-start = (bf16[1024,256]{1,0:T(8,128)(2,1)S(1)}, bf16[1024,256]{1,0:T(8,128)(2,1)S(1)}, u32[]{:S(2)}, u32[]{:S(2)}) collective-permute-start(bf16[1024,256]{1,0:T(8,128)(2,1)S(1)} %slice.8), channel_id=1, source_target_pairs={{0,128},{128,256},{256,384},{1,129},{129,257},{257,385},{2,130},{1... | collective-permute-start | bytes 1572872 | tf_op jit(solution)/shard_map/ppermute | solution.py:158
  80.9 0.0 copy-done
  80.9 0.1 copy.12
  81.0 0.1 reduce-window.8
  81.1 0.1 reduce
  81.2 0.1 select_reduce_fusion
  81.3 0.7 slice.6.low_ref
  82.0 10.6 %collective-permute-done.halo_ref = bf16[1024,256]{1,0:T(8,128)(2,1)S(1)} collective-permute-done((bf16[1024,256]{1,0:T(8,128)(2,1)S(1)}, bf16[1024,256]{1,0:T(8,128)(2,1)S(1)}, u32[]{:S(2)}, u32[]{:S(2)}) %collective-permute-start) | collective-permute-done | bytes 524320 | tf_op jit(solution)/shard_map/ppermute | solution.py:158
  92.7 1.3 broadcast_in_dim.13.start_ref
  94.0 0.0 copy-done.1
  94.0 0.0 copy-done.3
  94.0 24.3 %attend.1 = (bf16[2048,256]{1,0:T(8,128)(2,1)}, f32[32,128]{1,0:T(8,128)}) custom-call(s32[16]{0:T(128)} %slice.6.low_ref, s32[2048,128]{1,0:T(8,128)} %broadcast_in_dim.13.start_ref, bf16[2048,512]{1,0:T(8,128)(2,1)} %bitcast.6, bf16[1024,256]{1,0:T(8,128)(2,1)} %copy-done.3), custom_call_target="tpu_custom_call" | custom-call | tf_op jit(solution)/shard_map/attend/pallas_call | solution.py:120
  118.3 0.7 reshape.49
  119.0 12.5 %all_to_all.15 = f32[8,2,256]{2,1,0:T(2,128)S(1)} all-to-all(f32[8,2,256]{2,1,0:T(2,128)S(1)} %reshape.49), channel_id=1, replica_groups=mesh['x'=4,'z'=8,'y'=8,'c'=2] {'z'}, dimensions={0} | all-to-all | bytes 32768 | tf_op jit(solution)/shard_map/all_to_all | solution.py:162
  131.5 5.5 %all-to-all-start.1 = ((bf16[128,16,256]{2,1,0:T(8,128)(2,1)}), bf16[128,16,256]{2,1,0:T(8,128)(2,1)S(1)}, u32[]{:S(2)}, u32[]{:S(2)}) async-start(bf16[128,16,256]{2,1,0:T(8,128)(2,1)} %bitcast.7), calls=%async_computation.1 | async-start | bytes 2097152 | tf_op jit(solution)/shard_map/all_to_all | solution.py:160
  137.0 0.6 copy.13
  137.7 30.8 %all-to-all-done.1.in_ref = bf16[128,16,256]{2,1,0:T(8,128)(2,1)S(1)} async-done(((bf16[128,16,256]{2,1,0:T(8,128)(2,1)}), bf16[128,16,256]{2,1,0:T(8,128)(2,1)S(1)}, u32[]{:S(2)}, u32[]{:S(2)}) %all-to-all-start.1) | async-done | bytes 1048608 | tf_op jit(solution)/shard_map/all_to_all | solution.py:160
  168.5 1.0 copy-done.2
  169.5 5.2 %unpack.1 = bf16[8,16,4096]{2,1,0:T(8,128)(2,1)} custom-call(bf16[128,16,256]{2,1,0:T(8,128)(2,1)} %copy-done.2), custom_call_target="tpu_custom_call" | custom-call | tf_op jit(solution)/shard_map/unpack/pallas_call | solution.py:48
  (6 shorter events, 0.1 us)
Async XLA Ops:
  0.6 80.3 %copy-start = (s32[8,32]{1,0:T(8,128)S(1)}, s32[8,32]{1,0:T(8,128)}, u32[]{:S(2)}) copy-start(s32[8,32]{1,0:T(8,128)} %param.7) | copy-start | bytes 3076
  6.3 71.4 %all-to-all-start = ((bf16[128,16,512]{2,1,0:T(8,128)(2,1)}), bf16[128,16,512]{2,1,0:T(8,128)(2,1)S(1)}, u32[]{:S(2)}, u32[]{:S(2)}) async-start(bf16[128,16,512]{2,1,0:T(8,128)(2,1)} %pack.1), calls=%async_computation | async-start | bytes 4194304 | tf_op jit(solution)/shard_map/all_to_all | solution.py:156
  77.7 16.2 %copy-start.1 = (bf16[128,16,512]{2,1,0:T(8,128)(2,1)}, bf16[128,16,512]{2,1,0:T(8,128)(2,1)S(1)}, u32[]{:S(2)}) copy-start(bf16[128,16,512]{2,1,0:T(8,128)(2,1)S(1)} %all-to-all-done) | copy-start | bytes 6291460
  77.8 14.9 %collective-permute-start = (bf16[1024,256]{1,0:T(8,128)(2,1)S(1)}, bf16[1024,256]{1,0:T(8,128)(2,1)S(1)}, u32[]{:S(2)}, u32[]{:S(2)}) collective-permute-start(bf16[1024,256]{1,0:T(8,128)(2,1)S(1)} %slice.8), channel_id=1, source_target_pairs={{0,128},{128,256},{256,384},{1,129},{129,257},{257,385},{2,130},{1... | collective-permute-start | bytes 1572872 | tf_op jit(solution)/shard_map/ppermute | solution.py:158
  92.6 1.3 copy-start.3
  131.5 37.0 %all-to-all-start.1 = ((bf16[128,16,256]{2,1,0:T(8,128)(2,1)}), bf16[128,16,256]{2,1,0:T(8,128)(2,1)S(1)}, u32[]{:S(2)}, u32[]{:S(2)}) async-start(bf16[128,16,256]{2,1,0:T(8,128)(2,1)} %bitcast.7), calls=%async_computation.1 | async-start | bytes 2097152 | tf_op jit(solution)/shard_map/all_to_all | solution.py:160
  168.5 1.0 copy-start.2

commit v2 on v1

v2 whole, which is shorter than its diff:
```python
import jax
import jax.numpy as jnp
from jax import lax
from jax.experimental import pallas as pl
from jax.experimental.pallas import tpu as pltpu
from jax.sharding import Mesh
from jax.sharding import PartitionSpec as P

HEAD = 128
ROWS = 8
KV_HEADS = 16
HALO = 1024
SPAN = 2048
TQ = 128
TK = 256
MOST_BLOCKS = 5
BLOCKS = SPAN // TQ
HALO_BLOCKS = HALO // TQ
LOG2E = 1.4426950408889634
SCALE = HEAD ** (-0.5)
ALL = ("x", "z", "y", "c")
PLANE = ("z", "y", "c")


def pack_body(q_ref, k_ref, v_ref, out_ref, sems):
    copies = []
    for h in range(KV_HEADS):
        for n, (ref, width, at) in enumerate(((q_ref, 256, 0), (k_ref, 128, 256), (v_ref, 128, 384))):
            copies.append(
                pltpu.make_async_copy(
                    ref.at[:, :, pl.ds(h * width, width)],
                    out_ref.at[:, h, :, pl.ds(at, width)],
                    sems.at[n, h],
                )
            )
    for copy in copies:
        copy.start()
    for copy in copies:
        copy.wait()


def pack(queries, keys, values):
    return pl.pallas_call(
        pack_body,
        in_specs=[pl.BlockSpec(memory_space=pl.ANY)] * 3,
        out_specs=pl.BlockSpec(memory_space=pl.ANY),
        out_shape=jax.ShapeDtypeStruct((ROWS, KV_HEADS, 16, 512), jnp.bfloat16),
        scratch_shapes=[pltpu.SemaphoreType.DMA((3, KV_HEADS))],
        name="pack",
    )(queries, keys, values)


def unpack_body(in_ref, out_ref, sems):
    copies = [
        pltpu.make_async_copy(
            in_ref.at[:, h], out_ref.at[:, :, pl.ds(h * 256, 256)], sems.at[h]
        )
        for h in range(KV_HEADS)
    ]
    for copy in copies:
        copy.start()
    for copy in copies:
        copy.wait()


def unpack(parts):
    return pl.pallas_call(
        unpack_body,
        in_specs=[pl.BlockSpec(memory_space=pl.ANY)],
        out_specs=pl.BlockSpec(memory_space=pl.ANY),
        out_shape=jax.ShapeDtypeStruct((ROWS, 16, 4096), jnp.bfloat16),
        scratch_shapes=[pltpu.SemaphoreType.DMA((KV_HEADS,))],
        name="unpack",
    )(parts)


def attend_block(i, j_low, ends_ref, qkv_ref, kv_ref, out_ref, s_ref, norm_acc):
    first = pl.multiple_of(i * TQ, TQ)
    slot = (i // 2) * 4 + i % 2
    count = (HALO + first) // TK + 1 - j_low

    def body(blocks):
        q = qkv_ref[pl.ds(first, TQ), 0:256]
        both = jnp.concatenate((q[:, 0:128], q[:, 128:256]), axis=0)
        row = lax.broadcasted_iota(jnp.int32, (TQ, TK), 0) + (HALO + first)
        top = None
        for n in range(blocks):
            at = pl.multiple_of((j_low + n) * TK, TK)
            s = lax.dot_general(
                both,
                kv_ref[pl.ds(at, TK), 0:128],
                (((1,), (1,)), ((), ())),
                preferred_element_type=jnp.float32,
            )
            seen = row < ends_ref[pl.ds(j_low + n, 1), :]
            if n == blocks - 1:
                seen = seen & (lax.broadcasted_iota(jnp.int32, (TQ, TK), 1) + at <= row)
            halves = []
            for h in range(2):
                part = jnp.where(seen, s[h * TQ : (h + 1) * TQ], -1e30)
                s_ref[n, h * TQ : (h + 1) * TQ] = part
                halves.append(jnp.maximum(part[:, 0:128], part[:, 128:256]))
            here = jnp.concatenate(halves, axis=0)
            top = here if top is None else jnp.maximum(top, here)
        top = jnp.max(top, axis=1, keepdims=True)
        total = acc = None
        for n in range(blocks):
            at = pl.multiple_of((j_low + n) * TK, TK)
            w = jnp.exp2((s_ref[n] - top) * (SCALE * LOG2E))
            part = w[:, 0:128] + w[:, 128:256]
            o = jnp.dot(
                w.astype(jnp.bfloat16),
                kv_ref[pl.ds(at, TK), 128:256],
                preferred_element_type=jnp.float32,
            )
            total = part if total is None else total + part
            acc = o if acc is None else acc + o
        total = jnp.sum(total, axis=1, keepdims=True)
        result = (acc / total).astype(jnp.bfloat16)
        out_ref[pl.ds(first, TQ), 0:128] = result[0:TQ]
        out_ref[pl.ds(first, TQ), 128:256] = result[TQ : 2 * TQ]
        norm = top * SCALE + jnp.log(total)
        lanes = lax.broadcasted_iota(jnp.int32, (TQ, 128), 1)
        held = jnp.where(lanes == slot, norm[0:TQ], norm_acc[...])
        norm_acc[...] = jnp.where(lanes == slot + 2, norm[TQ : 2 * TQ], held)

    for blocks in range(1, MOST_BLOCKS + 1):

        @pl.when(count == blocks)
        def _():
            body(blocks)


def local_body(low_ref, ends_ref, qkv_ref, out_ref, norm_ref, kv_ref, s_ref):
    kv_ref[HALO : HALO + SPAN] = qkv_ref[:, 256:512]
    norm_ref[...] = jnp.zeros((TQ, 128), jnp.float32)

    def block(i, carry):
        @pl.when(low_ref[i] >= HALO)
        def _():
            attend_block(i, low_ref[i] // TK, ends_ref, qkv_ref, kv_ref, out_ref, s_ref, norm_ref)

        return carry

    lax.fori_loop(0, BLOCKS, block, 0)


def attend_local(low, ends, qkv):
    vmem = pl.BlockSpec(memory_space=pltpu.VMEM)
    return pl.pallas_call(
        local_body,
        in_specs=[pl.BlockSpec(memory_space=pltpu.SMEM), vmem, vmem],
        out_specs=[vmem, vmem],
        out_shape=[
            jax.ShapeDtypeStruct((SPAN, 256), jnp.bfloat16),
            jax.ShapeDtypeStruct((TQ, 128), jnp.float32),
        ],
        scratch_shapes=[
            pltpu.VMEM((HALO + SPAN, 256), jnp.bfloat16),
            pltpu.VMEM((MOST_BLOCKS, 2 * TQ, TK), jnp.float32),
        ],
        name="attend_local",
    )(low, ends, qkv)


def halo_body(low_ref, ends_ref, qkv_ref, halo_ref, prev_ref, prev_norm, out_ref, norm_ref, kv_ref, s_ref, norm_acc):
    kv_ref[0:HALO] = halo_ref[...]
    kv_ref[HALO : 2 * HALO] = qkv_ref[:, 256:512]
    out_ref[...] = prev_ref[...]
    norm_acc[...] = prev_norm[...]

    def block(i, carry):
        @pl.when(low_ref[i] < HALO)
        def _():
            attend_block(i, low_ref[i] // TK, ends_ref, qkv_ref, kv_ref, out_ref, s_ref, norm_acc)

        return carry

    lax.fori_loop(0, HALO_BLOCKS, block, 0)
    norm_ref[...] = jnp.transpose(norm_acc[...])[0:32]


def attend_halo(low, ends, qkv, halo, out, norm):
    at_first = lambda *shape: pl.BlockSpec(shape, lambda n: (0, 0))
    return pl.pallas_call(
        halo_body,
        grid=(1,),
        in_specs=[
            pl.BlockSpec(memory_space=pltpu.SMEM),
            at_first(12, TK),
            at_first(HALO, 512),
            at_first(HALO, 256),
            at_first(HALO, 256),
            at_first(TQ, 128),
        ],
        out_specs=[at_first(HALO, 256), at_first(32, 128)],
        out_shape=[
            jax.ShapeDtypeStruct((SPAN, 256), jnp.bfloat16),
            jax.ShapeDtypeStruct((32, 128), jnp.float32),
        ],
        scratch_shapes=[
            pltpu.VMEM((2 * HALO, 256), jnp.bfloat16),
            pltpu.VMEM((MOST_BLOCKS, 2 * TQ, TK), jnp.float32),
            pltpu.VMEM((TQ, 128), jnp.float32),
        ],
        input_output_aliases={4: 0},
        name="attend_halo",
    )(low, ends, qkv, halo, out, norm)


def doc_bounds(lengths, row, base):
    own = lax.dynamic_index_in_dim(lengths, row, 0, keepdims=False)
    upto = jnp.arange(32)[:, None] <= jnp.arange(32)[None, :]
    ends = jnp.sum(jnp.where(upto, own[:, None], 0), axis=0)
    first = base + jnp.arange(BLOCKS, dtype=jnp.int32) * TQ
    low = jnp.max(jnp.where(ends[None, :] <= first[:, None], ends[None, :], 0), axis=1)
    pos = (base - HALO) + jnp.arange(HALO + SPAN, dtype=jnp.int32).reshape(12, TK)
    after = jnp.where(ends[:, None, None] > pos[None], ends[:, None, None], 1 << 20)
    end = jnp.where(pos >= 0, jnp.min(after, axis=0), -(1 << 20))
    return low - base + HALO, end - base + HALO


def per_device(queries, keys, values, lengths):
    low, ends = doc_bounds(lengths, lax.axis_index("z"), lax.axis_index("x") * SPAN)
    packed = pack(queries, keys, values).reshape(128, 16, 512)
    moved = lax.all_to_all(packed, PLANE, 0, 0, tiled=True)
    qkv = moved.reshape(SPAN, 512)
    halo = lax.ppermute(qkv[SPAN - HALO :, 256:512], "x", [(i, i + 1) for i in range(3)])
    out, norm = attend_local(low, ends, qkv)
    out, norm = attend_halo(low, ends, qkv, halo, out, norm)
    back = lax.all_to_all(out.reshape(128, 16, 256), PLANE, 0, 0, tiled=True)
    attended = unpack(back.reshape(ROWS, KV_HEADS, 16, 256))
    norms = lax.all_gather(norm, "z", axis=0, tiled=False)
    norms = lax.dynamic_slice_in_dim(norms, lax.axis_index("z") * 4, 4, 1)
    return attended, jnp.transpose(norms.reshape(8, 2, 256), (1, 0, 2))


def solution(mesh):
    split = Mesh(mesh.devices.reshape(4, 8, 8, 2), ALL)
    wide = P(None, ALL, None)
    return jax.shard_map(
        per_device,
        mesh=split,
        in_specs=(wide, wide, wide, P()),
        out_specs=(wide, P(("y", "c"), None, ("x", "z"))),
        check_vma=False,
    )
```

time: 176 us -> 245 us (1.39)
  the two profiles are of different devices: /device:TPU:12 before, /device:TPU:34 now
where the time goes in v2:
time: 245 us; the launch traced here: 244 us
  Pallas kernels  113 us (46%)
  waiting for transfers between devices  54 us (22%)
  blocking collectives  43.7 us (18%)
  starting transfers between devices  29.1 us (12%)
  local copies, waits for them, and re-layouts  2.46 us (1%)
    pallas_call x1, Pallas kernels, pack(): pl.pallas_call(pack_body, in_specs=[pl.BlockSpec(memory_space=pl.ANY)] *...  65.1 us
    all_to_all x1, waiting for transfers between devices, per_device(): moved = lax.all_to_all(packed, PLANE, 0, 0, tiled=True)  50.1 us
    all_gather x1, blocking collectives, per_device(): norms = lax.all_gather(norm, 'z', axis=0, tiled=False)  43.7 us
    pallas_call x1, Pallas kernels, unpack(): pl.pallas_call(unpack_body, in_specs=[pl.BlockSpec(memory_space=pl.ANY)],...  33 us
    all_to_all x1, starting transfers between devices, per_device(): moved = lax.all_to_all(packed, PLANE, 0, 0, tiled=True)  17 us
    all_to_all x1, starting transfers between devices, per_device(): back = lax.all_to_all(out.reshape(128, 16, 256), PLANE, 0, 0, tiled=True)  8.68 us
    pallas_call x1, Pallas kernels, attend_halo(): pl.pallas_call(halo_body, grid=(1,), in_specs=[pl.BlockSpec(memory_space=...  7.93 us
    pallas_call x1, Pallas kernels, attend_local(): pl.pallas_call(local_body, in_specs=[pl.BlockSpec(memory_space=pltpu.SMEM...  6.66 us
  transfers between devices with their start and end apart: 3, of which 2 were waited for; matrix products, arithmetic and copies ran while one was open for 1% of the time, Pallas kernels for 3%

profile of v2, /device:TPU:34, one launch (start us, length us, event | category | flops | bytes accessed | tf_op | source)
XLA Modules:
  0.0 244.3 jit_solution(8357727419905207680)
XLA Ops:
  0.6 0.0 copy-start
  0.6 65.1 %pack.1 = bf16[8,16,16,512]{3,2,1,0:T(8,128)(2,1)} custom-call(bf16[8,16,4096]{2,1,0:T(8,128)(2,1)} %q_ref.1, bf16[8,16,2048]{2,1,0:T(8,128)(2,1)} %k_ref.1, bf16[8,16,2048]{2,1,0:T(8,128)(2,1)} %v_ref.1), custom_call_target="tpu_custom_call" | custom-call | tf_op jit(solution)/shard_map/pack/pallas_call | solution.py:43
  65.7 17.0 %all-to-all-start = ((bf16[128,16,512]{2,1,0:T(8,128)(2,1)}), bf16[128,16,512]{2,1,0:T(8,128)(2,1)S(1)}, u32[]{:S(2)}, u32[]{:S(2)}) async-start(bf16[128,16,512]{2,1,0:T(8,128)(2,1)} %bitcast.11), calls=%async_computation | async-start | bytes 4194304 | tf_op jit(solution)/shard_map/all_to_all | solution.py:226
  82.8 0.0 copy-done
  82.8 0.1 select_reduce_fusion.1
  82.9 0.2 select_reduce_fusion
  83.1 50.1 %all-to-all-done = bf16[128,16,512]{2,1,0:T(8,128)(2,1)S(1)} async-done(((bf16[128,16,512]{2,1,0:T(8,128)(2,1)}), bf16[128,16,512]{2,1,0:T(8,128)(2,1)S(1)}, u32[]{:S(2)}, u32[]{:S(2)}) %all-to-all-start) | async-done | bytes 2097184 | tf_op jit(solution)/shard_map/all_to_all | solution.py:226
  133.2 0.0 copy-start.1
  133.2 3.4 %collective-permute-start = (bf16[1024,256]{1,0:T(8,128)(2,1)S(1)}, bf16[1024,256]{1,0:T(8,128)(2,1)S(1)}, u32[]{:S(2)}, u32[]{:S(2)}) collective-permute-start(bf16[1024,256]{1,0:T(8,128)(2,1)S(1)} %slice.4), channel_id=1, source_target_pairs={{0,128},{128,256},{256,384},{1,129},{129,257},{257,385},{2,130},{1... | collective-permute-start | bytes 1572872 | tf_op jit(solution)/shard_map/ppermute | solution.py:228
  136.7 0.2 select_reduce_fusion.2
  136.8 0.5 subtract_add_fusion.1.low_ref
  137.4 0.6 subtract_add_fusion.ends_ref
  138.0 0.0 copy-done.1
  138.0 6.7 %attend_local.1 = (bf16[2048,256]{1,0:T(8,128)(2,1)}, f32[128,128]{1,0:T(8,128)}) custom-call(s32[16]{0:T(128)} %subtract_add_fusion.1.low_ref, s32[12,256]{1,0:T(8,128)} %subtract_add_fusion.ends_ref, bf16[2048,512]{1,0:T(8,128)(2,1)} %bitcast.9), custom_call_target="tpu_custom_call" | custom-call | tf_op jit(solution)/shard_map/attend_local/pallas_call | solution.py:150
  144.6 3.9 %collective-permute-done.halo_ref = bf16[1024,256]{1,0:T(8,128)(2,1)S(1)} collective-permute-done((bf16[1024,256]{1,0:T(8,128)(2,1)S(1)}, bf16[1024,256]{1,0:T(8,128)(2,1)S(1)}, u32[]{:S(2)}, u32[]{:S(2)}) %collective-permute-start) | collective-permute-done | bytes 524320 | tf_op jit(solution)/shard_map/ppermute | solution.py:228
  148.5 0.8 copy-done.3
  149.3 7.9 %attend_halo.1 = (bf16[2048,256]{1,0:T(8,128)(2,1)}, f32[32,128]{1,0:T(8,128)}) custom-call(s32[16]{0:T(128)} %subtract_add_fusion.1.low_ref, s32[12,256]{1,0:T(8,128)} %subtract_add_fusion.ends_ref, bf16[2048,512]{1,0:T(8,128)(2,1)} %bitcast.10, bf16[1024,256]{1,0:T(8,128)(2,1)} %copy-done.3, ...), custom_call_target="tpu_custom_call", output_to_operand_aliasing={{0}: (4, {})} | custom-call | tf_op jit(solution)/shard_map/attend_halo/pallas_call | solution.py:185
  157.3 8.7 %all-to-all-start.1 = ((bf16[128,16,256]{2,1,0:T(8,128)(2,1)}), bf16[128,16,256]{2,1,0:T(8,128)(2,1)S(1)}, u32[]{:S(2)}, u32[]{:S(2)}) async-start(bf16[128,16,256]{2,1,0:T(8,128)(2,1)} %bitcast.13), calls=%async_computation.1 | async-start | bytes 2097152 | tf_op jit(solution)/shard_map/all_to_all | solution.py:231
  166.0 0.0 copy-done.4
  166.0 43.7 %all-gather = f32[256,128]{1,0:T(8,128)S(1)} all-gather(f32[32,128]{1,0:T(8,128)S(1)} %copy-done.4), channel_id=2, replica_groups=mesh['x'=4,'z'=8,'y'=8,'c'=2] {'z'}, dimensions={0}, use_global_device_ids=true | all-gather | bytes 147456 | tf_op jit(solution)/shard_map/all_gather | solution.py:233
  209.7 0.6 copy.8
  210.3 0.0 all-to-all-done.1
  210.3 1.0 copy-done.2
  211.3 33.0 %unpack.1 = bf16[8,16,4096]{2,1,0:T(8,128)(2,1)} custom-call(bf16[8,16,16,256]{3,2,1,0:T(8,128)(2,1)} %bitcast.12), custom_call_target="tpu_custom_call" | custom-call | tf_op jit(solution)/shard_map/unpack/pallas_call | solution.py:67
  (9 shorter events, 0.1 us)
Async XLA Ops:
  0.6 82.2 %copy-start = (s32[8,32]{1,0:T(8,128)S(1)}, s32[8,32]{1,0:T(8,128)}, u32[]{:S(2)}) copy-start(s32[8,32]{1,0:T(8,128)} %param.7) | copy-start | bytes 3076
  65.7 67.5 %all-to-all-start = ((bf16[128,16,512]{2,1,0:T(8,128)(2,1)}), bf16[128,16,512]{2,1,0:T(8,128)(2,1)S(1)}, u32[]{:S(2)}, u32[]{:S(2)}) async-start(bf16[128,16,512]{2,1,0:T(8,128)(2,1)} %bitcast.11), calls=%async_computation | async-start | bytes 4194304 | tf_op jit(solution)/shard_map/all_to_all | solution.py:226
  133.2 4.8 %copy-start.1 = (bf16[128,16,512]{2,1,0:T(8,128)(2,1)}, bf16[128,16,512]{2,1,0:T(8,128)(2,1)S(1)}, u32[]{:S(2)}) copy-start(bf16[128,16,512]{2,1,0:T(8,128)(2,1)S(1)} %all-to-all-done) | copy-start | bytes 6291460
  133.2 15.3 %collective-permute-start = (bf16[1024,256]{1,0:T(8,128)(2,1)S(1)}, bf16[1024,256]{1,0:T(8,128)(2,1)S(1)}, u32[]{:S(2)}, u32[]{:S(2)}) collective-permute-start(bf16[1024,256]{1,0:T(8,128)(2,1)S(1)} %slice.4), channel_id=1, source_target_pairs={{0,128},{128,256},{256,384},{1,129},{129,257},{257,385},{2,130},{1... | collective-permute-start | bytes 1572872 | tf_op jit(solution)/shard_map/ppermute | solution.py:228
  148.5 0.8 copy-start.3
  157.3 8.7 %copy-start.4 = (f32[32,128]{1,0:T(8,128)S(1)}, f32[32,128]{1,0:T(8,128)}, u32[]{:S(2)}) copy-start(f32[32,128]{1,0:T(8,128)} %get-tuple-element.9) | copy-start | bytes 49156
  157.3 53.1 %all-to-all-start.1 = ((bf16[128,16,256]{2,1,0:T(8,128)(2,1)}), bf16[128,16,256]{2,1,0:T(8,128)(2,1)S(1)}, u32[]{:S(2)}, u32[]{:S(2)}) async-start(bf16[128,16,256]{2,1,0:T(8,128)(2,1)} %bitcast.13), calls=%async_computation.1 | async-start | bytes 2097152 | tf_op jit(solution)/shard_map/all_to_all | solution.py:231
  210.3 1.0 copy-start.2

commit v3 on v2

--- a/solution.py
+++ b/solution.py
@@ -22,20 +22,35 @@
 PLANE = ("z", "y", "c")
 
 
-def pack_body(q_ref, k_ref, v_ref, out_ref, sems):
-    copies = []
+def in_vmem(*arrays):
+    return [pltpu.with_memory_space_constraint(a, pltpu.VMEM) for a in arrays]
+
+
+def pack_body(q_ref, k_ref, v_ref, out_ref, held_ref, sems):
+    parts = ((q_ref, 256, 0), (k_ref, 128, 256), (v_ref, 128, 384))
+    reads = [
+        [
+            pltpu.make_async_copy(
+                ref.at[:, :, pl.ds(h * width, width)],
+                held_ref.at[:, h, :, pl.ds(at, width)],
+                sems.at[n, h],
+            )
+            for n, (ref, width, at) in enumerate(parts)
+        ]
+        for h in range(KV_HEADS)
+    ]
+    writes = [
+        pltpu.make_async_copy(held_ref.at[:, h], out_ref.at[:, h], sems.at[3, h])
+        for h in range(KV_HEADS)
+    ]
+    for copies in reads:
+        for copy in copies:
+            copy.start()
     for h in range(KV_HEADS):
-        for n, (ref, width, at) in enumerate(((q_ref, 256, 0), (k_ref, 128, 256), (v_ref, 128, 384))):
-            copies.append(
-                pltpu.make_async_copy(
-                    ref.at[:, :, pl.ds(h * width, width)],
-                    out_ref.at[:, h, :, pl.ds(at, width)],
-                    sems.at[n, h],
-                )
-            )
-    for copy in copies:
-        copy.start()
-    for copy in copies:
+        for copy in reads[h]:
+            copy.wait()
+        writes[h].start()
+    for copy in writes:
         copy.wait()
 
 
@@ -45,7 +60,10 @@
         in_specs=[pl.BlockSpec(memory_space=pl.ANY)] * 3,
         out_specs=pl.BlockSpec(memory_space=pl.ANY),
         out_shape=jax.ShapeDtypeStruct((ROWS, KV_HEADS, 16, 512), jnp.bfloat16),
-        scratch_shapes=[pltpu.SemaphoreType.DMA((3, KV_HEADS))],
+        scratch_shapes=[
+            pltpu.VMEM((ROWS, KV_HEADS, 16, 512), jnp.bfloat16),
+            pltpu.SemaphoreType.DMA((4, KV_HEADS)),
+        ],
         name="pack",
     )(queries, keys, values)
 
@@ -66,15 +84,15 @@
 def unpack(parts):
     return pl.pallas_call(
         unpack_body,
-        in_specs=[pl.BlockSpec(memory_space=pl.ANY)],
+        in_specs=[pl.BlockSpec(memory_space=pltpu.VMEM)],
         out_specs=pl.BlockSpec(memory_space=pl.ANY),
         out_shape=jax.ShapeDtypeStruct((ROWS, 16, 4096), jnp.bfloat16),
         scratch_shapes=[pltpu.SemaphoreType.DMA((KV_HEADS,))],
         name="unpack",
-    )(parts)
-
-
-def attend_block(i, j_low, ends_ref, qkv_ref, kv_ref, out_ref, s_ref, norm_acc):
+    )(*in_vmem(parts))
+
+
+def attend_block(i, j_low, ends_ref, qkv_ref, keys_at, values_at, out_ref, s_ref, norm_acc):
     first = pl.multiple_of(i * TQ, TQ)
     slot = (i // 2) * 4 + i % 2
     count = (HALO + first) // TK + 1 - j_low
@@ -88,7 +106,7 @@
             at = pl.multiple_of((j_low + n) * TK, TK)
             s = lax.dot_general(
                 both,
-                kv_ref[pl.ds(at, TK), 0:128],
+                keys_at(at),
                 (((1,), (1,)), ((), ())),
                 preferred_element_type=jnp.float32,
             )
@@ -110,15 +128,15 @@
             part = w[:, 0:128] + w[:, 128:256]
             o = jnp.dot(
                 w.astype(jnp.bfloat16),
-                kv_ref[pl.ds(at, TK), 128:256],
+                values_at(at),
                 preferred_element_type=jnp.float32,
             )
             total = part if total is None else total + part
             acc = o if acc is None else acc + o
         total = jnp.sum(total, axis=1, keepdims=True)
         result = (acc / total).astype(jnp.bfloat16)
-        out_ref[pl.ds(first, TQ), 0:128] = result[0:TQ]
-        out_ref[pl.ds(first, TQ), 128:256] = result[TQ : 2 * TQ]
+        out_ref[i, :, 0:128] = result[0:TQ]
+        out_ref[i, :, 128:256] = result[TQ : 2 * TQ]
         norm = top * SCALE + jnp.log(total)
         lanes = lax.broadcasted_iota(jnp.int32, (TQ, 128), 1)
         held = jnp.where(lanes == slot, norm[0:TQ], norm_acc[...])
@@ -131,18 +149,31 @@
             body(blocks)
 
 
-def local_body(low_ref, ends_ref, qkv_ref, out_ref, norm_ref, kv_ref, s_ref):
-    kv_ref[HALO : HALO + SPAN] = qkv_ref[:, 256:512]
+def out_copy(i, held_ref, out_ref, sems):
+    return pltpu.make_async_copy(held_ref.at[i], out_ref.at[pl.ds(i * TQ, TQ)], sems.at[i])
+
+
+def local_body(low_ref, ends_ref, qkv_ref, out_ref, norm_ref, held_ref, s_ref, sems):
     norm_ref[...] = jnp.zeros((TQ, 128), jnp.float32)
+    keys_at = lambda at: qkv_ref[pl.ds(pl.multiple_of(at - HALO, TK), TK), 256:384]
+    values_at = lambda at: qkv_ref[pl.ds(pl.multiple_of(at - HALO, TK), TK), 384:512]
 
     def block(i, carry):
         @pl.when(low_ref[i] >= HALO)
         def _():
-            attend_block(i, low_ref[i] // TK, ends_ref, qkv_ref, kv_ref, out_ref, s_ref, norm_ref)
+            attend_block(
+                i, low_ref[i] // TK, ends_ref, qkv_ref, keys_at, values_at, held_ref, s_ref, norm_ref
+            )
+            out_copy(i, held_ref, out_ref, sems).start()
 
         return carry
 
     lax.fori_loop(0, BLOCKS, block, 0)
+    for i in range(BLOCKS):
+
+        @pl.when(low_ref[i] >= HALO)
+        def _():
+            out_copy(i, held_ref, out_ref, sems).wait()
 
 
 def attend_local(low, ends, qkv):
@@ -150,62 +181,75 @@
     return pl.pallas_call(
         local_body,
         in_specs=[pl.BlockSpec(memory_space=pltpu.SMEM), vmem, vmem],
-        out_specs=[vmem, vmem],
+        out_specs=[pl.BlockSpec(memory_space=pl.ANY), vmem],
         out_shape=[
             jax.ShapeDtypeStruct((SPAN, 256), jnp.bfloat16),
             jax.ShapeDtypeStruct((TQ, 128), jnp.float32),
         ],
         scratch_shapes=[
-            pltpu.VMEM((HALO + SPAN, 256), jnp.bfloat16),
+            pltpu.VMEM((BLOCKS, TQ, 256), jnp.bfloat16),
             pltpu.VMEM((MOST_BLOCKS, 2 * TQ, TK), jnp.float32),
+            pltpu.SemaphoreType.DMA((BLOCKS,)),
         ],
         name="attend_local",
-    )(low, ends, qkv)
-
-
-def halo_body(low_ref, ends_ref, qkv_ref, halo_ref, prev_ref, prev_norm, out_ref, norm_ref, kv_ref, s_ref, norm_acc):
+    )(low, ends, *in_vmem(qkv))
+
+
+def halo_body(
+    low_ref, ends_ref, qkv_ref, halo_ref, prev_ref, prev_norm, out_ref, norm_ref, kv_ref, held_ref, s_ref, norm_acc, sems
+):
     kv_ref[0:HALO] = halo_ref[...]
-    kv_ref[HALO : 2 * HALO] = qkv_ref[:, 256:512]
-    out_ref[...] = prev_ref[...]
+    kv_ref[HALO : 2 * HALO] = qkv_ref[0:HALO, 256:512]
     norm_acc[...] = prev_norm[...]
+    keys_at = lambda at: kv_ref[pl.ds(at, TK), 0:128]
+    values_at = lambda at: kv_ref[pl.ds(at, TK), 128:256]
 
     def block(i, carry):
         @pl.when(low_ref[i] < HALO)
         def _():
-            attend_block(i, low_ref[i] // TK, ends_ref, qkv_ref, kv_ref, out_ref, s_ref, norm_acc)
+            attend_block(
+                i, low_ref[i] // TK, ends_ref, qkv_ref, keys_at, values_at, held_ref, s_ref, norm_acc
+            )
+            out_copy(i, held_ref, out_ref, sems).start()
 
         return carry
 
     lax.fori_loop(0, HALO_BLOCKS, block, 0)
     norm_ref[...] = jnp.transpose(norm_acc[...])[0:32]
+    for i in range(HALO_BLOCKS):
+
+        @pl.when(low_ref[i] < HALO)
+        def _():
+            out_copy(i, held_ref, out_ref, sems).wait()
 
 
 def attend_halo(low, ends, qkv, halo, out, norm):
-    at_first = lambda *shape: pl.BlockSpec(shape, lambda n: (0, 0))
+    vmem = pl.BlockSpec(memory_space=pltpu.VMEM)
     return pl.pallas_call(
         halo_body,
-        grid=(1,),
         in_specs=[
             pl.BlockSpec(memory_space=pltpu.SMEM),
-            at_first(12, TK),
-            at_first(HALO, 512),
-            at_first(HALO, 256),
-            at_first(HALO, 256),
-            at_first(TQ, 128),
-        ],
-        out_specs=[at_first(HALO, 256), at_first(32, 128)],
+            vmem,
+            vmem,
+            vmem,
+            pl.BlockSpec(memory_space=pl.ANY),
+            vmem,
+        ],
+        out_specs=[pl.BlockSpec(memory_space=pl.ANY), vmem],
         out_shape=[
             jax.ShapeDtypeStruct((SPAN, 256), jnp.bfloat16),
-            jax.ShapeDtypeStruct((32, 128), jnp.float32),
+            pltpu.VMEM((32, 128), jnp.float32),
         ],
         scratch_shapes=[
             pltpu.VMEM((2 * HALO, 256), jnp.bfloat16),
+            pltpu.VMEM((HALO_BLOCKS, TQ, 256), jnp.bfloat16),
             pltpu.VMEM((MOST_BLOCKS, 2 * TQ, TK), jnp.float32),
             pltpu.VMEM((TQ, 128), jnp.float32),
+            pltpu.SemaphoreType.DMA((HALO_BLOCKS,)),
         ],
         input_output_aliases={4: 0},
         name="attend_halo",
-    )(low, ends, qkv, halo, out, norm)
+    )(low, ends, *in_vmem(qkv, halo), out, norm)
 
 
 def doc_bounds(lengths, row, base):

time: 245 us -> 148 us (0.60)
  Pallas kernels: 113 us -> 17.2 us
  waiting for transfers between devices: 54 us -> 51.4 us
    pallas_call x1, Pallas kernels: 65.1 us -> 2.9 us  [pack(): pl.pallas_call(pack_body, in_specs=[pl.BlockSpec(memory_space=pl.ANY)] *...]
    pallas_call x2, Pallas kernels: 40.9 us -> 5.08 us  [the longest x1 3.99 us: attend_halo(): pl.pallas_call(halo_body, in_specs=[pl.BlockSpec(memory_space=pltpu.SMEM)...]
    ppermute x1, waiting for transfers between devices: 3.88 us -> 1.29 us  [per_device(): lax.ppermute(qkv[SPAN - HALO:, 256:512], 'x', [(i, i + 1) for i in range(...]
    pallas_call x1, Pallas kernels: 6.66 us -> 9.22 us  [attend_local(): pl.pallas_call(local_body, in_specs=[pl.BlockSpec(memory_space=pltpu.SMEM...]
  transfers between devices with their start and end apart: 3 -> 3, of which waited for: 2 -> 2; matrix products, arithmetic and copies ran while one was open for 1% -> 2% of each run, Pallas kernels for 3% -> 6%
where the time goes in v3:
time: 148 us; the launch traced here: 146 us
  waiting for transfers between devices  51.4 us (35%)
  blocking collectives  43.7 us (30%)
  starting transfers between devices  31 us (21%)
  Pallas kernels  17.2 us (12%)
  other arithmetic  1.61 us (1%)
    all_to_all x1, waiting for transfers between devices, per_device(): moved = lax.all_to_all(packed, PLANE, 0, 0, tiled=True)  50.1 us
    all_gather x1, blocking collectives, per_device(): norms = lax.all_gather(norm, 'z', axis=0, tiled=False)  43.7 us
    all_to_all x1, starting transfers between devices, per_device(): moved = lax.all_to_all(packed, PLANE, 0, 0, tiled=True)  17 us
    all_to_all x1, starting transfers between devices, per_device(): back = lax.all_to_all(out.reshape(128, 16, 256), PLANE, 0, 0, tiled=True)  10.5 us
    pallas_call x1, Pallas kernels, attend_local(): pl.pallas_call(local_body, in_specs=[pl.BlockSpec(memory_space=pltpu.SMEM...  9.22 us
    pallas_call x1, Pallas kernels, attend_halo(): pl.pallas_call(halo_body, in_specs=[pl.BlockSpec(memory_space=pltpu.SMEM)...  3.99 us
    ppermute x1, starting transfers between devices, per_device(): lax.ppermute(qkv[SPAN - HALO:, 256:512], 'x', [(i, i + 1) for i in range(...  3.4 us
  transfers between devices with their start and end apart: 3, of which 2 were waited for; matrix products, arithmetic and copies ran while one was open for 2% of the time, Pallas kernels for 6%

profile of v3, /device:TPU:34, one launch (start us, length us, event | category | flops | bytes accessed | tf_op | source)
XLA Modules:
  0.0 146.4 jit_solution(2190691588561512509)
XLA Ops:
  0.6 0.0 copy-start
  0.6 2.9 %pack.1 = bf16[8,16,16,512]{3,2,1,0:T(8,128)(2,1)} custom-call(bf16[8,16,4096]{2,1,0:T(8,128)(2,1)} %q_ref.1, bf16[8,16,2048]{2,1,0:T(8,128)(2,1)} %k_ref.1, bf16[8,16,2048]{2,1,0:T(8,128)(2,1)} %v_ref.1), custom_call_target="tpu_custom_call" | custom-call | tf_op jit(solution)/shard_map/pack/pallas_call | solution.py:58
  3.6 17.0 %all-to-all-start = ((bf16[128,16,512]{2,1,0:T(8,128)(2,1)}), bf16[128,16,512]{2,1,0:T(8,128)(2,1)S(1)}, u32[]{:S(2)}, u32[]{:S(2)}) async-start(bf16[128,16,512]{2,1,0:T(8,128)(2,1)} %bitcast.12), calls=%async_computation | async-start | bytes 4194304 | tf_op jit(solution)/shard_map/all_to_all | solution.py:270
  20.6 0.0 copy-done
  20.7 0.1 select_reduce_fusion.1
  20.8 0.2 select_reduce_fusion
  20.9 50.1 %all-to-all-done = bf16[128,16,512]{2,1,0:T(8,128)(2,1)S(1)} async-done(((bf16[128,16,512]{2,1,0:T(8,128)(2,1)}), bf16[128,16,512]{2,1,0:T(8,128)(2,1)S(1)}, u32[]{:S(2)}, u32[]{:S(2)}) %all-to-all-start) | async-done | bytes 2097184 | tf_op jit(solution)/shard_map/all_to_all | solution.py:270
  71.1 3.4 %collective-permute-start = (bf16[1024,256]{1,0:T(8,128)(2,1)S(1)}, bf16[1024,256]{1,0:T(8,128)(2,1)S(1)}, u32[]{:S(2)}, u32[]{:S(2)}) collective-permute-start(bf16[1024,256]{1,0:T(8,128)(2,1)S(1)} %slice.4), channel_id=1, source_target_pairs={{0,128},{128,256},{256,384},{1,129},{129,257},{257,385},{2,130},{1... | collective-permute-start | bytes 1572872 | tf_op jit(solution)/shard_map/ppermute | solution.py:272
  74.5 0.2 select_reduce_fusion.2
  74.7 0.5 subtract_add_fusion.1.low_ref
  75.2 0.6 subtract_add_fusion.ends_ref
  75.8 9.2 %attend_local.1 = (bf16[2048,256]{1,0:T(8,128)(2,1)}, f32[128,128]{1,0:T(8,128)}) custom-call(s32[16]{0:T(128)} %subtract_add_fusion.1.low_ref, s32[12,256]{1,0:T(8,128)} %subtract_add_fusion.ends_ref, bf16[2048,512]{1,0:T(8,128)(2,1)S(1)} %bitcast.9), custom_call_target="tpu_custom_call" | custom-call | tf_op jit(solution)/shard_map/attend_local/pallas_call | solution.py:181
  85.1 1.3 collective-permute-done.halo_ref
  86.4 4.0 %attend_halo.1 = (bf16[2048,256]{1,0:T(8,128)(2,1)}, f32[32,128]{1,0:T(8,128)S(1)}) custom-call(s32[16]{0:T(128)} %subtract_add_fusion.1.low_ref, s32[12,256]{1,0:T(8,128)} %subtract_add_fusion.ends_ref, bf16[2048,512]{1,0:T(8,128)(2,1)S(1)} %bitcast.10, bf16[1024,256]{1,0:T(8,128)(2,1)S(1)} %collective-permute-done.halo_ref, ...), custom_call_target="tpu_custom_call", output_to_operand_aliasing={{0}: (4, {})} | custom-call | tf_op jit(solution)/shard_map/attend_halo/pallas_call | solution.py:228
  90.4 10.5 %all-to-all-start.1 = ((bf16[128,16,256]{2,1,0:T(8,128)(2,1)}), bf16[128,16,256]{2,1,0:T(8,128)(2,1)S(1)}, u32[]{:S(2)}, u32[]{:S(2)}) async-start(bf16[128,16,256]{2,1,0:T(8,128)(2,1)} %bitcast.13), calls=%async_computation.1 | async-start | bytes 2097152 | tf_op jit(solution)/shard_map/all_to_all | solution.py:275
  100.9 43.7 %all-gather = f32[256,128]{1,0:T(8,128)S(1)} all-gather(f32[32,128]{1,0:T(8,128)S(1)} %get-tuple-element.9), channel_id=2, replica_groups=mesh['x'=4,'z'=8,'y'=8,'c'=2] {'z'}, dimensions={0}, use_global_device_ids=true | all-gather | bytes 147456 | tf_op jit(solution)/shard_map/all_gather | solution.py:277
  144.7 0.6 copy.8
  145.3 0.0 all-to-all-done.1
  145.3 1.1 unpack.1
  (6 shorter events, 0.1 us)
Async XLA Ops:
  0.6 20.0 %copy-start = (s32[8,32]{1,0:T(8,128)S(1)}, s32[8,32]{1,0:T(8,128)}, u32[]{:S(2)}) copy-start(s32[8,32]{1,0:T(8,128)} %param.7) | copy-start | bytes 3076
  3.6 67.5 %all-to-all-start = ((bf16[128,16,512]{2,1,0:T(8,128)(2,1)}), bf16[128,16,512]{2,1,0:T(8,128)(2,1)S(1)}, u32[]{:S(2)}, u32[]{:S(2)}) async-start(bf16[128,16,512]{2,1,0:T(8,128)(2,1)} %bitcast.12), calls=%async_computation | async-start | bytes 4194304 | tf_op jit(solution)/shard_map/all_to_all | solution.py:270
  71.1 15.3 %collective-permute-start = (bf16[1024,256]{1,0:T(8,128)(2,1)S(1)}, bf16[1024,256]{1,0:T(8,128)(2,1)S(1)}, u32[]{:S(2)}, u32[]{:S(2)}) collective-permute-start(bf16[1024,256]{1,0:T(8,128)(2,1)S(1)} %slice.4), channel_id=1, source_target_pairs={{0,128},{128,256},{256,384},{1,129},{129,257},{257,385},{2,130},{1... | collective-permute-start | bytes 1572872 | tf_op jit(solution)/shard_map/ppermute | solution.py:272
  90.4 54.9 %all-to-all-start.1 = ((bf16[128,16,256]{2,1,0:T(8,128)(2,1)}), bf16[128,16,256]{2,1,0:T(8,128)(2,1)S(1)}, u32[]{:S(2)}, u32[]{:S(2)}) async-start(bf16[128,16,256]{2,1,0:T(8,128)(2,1)} %bitcast.13), calls=%async_computation.1 | async-start | bytes 2097152 | tf_op jit(solution)/shard_map/all_to_all | solution.py:275

commit v4 on v3

--- a/solution.py
+++ b/solution.py
@@ -16,6 +16,7 @@
 MOST_BLOCKS = 5
 BLOCKS = SPAN // TQ
 HALO_BLOCKS = HALO // TQ
+FAR = 1 << 20
 LOG2E = 1.4426950408889634
 SCALE = HEAD ** (-0.5)
 ALL = ("x", "z", "y", "c")
@@ -24,6 +25,41 @@
 
 def in_vmem(*arrays):
     return [pltpu.with_memory_space_constraint(a, pltpu.VMEM) for a in arrays]
+
+
+def doc_bounds(lengths_ref, row, base, low_ref, ends_ref):
+    origin = HALO - base
+    slot = lax.broadcasted_iota(jnp.int32, (12, TK), 0) * TK
+    slot = slot + lax.broadcasted_iota(jnp.int32, (12, TK), 1)
+    end = origin
+    low = [origin] * BLOCKS
+    after = jnp.full((12, TK), FAR, jnp.int32)
+    for n in range(32):
+        end = end + lengths_ref[row, n]
+        low = [jnp.where(end <= HALO + i * TQ, end, low[i]) for i in range(BLOCKS)]
+        after = jnp.minimum(after, jnp.where(slot < end, end, FAR))
+    ends_ref[...] = jnp.where(slot < origin, 0, after)
+    for i in range(BLOCKS):
+        low_ref[i] = low[i]
+    low_ref[BLOCKS] = row
+
+
+def bounds_body(lengths_ref, row_ref, base_ref, low_ref, ends_ref):
+    doc_bounds(lengths_ref, row_ref[0], base_ref[0], low_ref, ends_ref)
+
+
+def bounds(lengths, row, base):
+    smem = pl.BlockSpec(memory_space=pltpu.SMEM)
+    return pl.pallas_call(
+        bounds_body,
+        in_specs=[smem] * 3,
+        out_specs=[smem, pl.BlockSpec(memory_space=pltpu.VMEM)],
+        out_shape=[
+            jax.ShapeDtypeStruct((BLOCKS + 1,), jnp.int32),
+            jax.ShapeDtypeStruct((12, TK), jnp.int32),
+        ],
+        name="doc_bounds",
+    )(lengths, row, base)
 
 
 def pack_body(q_ref, k_ref, v_ref, out_ref, held_ref, sems):
@@ -94,7 +130,7 @@
 
 def attend_block(i, j_low, ends_ref, qkv_ref, keys_at, values_at, out_ref, s_ref, norm_acc):
     first = pl.multiple_of(i * TQ, TQ)
-    slot = (i // 2) * 4 + i % 2
+    slot = (i // 2) * 8 + i % 2
     count = (HALO + first) // TK + 1 - j_low
 
     def body(blocks):
@@ -196,8 +232,10 @@
 
 
 def halo_body(
-    low_ref, ends_ref, qkv_ref, halo_ref, prev_ref, prev_norm, out_ref, norm_ref, kv_ref, held_ref, s_ref, norm_acc, sems
+    low_ref, ends_ref, qkv_ref, halo_ref, prev_ref, prev_norm, *refs
 ):
+    out_ref, *norm_refs = refs[:9]
+    kv_ref, held_ref, s_ref, norm_acc, norm_t, sems = refs[9:]
     kv_ref[0:HALO] = halo_ref[...]
     kv_ref[HALO : 2 * HALO] = qkv_ref[0:HALO, 256:512]
     norm_acc[...] = prev_norm[...]
@@ -215,7 +253,9 @@
         return carry
 
     lax.fori_loop(0, HALO_BLOCKS, block, 0)
-    norm_ref[...] = jnp.transpose(norm_acc[...])[0:32]
+    norm_t[...] = jnp.transpose(norm_acc[...])
+    for d in range(8):
+        norm_refs[d][...] = norm_t[pl.ds(pl.multiple_of(((low_ref[BLOCKS] + d) % 8) * 8, 8), 8)]
     for i in range(HALO_BLOCKS):
 
         @pl.when(low_ref[i] < HALO)
@@ -235,16 +275,15 @@
             pl.BlockSpec(memory_space=pl.ANY),
             vmem,
         ],
-        out_specs=[pl.BlockSpec(memory_space=pl.ANY), vmem],
-        out_shape=[
-            jax.ShapeDtypeStruct((SPAN, 256), jnp.bfloat16),
-            pltpu.VMEM((32, 128), jnp.float32),
-        ],
+        out_specs=[pl.BlockSpec(memory_space=pl.ANY)] + [vmem] * 8,
+        out_shape=[jax.ShapeDtypeStruct((SPAN, 256), jnp.bfloat16)]
+        + [pltpu.VMEM((8, 128), jnp.float32)] * 8,
         scratch_shapes=[
             pltpu.VMEM((2 * HALO, 256), jnp.bfloat16),
             pltpu.VMEM((HALO_BLOCKS, TQ, 256), jnp.bfloat16),
             pltpu.VMEM((MOST_BLOCKS, 2 * TQ, TK), jnp.float32),
             pltpu.VMEM((TQ, 128), jnp.float32),
+            pltpu.VMEM((TQ, 128), jnp.float32),
             pltpu.SemaphoreType.DMA((HALO_BLOCKS,)),
         ],
         input_output_aliases={4: 0},
@@ -252,31 +291,44 @@
     )(low, ends, *in_vmem(qkv, halo), out, norm)
 
 
-def doc_bounds(lengths, row, base):
-    own = lax.dynamic_index_in_dim(lengths, row, 0, keepdims=False)
-    upto = jnp.arange(32)[:, None] <= jnp.arange(32)[None, :]
-    ends = jnp.sum(jnp.where(upto, own[:, None], 0), axis=0)
-    first = base + jnp.arange(BLOCKS, dtype=jnp.int32) * TQ
-    low = jnp.max(jnp.where(ends[None, :] <= first[:, None], ends[None, :], 0), axis=1)
-    pos = (base - HALO) + jnp.arange(HALO + SPAN, dtype=jnp.int32).reshape(12, TK)
-    after = jnp.where(ends[:, None, None] > pos[None], ends[:, None, None], 1 << 20)
-    end = jnp.where(pos >= 0, jnp.min(after, axis=0), -(1 << 20))
-    return low - base + HALO, end - base + HALO
+def norm_body(row_ref, *refs):
+    *pieces, out_ref = refs
+    rows = lax.broadcasted_iota(jnp.int32, (8, 128), 0)
+    for h in range(2):
+        for n in range(2):
+            at = 2 * h + n
+            held = jnp.zeros((8, 128), jnp.float32)
+            for d in range(8):
+                held = jnp.where(rows == (row_ref[0] + 8 - d) % 8, pieces[d][at : at + 1], held)
+            out_ref[h, :, n * 128 : (n + 1) * 128] = held
+
+
+def norm_rows(row, pieces):
+    vmem = pl.BlockSpec(memory_space=pltpu.VMEM)
+    return pl.pallas_call(
+        norm_body,
+        in_specs=[pl.BlockSpec(memory_space=pltpu.SMEM)] + [vmem] * 8,
+        out_specs=vmem,
+        out_shape=jax.ShapeDtypeStruct((2, ROWS, 256), jnp.float32),
+        name="norm_rows",
+    )(row, *pieces)
 
 
 def per_device(queries, keys, values, lengths):
-    low, ends = doc_bounds(lengths, lax.axis_index("z"), lax.axis_index("x") * SPAN)
+    row = lax.axis_index("z")
+    base = lax.axis_index("x") * SPAN
     packed = pack(queries, keys, values).reshape(128, 16, 512)
     moved = lax.all_to_all(packed, PLANE, 0, 0, tiled=True)
+    low, ends = bounds(lengths, row[None], base[None])
     qkv = moved.reshape(SPAN, 512)
     halo = lax.ppermute(qkv[SPAN - HALO :, 256:512], "x", [(i, i + 1) for i in range(3)])
     out, norm = attend_local(low, ends, qkv)
-    out, norm = attend_halo(low, ends, qkv, halo, out, norm)
+    out, *norms = attend_halo(low, ends, qkv, halo, out, norm)
     back = lax.all_to_all(out.reshape(128, 16, 256), PLANE, 0, 0, tiled=True)
     attended = unpack(back.reshape(ROWS, KV_HEADS, 16, 256))
-    norms = lax.all_gather(norm, "z", axis=0, tiled=False)
-    norms = lax.dynamic_slice_in_dim(norms, lax.axis_index("z") * 4, 4, 1)
-    return attended, jnp.transpose(norms.reshape(8, 2, 256), (1, 0, 2))
+    for d in range(1, 8):
+        norms[d] = lax.ppermute(norms[d], "z", [(i, (i + d) % 8) for i in range(8)])
+    return attended, norm_rows(row[None], norms)
 
 
 def solution(mesh):

time: 148 us -> 140 us (0.946)
  the two profiles are of different devices: /device:TPU:34 before, /device:TPU:4 now
where the time goes in v4:
time: 140 us; the launch traced here: 139 us
  blocking collectives  70.4 us (50%)
  starting transfers between devices  43.3 us (31%)
  Pallas kernels  18.8 us (13%)
  local copies, waits for them, and re-layouts  3.51 us (3%)
  waiting for transfers between devices  2.17 us (2%)
    all_to_all x1, blocking collectives, per_device(): moved = lax.all_to_all(packed, PLANE, 0, 0, tiled=True)  70.4 us
    ppermute x7, starting transfers between devices, per_device(): norms[d] = lax.ppermute(norms[d], 'z', [(i, (i + d) % 8) for i in range(8)])  29.9 us
    all_to_all x1, starting transfers between devices, per_device(): back = lax.all_to_all(out.reshape(128, 16, 256), PLANE, 0, 0, tiled=True)  10.3 us
    pallas_call x1, Pallas kernels, attend_local(): pl.pallas_call(local_body, in_specs=[pl.BlockSpec(memory_space=pltpu.SMEM...  9.59 us
    unnamed x20, local copies, waits for them, and re-layouts  3.48 us
    ppermute x1, starting transfers between devices, per_device(): lax.ppermute(qkv[SPAN - HALO:, 256:512], 'x', [(i, i + 1) for i in range(...  3.09 us
    pallas_call x1, Pallas kernels, pack(): pl.pallas_call(pack_body, in_specs=[pl.BlockSpec(memory_space=pl.ANY)] *...  2.91 us
  transfers between devices with their start and end apart: 9, of which 1 were waited for; matrix products, arithmetic and copies ran while one was open for 0% of the time, Pallas kernels for 9%

profile of v4, /device:TPU:4, one launch (start us, length us, event | category | flops | bytes accessed | tf_op | source)
XLA Modules:
  0.0 139.1 jit_solution(2714818618217133543)
XLA Ops:
  0.6 2.9 %pack.1 = bf16[8,16,16,512]{3,2,1,0:T(8,128)(2,1)} custom-call(bf16[8,16,4096]{2,1,0:T(8,128)(2,1)} %q_ref.1, bf16[8,16,2048]{2,1,0:T(8,128)(2,1)} %k_ref.1, bf16[8,16,2048]{2,1,0:T(8,128)(2,1)} %v_ref.1), custom_call_target="tpu_custom_call" | custom-call | tf_op jit(solution)/shard_map/pack/pallas_call | solution.py:94
  3.5 70.4 %all_to_all.10 = bf16[128,16,512]{2,1,0:T(8,128)(2,1)S(1)} all-to-all(bf16[128,16,512]{2,1,0:T(8,128)(2,1)} %bitcast.10), channel_id=1, replica_groups=mesh['x'=4,'z'=8,'y'=8,'c'=2] {'z','y','c'}, dimensions={0} | all-to-all | bytes 4194304 | tf_op jit(solution)/shard_map/all_to_all | solution.py:321
  74.0 1.3 copy-done
  75.3 3.1 %collective-permute-start = (bf16[1024,256]{1,0:T(8,128)(2,1)S(1)}, bf16[1024,256]{1,0:T(8,128)(2,1)S(1)}, u32[]{:S(2)}, u32[]{:S(2)}) collective-permute-start(bf16[1024,256]{1,0:T(8,128)(2,1)S(1)} %slice.4), channel_id=1, source_target_pairs={{0,128},{128,256},{256,384},{1,129},{129,257},{257,385},{2,130},{1... | collective-permute-start | bytes 1572872 | tf_op jit(solution)/shard_map/ppermute | solution.py:324
  78.4 1.8 %doc_bounds.1 = (s32[17]{0:T(128)}, s32[12,256]{1,0:T(8,128)}) custom-call(s32[8,32]{1,0:T(8,128)} %lengths_ref.1, s32[1]{0:T(128)} %bitcast.row_ref, s32[1]{0:T(128)} %bitcast.1.base_ref), custom_call_target="tpu_custom_call" | custom-call | tf_op jit(solution)/shard_map/doc_bounds/pallas_call | solution.py:53
  80.2 1.6 %copy-done.1 = bf16[128,16,512]{2,1,0:T(8,128)(2,1)S(1)} copy-done((bf16[128,16,512]{2,1,0:T(8,128)(2,1)S(1)}, bf16[128,16,512]{2,1,0:T(8,128)(2,1)}, u32[]{:S(2)}) %copy-start.1) | copy-done | bytes 2097176
  81.8 9.6 %attend_local.1 = (bf16[2048,256]{1,0:T(8,128)(2,1)}, f32[128,128]{1,0:T(8,128)}) custom-call(s32[17]{0:T(128)} %get-tuple-element.15.low_ref, s32[12,256]{1,0:T(8,128)} %get-tuple-element.16.ends_ref, bf16[2048,512]{1,0:T(8,128)(2,1)S(1)} %bitcast.7), custom_call_target="tpu_custom_call" | custom-call | tf_op jit(solution)/shard_map/attend_local/pallas_call | solution.py:217
  91.4 0.0 collective-permute-done.halo_ref
  91.4 2.1 %attend_halo.1 = (bf16[2048,256]{1,0:T(8,128)(2,1)}, f32[8,128]{1,0:T(8,128)S(1)}, f32[8,128]{1,0:T(8,128)S(1)}, f32[8,128]{1,0:T(8,128)S(1)}, f32[8,128]{1,0:T(...) custom-call(s32[17]{0:T(128)} %get-tuple-element.15.low_ref, ...), custom_call_target="tpu_custom_call", output_to_operand_aliasing={{0}: (4, {})} | custom-call | tf_op jit(solution)/shard_map/attend_halo/pallas_call | solution.py:268
  93.5 10.3 %all-to-all-start.1 = ((bf16[128,16,256]{2,1,0:T(8,128)(2,1)}), bf16[128,16,256]{2,1,0:T(8,128)(2,1)S(1)}, u32[]{:S(2)}, u32[]{:S(2)}) async-start(bf16[128,16,256]{2,1,0:T(8,128)(2,1)} %bitcast.11), calls=%async_computation.1 | async-start | bytes 2097152 | tf_op jit(solution)/shard_map/all_to_all | solution.py:327
  103.9 3.0 %collective-permute-start.1 = (f32[8,128]{1,0:T(8,128)S(1)}, f32[8,128]{1,0:T(8,128)S(1)}, u32[]{:S(2)}, u32[]{:S(2)}) collective-permute-start(f32[8,128]{1,0:T(8,128)S(1)} %get-tuple-element.21), channel_id=1, source_target_pairs={{0,16},{16,32},{32,48},{48,64},{64,80},{80,96},{96,112},{112,0},{1... | collective-permute-start | bytes 12296 | tf_op jit(solution)/shard_map/ppermute | solution.py:330
  106.9 4.5 %collective-permute-start.2 = (f32[8,128]{1,0:T(8,128)S(1)}, f32[8,128]{1,0:T(8,128)S(1)}, u32[]{:S(2)}, u32[]{:S(2)}) collective-permute-start(f32[8,128]{1,0:T(8,128)S(1)} %get-tuple-element.22), channel_id=1, source_target_pairs={{0,32},{16,48},{32,64},{48,80},{64,96},{80,112},{96,0},{112,16},{1... | collective-permute-start | bytes 12296 | tf_op jit(solution)/shard_map/ppermute | solution.py:330
  111.4 4.9 %collective-permute-start.3 = (f32[8,128]{1,0:T(8,128)S(1)}, f32[8,128]{1,0:T(8,128)S(1)}, u32[]{:S(2)}, u32[]{:S(2)}) collective-permute-start(f32[8,128]{1,0:T(8,128)S(1)} %get-tuple-element.23), channel_id=1, source_target_pairs={{0,48},{16,64},{32,80},{48,96},{64,112},{80,0},{96,16},{112,32},{1... | collective-permute-start | bytes 12296 | tf_op jit(solution)/shard_map/ppermute | solution.py:330
  116.3 3.8 %collective-permute-start.4 = (f32[8,128]{1,0:T(8,128)S(1)}, f32[8,128]{1,0:T(8,128)S(1)}, u32[]{:S(2)}, u32[]{:S(2)}) collective-permute-start(f32[8,128]{1,0:T(8,128)S(1)} %get-tuple-element.24), channel_id=1, source_target_pairs={{0,64},{16,80},{32,96},{48,112},{64,0},{80,16},{96,32},{112,48},{1... | collective-permute-start | bytes 12296 | tf_op jit(solution)/shard_map/ppermute | solution.py:330
  120.2 5.1 %collective-permute-start.5 = (f32[8,128]{1,0:T(8,128)S(1)}, f32[8,128]{1,0:T(8,128)S(1)}, u32[]{:S(2)}, u32[]{:S(2)}) collective-permute-start(f32[8,128]{1,0:T(8,128)S(1)} %get-tuple-element.25), channel_id=1, source_target_pairs={{0,80},{16,96},{32,112},{48,0},{64,16},{80,32},{96,48},{112,64},{1... | collective-permute-start | bytes 12296 | tf_op jit(solution)/shard_map/ppermute | solution.py:330
  125.3 0.0 collective-permute-done.1.refs_1_
  125.3 5.3 %collective-permute-start.6 = (f32[8,128]{1,0:T(8,128)S(1)}, f32[8,128]{1,0:T(8,128)S(1)}, u32[]{:S(2)}, u32[]{:S(2)}) collective-permute-start(f32[8,128]{1,0:T(8,128)S(1)} %get-tuple-element.26), channel_id=1, source_target_pairs={{0,96},{16,112},{32,0},{48,16},{64,32},{80,48},{96,64},{112,80},{1... | collective-permute-start | bytes 12296 | tf_op jit(solution)/shard_map/ppermute | solution.py:330
  130.6 3.3 %collective-permute-start.7 = (f32[8,128]{1,0:T(8,128)S(1)}, f32[8,128]{1,0:T(8,128)S(1)}, u32[]{:S(2)}, u32[]{:S(2)}) collective-permute-start(f32[8,128]{1,0:T(8,128)S(1)} %get-tuple-element.27), channel_id=1, source_target_pairs={{0,112},{16,0},{32,16},{48,32},{64,48},{80,64},{96,80},{112,96},{1... | collective-permute-start | bytes 12296 | tf_op jit(solution)/shard_map/ppermute | solution.py:330
  133.9 0.0 collective-permute-done.3.refs_3_
  133.9 0.0 collective-permute-done.6.refs_6_
  134.0 2.1 %collective-permute-done.7.refs_7_ = f32[8,128]{1,0:T(8,128)S(1)} collective-permute-done((f32[8,128]{1,0:T(8,128)S(1)}, f32[8,128]{1,0:T(8,128)S(1)}, u32[]{:S(2)}, u32[]{:S(2)}) %collective-permute-start.7) | collective-permute-done | bytes 4128 | tf_op jit(solution)/shard_map/ppermute | solution.py:330
  136.2 0.5 copy-done.9
  136.7 1.3 norm_rows.1
  138.0 1.1 unpack.1
  (22 shorter events, 0.1 us)
Async XLA Ops:
  74.0 1.3 copy-start
  75.3 16.1 %collective-permute-start = (bf16[1024,256]{1,0:T(8,128)(2,1)S(1)}, bf16[1024,256]{1,0:T(8,128)(2,1)S(1)}, u32[]{:S(2)}, u32[]{:S(2)}) collective-permute-start(bf16[1024,256]{1,0:T(8,128)(2,1)S(1)} %slice.4), channel_id=1, source_target_pairs={{0,128},{128,256},{256,384},{1,129},{129,257},{257,385},{2,130},{1... | collective-permute-start | bytes 1572872 | tf_op jit(solution)/shard_map/ppermute | solution.py:324
  80.2 1.6 %copy-start.1 = (bf16[128,16,512]{2,1,0:T(8,128)(2,1)S(1)}, bf16[128,16,512]{2,1,0:T(8,128)(2,1)}, u32[]{:S(2)}) copy-start(bf16[128,16,512]{2,1,0:T(8,128)(2,1)} %copy-done) | copy-start | bytes 6291460
  93.5 42.6 %copy-start.2 = (f32[8,128]{1,0:T(8,128)}, f32[8,128]{1,0:T(8,128)S(1)}, u32[]{:S(2)}) copy-start(f32[8,128]{1,0:T(8,128)S(1)} %get-tuple-element.20.refs_0_) | copy-start | bytes 12292
  93.5 44.5 %all-to-all-start.1 = ((bf16[128,16,256]{2,1,0:T(8,128)(2,1)}), bf16[128,16,256]{2,1,0:T(8,128)(2,1)S(1)}, u32[]{:S(2)}, u32[]{:S(2)}) async-start(bf16[128,16,256]{2,1,0:T(8,128)(2,1)} %bitcast.11), calls=%async_computation.1 | async-start | bytes 2097152 | tf_op jit(solution)/shard_map/all_to_all | solution.py:327
  103.9 21.4 %collective-permute-start.1 = (f32[8,128]{1,0:T(8,128)S(1)}, f32[8,128]{1,0:T(8,128)S(1)}, u32[]{:S(2)}, u32[]{:S(2)}) collective-permute-start(f32[8,128]{1,0:T(8,128)S(1)} %get-tuple-element.21), channel_id=1, source_target_pairs={{0,16},{16,32},{32,48},{48,64},{64,80},{80,96},{96,112},{112,0},{1... | collective-permute-start | bytes 12296 | tf_op jit(solution)/shard_map/ppermute | solution.py:330
  106.9 23.7 %collective-permute-start.2 = (f32[8,128]{1,0:T(8,128)S(1)}, f32[8,128]{1,0:T(8,128)S(1)}, u32[]{:S(2)}, u32[]{:S(2)}) collective-permute-start(f32[8,128]{1,0:T(8,128)S(1)} %get-tuple-element.22), channel_id=1, source_target_pairs={{0,32},{16,48},{32,64},{48,80},{64,96},{80,112},{96,0},{112,16},{1... | collective-permute-start | bytes 12296 | tf_op jit(solution)/shard_map/ppermute | solution.py:330
  111.4 22.5 %collective-permute-start.3 = (f32[8,128]{1,0:T(8,128)S(1)}, f32[8,128]{1,0:T(8,128)S(1)}, u32[]{:S(2)}, u32[]{:S(2)}) collective-permute-start(f32[8,128]{1,0:T(8,128)S(1)} %get-tuple-element.23), channel_id=1, source_target_pairs={{0,48},{16,64},{32,80},{48,96},{64,112},{80,0},{96,16},{112,32},{1... | collective-permute-start | bytes 12296 | tf_op jit(solution)/shard_map/ppermute | solution.py:330
  116.3 17.6 %collective-permute-start.4 = (f32[8,128]{1,0:T(8,128)S(1)}, f32[8,128]{1,0:T(8,128)S(1)}, u32[]{:S(2)}, u32[]{:S(2)}) collective-permute-start(f32[8,128]{1,0:T(8,128)S(1)} %get-tuple-element.24), channel_id=1, source_target_pairs={{0,64},{16,80},{32,96},{48,112},{64,0},{80,16},{96,32},{112,48},{1... | collective-permute-start | bytes 12296 | tf_op jit(solution)/shard_map/ppermute | solution.py:330
  120.2 13.8 %collective-permute-start.5 = (f32[8,128]{1,0:T(8,128)S(1)}, f32[8,128]{1,0:T(8,128)S(1)}, u32[]{:S(2)}, u32[]{:S(2)}) collective-permute-start(f32[8,128]{1,0:T(8,128)S(1)} %get-tuple-element.25), channel_id=1, source_target_pairs={{0,80},{16,96},{32,112},{48,0},{64,16},{80,32},{96,48},{112,64},{1... | collective-permute-start | bytes 12296 | tf_op jit(solution)/shard_map/ppermute | solution.py:330
  125.3 10.8 %copy-start.3 = (f32[8,128]{1,0:T(8,128)}, f32[8,128]{1,0:T(8,128)S(1)}, u32[]{:S(2)}) copy-start(f32[8,128]{1,0:T(8,128)S(1)} %collective-permute-done.1.refs_1_) | copy-start | bytes 12292
  125.3 8.6 %collective-permute-start.6 = (f32[8,128]{1,0:T(8,128)S(1)}, f32[8,128]{1,0:T(8,128)S(1)}, u32[]{:S(2)}, u32[]{:S(2)}) collective-permute-start(f32[8,128]{1,0:T(8,128)S(1)} %get-tuple-element.26), channel_id=1, source_target_pairs={{0,96},{16,112},{32,0},{48,16},{64,32},{80,48},{96,64},{112,80},{1... | collective-permute-start | bytes 12296 | tf_op jit(solution)/shard_map/ppermute | solution.py:330
  130.6 5.5 %copy-start.4 = (f32[8,128]{1,0:T(8,128)}, f32[8,128]{1,0:T(8,128)S(1)}, u32[]{:S(2)}) copy-start(f32[8,128]{1,0:T(8,128)S(1)} %collective-permute-done.2.refs_2_) | copy-start | bytes 12292
  130.6 5.5 %collective-permute-start.7 = (f32[8,128]{1,0:T(8,128)S(1)}, f32[8,128]{1,0:T(8,128)S(1)}, u32[]{:S(2)}, u32[]{:S(2)}) collective-permute-start(f32[8,128]{1,0:T(8,128)S(1)} %get-tuple-element.27), channel_id=1, source_target_pairs={{0,112},{16,0},{32,16},{48,32},{64,48},{80,64},{96,80},{112,96},{1... | collective-permute-start | bytes 12296 | tf_op jit(solution)/shard_map/ppermute | solution.py:330
  133.9 2.2 %copy-start.5 = (f32[8,128]{1,0:T(8,128)}, f32[8,128]{1,0:T(8,128)S(1)}, u32[]{:S(2)}) copy-start(f32[8,128]{1,0:T(8,128)S(1)} %collective-permute-done.3.refs_3_) | copy-start | bytes 12292
  133.9 2.2 %copy-start.6 = (f32[8,128]{1,0:T(8,128)}, f32[8,128]{1,0:T(8,128)S(1)}, u32[]{:S(2)}) copy-start(f32[8,128]{1,0:T(8,128)S(1)} %collective-permute-done.4.refs_4_) | copy-start | bytes 12292
  133.9 2.2 %copy-start.7 = (f32[8,128]{1,0:T(8,128)}, f32[8,128]{1,0:T(8,128)S(1)}, u32[]{:S(2)}) copy-start(f32[8,128]{1,0:T(8,128)S(1)} %collective-permute-done.5.refs_5_) | copy-start | bytes 12292
  133.9 2.2 %copy-start.8 = (f32[8,128]{1,0:T(8,128)}, f32[8,128]{1,0:T(8,128)S(1)}, u32[]{:S(2)}) copy-start(f32[8,128]{1,0:T(8,128)S(1)} %collective-permute-done.6.refs_6_) | copy-start | bytes 12292
  136.1 0.6 copy-start.9

commit v5 on v4

v5 whole, which is shorter than its diff:
```python
import jax
import jax.numpy as jnp
from jax import lax
from jax.experimental import pallas as pl
from jax.experimental.pallas import tpu as pltpu
from jax.sharding import Mesh
from jax.sharding import PartitionSpec as P

HEAD = 128
ROWS = 8
KV_HEADS = 16
HALO = 1024
SPAN = 2048
TQ = 128
TK = 256
MOST_BLOCKS = 5
BLOCKS = SPAN // TQ
HALO_BLOCKS = HALO // TQ
FAR = 1 << 20
LOG2E = 1.4426950408889634
SCALE = HEAD ** (-0.5)
ALL = ("x", "z", "y", "c")
PLANE = ("z", "y", "c")


def in_vmem(*arrays):
    return [pltpu.with_memory_space_constraint(a, pltpu.VMEM) for a in arrays]


def doc_bounds(lengths_ref, row, base, low_ref, ends_ref):
    origin = HALO - base
    slot = lax.broadcasted_iota(jnp.int32, (12, TK), 0) * TK
    slot = slot + lax.broadcasted_iota(jnp.int32, (12, TK), 1)
    end = origin
    low = [origin] * BLOCKS
    after = jnp.full((12, TK), FAR, jnp.int32)
    for n in range(32):
        end = end + lengths_ref[row, n]
        low = [jnp.where(end <= HALO + i * TQ, end, low[i]) for i in range(BLOCKS)]
        after = jnp.minimum(after, jnp.where(slot < end, end, FAR))
    ends_ref[...] = jnp.where(slot < origin, 0, after)
    for i in range(BLOCKS):
        low_ref[i] = low[i]
    low_ref[BLOCKS] = row


def bounds_body(lengths_ref, row_ref, base_ref, low_ref, ends_ref):
    doc_bounds(lengths_ref, row_ref[0], base_ref[0], low_ref, ends_ref)


def bounds(lengths, row, base):
    smem = pl.BlockSpec(memory_space=pltpu.SMEM)
    return pl.pallas_call(
        bounds_body,
        in_specs=[smem] * 3,
        out_specs=[smem, pl.BlockSpec(memory_space=pltpu.VMEM)],
        out_shape=[
            jax.ShapeDtypeStruct((BLOCKS + 1,), jnp.int32),
            jax.ShapeDtypeStruct((12, TK), jnp.int32),
        ],
        name="doc_bounds",
    )(lengths, row, base)


def pack_body(q_ref, k_ref, v_ref, out_ref, held_ref, sems):
    parts = ((q_ref, 256, 0), (k_ref, 128, 256), (v_ref, 128, 384))
    reads = [
        [
            pltpu.make_async_copy(
                ref.at[:, :, pl.ds(h * width, width)],
                held_ref.at[:, h, :, pl.ds(at, width)],
                sems.at[n, h],
            )
            for n, (ref, width, at) in enumerate(parts)
        ]
        for h in range(KV_HEADS)
    ]
    writes = [
        pltpu.make_async_copy(held_ref.at[:, h], out_ref.at[:, h], sems.at[3, h])
        for h in range(KV_HEADS)
    ]
    for copies in reads:
        for copy in copies:
            copy.start()
    for h in range(KV_HEADS):
        for copy in reads[h]:
            copy.wait()
        writes[h].start()
    for copy in writes:
        copy.wait()


def pack(queries, keys, values):
    return pl.pallas_call(
        pack_body,
        in_specs=[pl.BlockSpec(memory_space=pl.ANY)] * 3,
        out_specs=pl.BlockSpec(memory_space=pl.ANY),
        out_shape=jax.ShapeDtypeStruct((ROWS, KV_HEADS, 16, 512), jnp.bfloat16),
        scratch_shapes=[
            pltpu.VMEM((ROWS, KV_HEADS, 16, 512), jnp.bfloat16),
            pltpu.SemaphoreType.DMA((4, KV_HEADS)),
        ],
        name="pack",
    )(queries, keys, values)


def unpack_body(row_ref, in_ref, *refs):
    *pieces, out_ref, norm_ref, sems = refs
    copies = [
        pltpu.make_async_copy(
            in_ref.at[:, h], out_ref.at[:, :, pl.ds(h * 256, 256)], sems.at[h]
        )
        for h in range(KV_HEADS)
    ]
    for copy in copies:
        copy.start()
    rows = lax.broadcasted_iota(jnp.int32, (8, 128), 0)
    for h in range(2):
        for n in range(2):
            at = 2 * h + n
            held = jnp.zeros((8, 128), jnp.float32)
            for d in range(8):
                held = jnp.where(rows == (row_ref[0] + 8 - d) % 8, pieces[d][at : at + 1], held)
            norm_ref[h, :, n * 128 : (n + 1) * 128] = held
    for copy in copies:
        copy.wait()


def unpack(row, parts, pieces):
    vmem = pl.BlockSpec(memory_space=pltpu.VMEM)
    return pl.pallas_call(
        unpack_body,
        in_specs=[pl.BlockSpec(memory_space=pltpu.SMEM)] + [vmem] * 9,
        out_specs=[pl.BlockSpec(memory_space=pl.ANY), vmem],
        out_shape=[
            jax.ShapeDtypeStruct((ROWS, 16, 4096), jnp.bfloat16),
            jax.ShapeDtypeStruct((2, ROWS, 256), jnp.float32),
        ],
        scratch_shapes=[pltpu.SemaphoreType.DMA((KV_HEADS,))],
        name="unpack",
    )(row, *in_vmem(parts, *pieces))


def partial_softmax(q, row, j_low, blocks, diagonal, ends_ref, keys_at, values_at, s_ref):
    both = jnp.concatenate((q[:, 0:128], q[:, 128:256]), axis=0)
    top = None
    for n in range(blocks):
        s = lax.dot_general(
            both,
            keys_at(j_low + n),
            (((1,), (1,)), ((), ())),
            preferred_element_type=jnp.float32,
        )
        seen = row < ends_ref[pl.ds(j_low + n, 1), :]
        if diagonal and n == blocks - 1:
            key = lax.broadcasted_iota(jnp.int32, (TQ, TK), 1) + (j_low + n) * TK
            seen = seen & (key <= row)
        halves = []
        for h in range(2):
            part = jnp.where(seen, s[h * TQ : (h + 1) * TQ], -1e30)
            s_ref[n, h * TQ : (h + 1) * TQ] = part
            halves.append(jnp.maximum(part[:, 0:128], part[:, 128:256]))
        here = jnp.concatenate(halves, axis=0)
        top = here if top is None else jnp.maximum(top, here)
    top = jnp.max(top, axis=1, keepdims=True)
    total = acc = None
    for n in range(blocks):
        w = jnp.exp2((s_ref[n] - top) * (SCALE * LOG2E))
        part = w[:, 0:128] + w[:, 128:256]
        o = jnp.dot(
            w.astype(jnp.bfloat16), values_at(j_low + n), preferred_element_type=jnp.float32
        )
        total = part if total is None else total + part
        acc = o if acc is None else acc + o
    return top, jnp.sum(total, axis=1, keepdims=True), acc


def out_copy(i, held_ref, out_ref, sems):
    return pltpu.make_async_copy(held_ref.at[i], out_ref.at[pl.ds(i * TQ, TQ)], sems.at[0, i])


def part_copy(i, src_ref, dst_ref, sems):
    return pltpu.make_async_copy(src_ref.at[i], dst_ref.at[i], sems.at[1, i])


def keep(held_ref, i, result):
    result = result.astype(jnp.bfloat16)
    held_ref[i, :, 0:128] = result[0:TQ]
    held_ref[i, :, 128:256] = result[TQ : 2 * TQ]


def norm_slot(i):
    return (i // 2) * 8 + i % 2


def keep_norm(norm_acc, i, norm):
    lanes = lax.broadcasted_iota(jnp.int32, (TQ, 128), 1)
    held = jnp.where(lanes == norm_slot(i), norm[0:TQ], norm_acc[...])
    norm_acc[...] = jnp.where(lanes == norm_slot(i) + 2, norm[TQ : 2 * TQ], held)


def local_body(
    low_ref, ends_ref, qkv_ref, out_ref, norm_ref, part_ref, held_ref, kept_ref, s_ref, sems
):
    norm_ref[...] = jnp.zeros((TQ, 128), jnp.float32)
    rows = lambda j: pl.ds(pl.multiple_of(j * TK - HALO, TK), TK)
    keys_at = lambda j: qkv_ref[rows(j), 256:384]
    values_at = lambda j: qkv_ref[rows(j), 384:512]

    def block(i, carry):
        first = pl.multiple_of(i * TQ, TQ)
        j_low = jnp.maximum(low_ref[i], HALO) // TK
        count = (HALO + first) // TK + 1 - j_low
        row = lax.broadcasted_iota(jnp.int32, (TQ, TK), 0) + (HALO + first)
        for blocks in range(1, MOST_BLOCKS + 1):

            @pl.when(count == blocks)
            def _():
                q = qkv_ref[pl.ds(first, TQ), 0:256]
                top, total, acc = partial_softmax(
                    q, row, j_low, blocks, True, ends_ref, keys_at, values_at, s_ref
                )
                result = acc / total
                kept_ref[i] = result
                keep(held_ref, i, result)
                keep_norm(norm_ref, i, top * SCALE + jnp.log(total))

        @pl.when(low_ref[i] >= HALO)
        def _():
            out_copy(i, held_ref, out_ref, sems).start()

        @pl.when(low_ref[i] < HALO)
        def _():
            part_copy(i, kept_ref, part_ref, sems).start()

        return carry

    lax.fori_loop(0, BLOCKS, block, 0)
    for i in range(BLOCKS):

        @pl.when(low_ref[i] >= HALO)
        def _():
            out_copy(i, held_ref, out_ref, sems).wait()

        if i < HALO_BLOCKS:

            @pl.when(low_ref[i] < HALO)
            def _():
                part_copy(i, kept_ref, part_ref, sems).wait()


def attend_local(low, ends, qkv):
    vmem = pl.BlockSpec(memory_space=pltpu.VMEM)
    any_space = pl.BlockSpec(memory_space=pl.ANY)
    return pl.pallas_call(
        local_body,
        in_specs=[pl.BlockSpec(memory_space=pltpu.SMEM), vmem, vmem],
        out_specs=[any_space, vmem, any_space],
        out_shape=[
            jax.ShapeDtypeStruct((SPAN, 256), jnp.bfloat16),
            jax.ShapeDtypeStruct((TQ, 128), jnp.float32),
            jax.ShapeDtypeStruct((HALO_BLOCKS, 2 * TQ, 128), jnp.float32),
        ],
        scratch_shapes=[
            pltpu.VMEM((BLOCKS, TQ, 256), jnp.bfloat16),
            pltpu.VMEM((BLOCKS, 2 * TQ, 128), jnp.float32),
            pltpu.VMEM((MOST_BLOCKS, 2 * TQ, TK), jnp.float32),
            pltpu.SemaphoreType.DMA((2, BLOCKS)),
        ],
        name="attend_local",
    )(low, ends, *in_vmem(qkv))


def halo_body(low_ref, ends_ref, qkv_ref, halo_ref, prev_ref, prev_norm, part_ref, *refs):
    out_ref, *norm_refs = refs[:9]
    held_ref, kept_ref, s_ref, norm_acc, norm_t, sems = refs[9:]
    for i in range(HALO_BLOCKS):

        @pl.when(low_ref[i] < HALO)
        def _():
            part_copy(i, part_ref, kept_ref, sems).start()

    norm_acc[...] = prev_norm[...]
    rows = lambda j: pl.ds(pl.multiple_of(j * TK, TK), TK)
    keys_at = lambda j: halo_ref[rows(j), 0:128]
    values_at = lambda j: halo_ref[rows(j), 128:256]

    def block(i, carry):
        first = pl.multiple_of(i * TQ, TQ)
        j_low = low_ref[i] // TK
        count = HALO // TK - j_low
        row = lax.broadcasted_iota(jnp.int32, (TQ, TK), 0) + (HALO + first)
        lanes = lax.broadcasted_iota(jnp.int32, (TQ, 128), 1)

        @pl.when(count > 0)
        def _():
            part_copy(i, part_ref, kept_ref, sems).wait()

        for blocks in range(1, HALO // TK + 1):

            @pl.when(count == blocks)
            def _():
                q = qkv_ref[pl.ds(first, TQ), 0:256]
                top, total, acc = partial_softmax(
                    q, row, j_low, blocks, False, ends_ref, keys_at, values_at, s_ref
                )
                own = jnp.concatenate(
                    [
                        jnp.sum(
                            jnp.where(lanes == norm_slot(i) + at, norm_acc[...], 0.0),
                            axis=1,
                            keepdims=True,
                        )
                        for at in (0, 2)
                    ],
                    axis=0,
                )
                top = top * SCALE
                most = jnp.maximum(own, top)
                own = jnp.exp(own - most)
                here = jnp.exp(top - most)
                total = own + total * here
                keep(held_ref, i, (kept_ref[i] * own + acc * here) / total)
                keep_norm(norm_acc, i, most + jnp.log(total))
                out_copy(i, held_ref, out_ref, sems).start()

        return carry

    lax.fori_loop(0, HALO_BLOCKS, block, 0)
    norm_t[...] = jnp.transpose(norm_acc[...])
    for d in range(8):
        norm_refs[d][...] = norm_t[pl.ds(pl.multiple_of(((low_ref[BLOCKS] + d) % 8) * 8, 8), 8)]
    for i in range(HALO_BLOCKS):

        @pl.when(low_ref[i] < HALO)
        def _():
            out_copy(i, held_ref, out_ref, sems).wait()


def attend_halo(low, ends, qkv, halo, out, norm, part):
    vmem = pl.BlockSpec(memory_space=pltpu.VMEM)
    any_space = pl.BlockSpec(memory_space=pl.ANY)
    return pl.pallas_call(
        halo_body,
        in_specs=[
            pl.BlockSpec(memory_space=pltpu.SMEM),
            vmem,
            vmem,
            vmem,
            any_space,
            vmem,
            any_space,
        ],
        out_specs=[any_space] + [vmem] * 8,
        out_shape=[jax.ShapeDtypeStruct((SPAN, 256), jnp.bfloat16)]
        + [pltpu.VMEM((8, 128), jnp.float32)] * 8,
        scratch_shapes=[
            pltpu.VMEM((HALO_BLOCKS, TQ, 256), jnp.bfloat16),
            pltpu.VMEM((HALO_BLOCKS, 2 * TQ, 128), jnp.float32),
            pltpu.VMEM((HALO // TK, 2 * TQ, TK), jnp.float32),
            pltpu.VMEM((TQ, 128), jnp.float32),
            pltpu.VMEM((TQ, 128), jnp.float32),
            pltpu.SemaphoreType.DMA((2, HALO_BLOCKS)),
        ],
        input_output_aliases={4: 0},
        name="attend_halo",
    )(low, ends, *in_vmem(qkv, halo), out, norm, part)


def per_device(queries, keys, values, lengths):
    row = lax.axis_index("z")
    base = lax.axis_index("x") * SPAN
    packed = pack(queries, keys, values).reshape(128, 16, 512)
    moved = lax.all_to_all(packed, PLANE, 0, 0, tiled=True)
    low, ends = bounds(lengths, row[None], base[None])
    qkv = moved.reshape(SPAN, 512)
    halo = lax.ppermute(qkv[SPAN - HALO :, 256:512], "x", [(i, i + 1) for i in range(3)])
    out, norm, part = attend_local(low, ends, qkv)
    out, *pieces = attend_halo(low, ends, qkv, halo, out, norm, part)
    back = lax.all_to_all(out.reshape(128, 16, 256), PLANE, 0, 0, tiled=True)
    for d in range(1, 8):
        pieces[d] = lax.ppermute(pieces[d], "z", [(i, (i + d) % 8) for i in range(8)])
    attended, log_norm = unpack(row[None], back.reshape(ROWS, KV_HEADS, 16, 256), pieces)
    return attended, log_norm


def solution(mesh):
    split = Mesh(mesh.devices.reshape(4, 8, 8, 2), ALL)
    wide = P(None, ALL, None)
    return jax.shard_map(
        per_device,
        mesh=split,
        in_specs=(wide, wide, wide, P()),
        out_specs=(wide, P(("y", "c"), None, ("x", "z"))),
        check_vma=False,
    )
```

time: 140 us -> 143 us (1.021)
  starting transfers between devices: 43.3 us -> 46.1 us
    all_to_all x1, starting transfers between devices: 10.3 us -> 13.1 us  [per_device(): back = lax.all_to_all(out.reshape(128, 16, 256), PLANE, 0, 0, tiled=True)]
    unnamed x20 -> x4, local copies, waits for them, and re-layouts: 3.48 us -> 2.92 us
  transfers between devices with their start and end apart: 9 -> 9, of which waited for: 1 -> 1; matrix products, arithmetic and copies ran while one was open for 0% -> 0% of each run, Pallas kernels for 9% -> 8%
where the time goes in v5:
time: 143 us; the launch traced here: 142 us
  blocking collectives  70.4 us (49%)
  starting transfers between devices  46.1 us (32%)
  Pallas kernels  19.9 us (14%)
  local copies, waits for them, and re-layouts  2.95 us (2%)
  waiting for transfers between devices  2.21 us (2%)
    all_to_all x1, blocking collectives, per_device(): moved = lax.all_to_all(packed, PLANE, 0, 0, tiled=True)  70.4 us
    ppermute x7, starting transfers between devices, per_device(): lax.ppermute(pieces[d], 'z', [(i, (i + d) % 8) for i in range(8)])  29.9 us
    all_to_all x1, starting transfers between devices, per_device(): back = lax.all_to_all(out.reshape(128, 16, 256), PLANE, 0, 0, tiled=True)  13.1 us
    pallas_call x1, Pallas kernels, attend_local(): pl.pallas_call(local_body, in_specs=[pl.BlockSpec(memory_space=pltpu.SMEM...  10 us
    pallas_call x1, Pallas kernels, attend_halo(): pl.pallas_call(halo_body, in_specs=[pl.BlockSpec(memory_space=pltpu.SMEM)...  3.43 us
    ppermute x1, starting transfers between devices, per_device(): lax.ppermute(qkv[SPAN - HALO:, 256:512], 'x', [(i, i + 1) for i in range(...  3.09 us
    pallas_call x1, Pallas kernels, pack(): pl.pallas_call(pack_body, in_specs=[pl.BlockSpec(memory_space=pl.ANY)] *...  2.94 us
    unnamed x4, local copies, waits for them, and re-layouts  2.92 us
  transfers between devices with their start and end apart: 9, of which 1 were waited for; matrix products, arithmetic and copies ran while one was open for 0% of the time, Pallas kernels for 8%

profile of v5, /device:TPU:4, one launch (start us, length us, event | category | flops | bytes accessed | tf_op | source)
XLA Modules:
  0.0 142.3 jit_solution(11283557964319919173)
XLA Ops:
  0.6 2.9 %pack.1 = bf16[8,16,16,512]{3,2,1,0:T(8,128)(2,1)} custom-call(bf16[8,16,4096]{2,1,0:T(8,128)(2,1)} %q_ref.1, bf16[8,16,2048]{2,1,0:T(8,128)(2,1)} %k_ref.1, bf16[8,16,2048]{2,1,0:T(8,128)(2,1)} %v_ref.1), custom_call_target="tpu_custom_call" | custom-call | tf_op jit(solution)/shard_map/pack/pallas_call | solution.py:94
  3.6 70.4 %all_to_all.10 = bf16[128,16,512]{2,1,0:T(8,128)(2,1)S(1)} all-to-all(bf16[128,16,512]{2,1,0:T(8,128)(2,1)} %bitcast.10), channel_id=1, replica_groups=mesh['x'=4,'z'=8,'y'=8,'c'=2] {'z','y','c'}, dimensions={0} | all-to-all | bytes 4194304 | tf_op jit(solution)/shard_map/all_to_all | solution.py:374
  74.0 1.3 copy-done
  75.3 3.1 %collective-permute-start = (bf16[1024,256]{1,0:T(8,128)(2,1)S(1)}, bf16[1024,256]{1,0:T(8,128)(2,1)S(1)}, u32[]{:S(2)}, u32[]{:S(2)}) collective-permute-start(bf16[1024,256]{1,0:T(8,128)(2,1)S(1)} %slice.4), channel_id=1, source_target_pairs={{0,128},{128,256},{256,384},{1,129},{129,257},{257,385},{2,130},{1... | collective-permute-start | bytes 1572872 | tf_op jit(solution)/shard_map/ppermute | solution.py:377
  78.4 1.8 %doc_bounds.1 = (s32[17]{0:T(128)}, s32[12,256]{1,0:T(8,128)}) custom-call(s32[8,32]{1,0:T(8,128)} %lengths_ref.1, s32[1]{0:T(128)} %bitcast.row_ref, s32[1]{0:T(128)} %bitcast.1.base_ref), custom_call_target="tpu_custom_call" | custom-call | tf_op jit(solution)/shard_map/doc_bounds/pallas_call | solution.py:53
  80.2 1.6 %copy-done.1 = bf16[128,16,512]{2,1,0:T(8,128)(2,1)S(1)} copy-done((bf16[128,16,512]{2,1,0:T(8,128)(2,1)S(1)}, bf16[128,16,512]{2,1,0:T(8,128)(2,1)}, u32[]{:S(2)}) %copy-start.1) | copy-done | bytes 2097176
  81.8 10.0 %attend_local.1 = (bf16[2048,256]{1,0:T(8,128)(2,1)}, f32[128,128]{1,0:T(8,128)}, f32[8,256,128]{2,1,0:T(8,128)}) custom-call(s32[17]{0:T(128)} %get-tuple-element.16.low_ref, s32[12,256]{1,0:T(8,128)} %get-tuple-element.17.ends_ref, bf16[2048,512]{1,0:T(8,128)(2,1)S(1)} %bitcast.7), custom_call_target="tpu_custom_call" | custom-call | tf_op jit(solution)/shard_map/attend_local/pallas_call | solution.py:255
  91.8 0.0 collective-permute-done.halo_ref
  91.8 3.4 %attend_halo.1 = (bf16[2048,256]{1,0:T(8,128)(2,1)}, f32[8,128]{1,0:T(8,128)S(1)}, f32[8,128]{1,0:T(8,128)S(1)}, f32[8,128]{1,0:T(8,128)S(1)}, f32[8,128]{1,0:T(...) custom-call(s32[17]{0:T(128)} %get-tuple-element.16.low_ref, ...), custom_call_target="tpu_custom_call", output_to_operand_aliasing={{0}: (4, {})} | custom-call | tf_op jit(solution)/shard_map/attend_halo/pallas_call | solution.py:343
  95.3 13.1 %all-to-all-start.1 = ((bf16[128,16,256]{2,1,0:T(8,128)(2,1)}), bf16[128,16,256]{2,1,0:T(8,128)(2,1)S(1)}, u32[]{:S(2)}, u32[]{:S(2)}) async-start(bf16[128,16,256]{2,1,0:T(8,128)(2,1)} %bitcast.11), calls=%async_computation.1 | async-start | bytes 2097152 | tf_op jit(solution)/shard_map/all_to_all | solution.py:380
  108.4 3.0 %collective-permute-start.1 = (f32[8,128]{1,0:T(8,128)S(1)}, f32[8,128]{1,0:T(8,128)S(1)}, u32[]{:S(2)}, u32[]{:S(2)}) collective-permute-start(f32[8,128]{1,0:T(8,128)S(1)} %get-tuple-element.23), channel_id=1, source_target_pairs={{0,16},{16,32},{32,48},{48,64},{64,80},{80,96},{96,112},{112,0},{1... | collective-permute-start | bytes 12296 | tf_op jit(solution)/shard_map/ppermute | solution.py:382
  111.5 4.5 %collective-permute-start.2 = (f32[8,128]{1,0:T(8,128)S(1)}, f32[8,128]{1,0:T(8,128)S(1)}, u32[]{:S(2)}, u32[]{:S(2)}) collective-permute-start(f32[8,128]{1,0:T(8,128)S(1)} %get-tuple-element.24), channel_id=1, source_target_pairs={{0,32},{16,48},{32,64},{48,80},{64,96},{80,112},{96,0},{112,16},{1... | collective-permute-start | bytes 12296 | tf_op jit(solution)/shard_map/ppermute | solution.py:382
  115.9 4.9 %collective-permute-start.3 = (f32[8,128]{1,0:T(8,128)S(1)}, f32[8,128]{1,0:T(8,128)S(1)}, u32[]{:S(2)}, u32[]{:S(2)}) collective-permute-start(f32[8,128]{1,0:T(8,128)S(1)} %get-tuple-element.25), channel_id=1, source_target_pairs={{0,48},{16,64},{32,80},{48,96},{64,112},{80,0},{96,16},{112,32},{1... | collective-permute-start | bytes 12296 | tf_op jit(solution)/shard_map/ppermute | solution.py:382
  120.9 3.8 %collective-permute-start.4 = (f32[8,128]{1,0:T(8,128)S(1)}, f32[8,128]{1,0:T(8,128)S(1)}, u32[]{:S(2)}, u32[]{:S(2)}) collective-permute-start(f32[8,128]{1,0:T(8,128)S(1)} %get-tuple-element.26), channel_id=1, source_target_pairs={{0,64},{16,80},{32,96},{48,112},{64,0},{80,16},{96,32},{112,48},{1... | collective-permute-start | bytes 12296 | tf_op jit(solution)/shard_map/ppermute | solution.py:382
  124.7 5.1 %collective-permute-start.5 = (f32[8,128]{1,0:T(8,128)S(1)}, f32[8,128]{1,0:T(8,128)S(1)}, u32[]{:S(2)}, u32[]{:S(2)}) collective-permute-start(f32[8,128]{1,0:T(8,128)S(1)} %get-tuple-element.27), channel_id=1, source_target_pairs={{0,80},{16,96},{32,112},{48,0},{64,16},{80,32},{96,48},{112,64},{1... | collective-permute-start | bytes 12296 | tf_op jit(solution)/shard_map/ppermute | solution.py:382
  129.8 0.0 collective-permute-done.1.refs_1_
  129.8 5.3 %collective-permute-start.6 = (f32[8,128]{1,0:T(8,128)S(1)}, f32[8,128]{1,0:T(8,128)S(1)}, u32[]{:S(2)}, u32[]{:S(2)}) collective-permute-start(f32[8,128]{1,0:T(8,128)S(1)} %get-tuple-element.28), channel_id=1, source_target_pairs={{0,96},{16,112},{32,0},{48,16},{64,32},{80,48},{96,64},{112,80},{1... | collective-permute-start | bytes 12296 | tf_op jit(solution)/shard_map/ppermute | solution.py:382
  135.1 0.0 collective-permute-done.2.refs_2_
  135.1 3.3 %collective-permute-start.7 = (f32[8,128]{1,0:T(8,128)S(1)}, f32[8,128]{1,0:T(8,128)S(1)}, u32[]{:S(2)}, u32[]{:S(2)}) collective-permute-start(f32[8,128]{1,0:T(8,128)S(1)} %get-tuple-element.29), channel_id=1, source_target_pairs={{0,112},{16,0},{32,16},{48,32},{64,48},{80,64},{96,80},{112,96},{1... | collective-permute-start | bytes 12296 | tf_op jit(solution)/shard_map/ppermute | solution.py:382
  138.4 0.0 collective-permute-done.3.refs_3_
  138.4 0.0 collective-permute-done.4.refs_4_
  138.4 0.0 collective-permute-done.6.refs_6_
  138.4 2.2 %collective-permute-done.7.refs_7_ = f32[8,128]{1,0:T(8,128)S(1)} collective-permute-done((f32[8,128]{1,0:T(8,128)S(1)}, f32[8,128]{1,0:T(8,128)S(1)}, u32[]{:S(2)}, u32[]{:S(2)}) %collective-permute-start.7) | collective-permute-done | bytes 4128 | tf_op jit(solution)/shard_map/ppermute | solution.py:382
  140.6 1.7 %unpack.1 = (bf16[8,16,4096]{2,1,0:T(8,128)(2,1)}, f32[2,8,256]{2,1,0:T(8,128)}) custom-call(s32[1]{0:T(128)} %bitcast.row_ref, bf16[8,16,16,256]{3,2,1,0:T(8,128)(2,1)S(1)} %bitcast.9, f32[8,128]{1,0:T(8,128)S(1)} %get-tuple-element.22.refs_0_, f32[8,128]{1,0:T(8,128)S(1)} %collective-permute-done.1.refs_1_, f32[8,128]{1,0:T(8,128)S(1)} %collective-permute-done.2.refs_2_, ...), custom_call_target="tpu_custom_call" | custom-call | tf_op jit(solution)/shard_map/unpack/pallas_call | solution.py:131
  (5 shorter events, 0.0 us)
Async XLA Ops:
  74.0 1.3 copy-start
  75.3 16.5 %collective-permute-start = (bf16[1024,256]{1,0:T(8,128)(2,1)S(1)}, bf16[1024,256]{1,0:T(8,128)(2,1)S(1)}, u32[]{:S(2)}, u32[]{:S(2)}) collective-permute-start(bf16[1024,256]{1,0:T(8,128)(2,1)S(1)} %slice.4), channel_id=1, source_target_pairs={{0,128},{128,256},{256,384},{1,129},{129,257},{257,385},{2,130},{1... | collective-permute-start | bytes 1572872 | tf_op jit(solution)/shard_map/ppermute | solution.py:377
  80.2 1.6 %copy-start.1 = (bf16[128,16,512]{2,1,0:T(8,128)(2,1)S(1)}, bf16[128,16,512]{2,1,0:T(8,128)(2,1)}, u32[]{:S(2)}) copy-start(bf16[128,16,512]{2,1,0:T(8,128)(2,1)} %copy-done) | copy-start | bytes 6291460
  95.3 45.3 %all-to-all-start.1 = ((bf16[128,16,256]{2,1,0:T(8,128)(2,1)}), bf16[128,16,256]{2,1,0:T(8,128)(2,1)S(1)}, u32[]{:S(2)}, u32[]{:S(2)}) async-start(bf16[128,16,256]{2,1,0:T(8,128)(2,1)} %bitcast.11), calls=%async_computation.1 | async-start | bytes 2097152 | tf_op jit(solution)/shard_map/all_to_all | solution.py:380
  108.4 21.4 %collective-permute-start.1 = (f32[8,128]{1,0:T(8,128)S(1)}, f32[8,128]{1,0:T(8,128)S(1)}, u32[]{:S(2)}, u32[]{:S(2)}) collective-permute-start(f32[8,128]{1,0:T(8,128)S(1)} %get-tuple-element.23), channel_id=1, source_target_pairs={{0,16},{16,32},{32,48},{48,64},{64,80},{80,96},{96,112},{112,0},{1... | collective-permute-start | bytes 12296 | tf_op jit(solution)/shard_map/ppermute | solution.py:382
  111.5 23.7 %collective-permute-start.2 = (f32[8,128]{1,0:T(8,128)S(1)}, f32[8,128]{1,0:T(8,128)S(1)}, u32[]{:S(2)}, u32[]{:S(2)}) collective-permute-start(f32[8,128]{1,0:T(8,128)S(1)} %get-tuple-element.24), channel_id=1, source_target_pairs={{0,32},{16,48},{32,64},{48,80},{64,96},{80,112},{96,0},{112,16},{1... | collective-permute-start | bytes 12296 | tf_op jit(solution)/shard_map/ppermute | solution.py:382
  115.9 22.5 %collective-permute-start.3 = (f32[8,128]{1,0:T(8,128)S(1)}, f32[8,128]{1,0:T(8,128)S(1)}, u32[]{:S(2)}, u32[]{:S(2)}) collective-permute-start(f32[8,128]{1,0:T(8,128)S(1)} %get-tuple-element.25), channel_id=1, source_target_pairs={{0,48},{16,64},{32,80},{48,96},{64,112},{80,0},{96,16},{112,32},{1... | collective-permute-start | bytes 12296 | tf_op jit(solution)/shard_map/ppermute | solution.py:382
  120.9 17.5 %collective-permute-start.4 = (f32[8,128]{1,0:T(8,128)S(1)}, f32[8,128]{1,0:T(8,128)S(1)}, u32[]{:S(2)}, u32[]{:S(2)}) collective-permute-start(f32[8,128]{1,0:T(8,128)S(1)} %get-tuple-element.26), channel_id=1, source_target_pairs={{0,64},{16,80},{32,96},{48,112},{64,0},{80,16},{96,32},{112,48},{1... | collective-permute-start | bytes 12296 | tf_op jit(solution)/shard_map/ppermute | solution.py:382
  124.7 13.7 %collective-permute-start.5 = (f32[8,128]{1,0:T(8,128)S(1)}, f32[8,128]{1,0:T(8,128)S(1)}, u32[]{:S(2)}, u32[]{:S(2)}) collective-permute-start(f32[8,128]{1,0:T(8,128)S(1)} %get-tuple-element.27), channel_id=1, source_target_pairs={{0,80},{16,96},{32,112},{48,0},{64,16},{80,32},{96,48},{112,64},{1... | collective-permute-start | bytes 12296 | tf_op jit(solution)/shard_map/ppermute | solution.py:382
  129.8 8.6 %collective-permute-start.6 = (f32[8,128]{1,0:T(8,128)S(1)}, f32[8,128]{1,0:T(8,128)S(1)}, u32[]{:S(2)}, u32[]{:S(2)}) collective-permute-start(f32[8,128]{1,0:T(8,128)S(1)} %get-tuple-element.28), channel_id=1, source_target_pairs={{0,96},{16,112},{32,0},{48,16},{64,32},{80,48},{96,64},{112,80},{1... | collective-permute-start | bytes 12296 | tf_op jit(solution)/shard_map/ppermute | solution.py:382
  135.1 5.5 %collective-permute-start.7 = (f32[8,128]{1,0:T(8,128)S(1)}, f32[8,128]{1,0:T(8,128)S(1)}, u32[]{:S(2)}, u32[]{:S(2)}) collective-permute-start(f32[8,128]{1,0:T(8,128)S(1)} %get-tuple-element.29), channel_id=1, source_target_pairs={{0,112},{16,0},{32,16},{48,32},{64,48},{80,64},{96,80},{112,96},{1... | collective-permute-start | bytes 12296 | tf_op jit(solution)/shard_map/ppermute | solution.py:382

commit v6 on v5

--- a/solution.py
+++ b/solution.py
@@ -11,7 +11,7 @@
 KV_HEADS = 16
 HALO = 1024
 SPAN = 2048
-TQ = 128
+TQ = 256
 TK = 256
 MOST_BLOCKS = 5
 BLOCKS = SPAN // TQ
@@ -189,20 +189,34 @@
     held_ref[i, :, 128:256] = result[TQ : 2 * TQ]
 
 
-def norm_slot(i):
-    return (i // 2) * 8 + i % 2
+def norm_lanes(i):
+    return [(8 * i + n, slice(n * 128, (n + 1) * 128)) for n in range(4)]
 
 
 def keep_norm(norm_acc, i, norm):
-    lanes = lax.broadcasted_iota(jnp.int32, (TQ, 128), 1)
-    held = jnp.where(lanes == norm_slot(i), norm[0:TQ], norm_acc[...])
-    norm_acc[...] = jnp.where(lanes == norm_slot(i) + 2, norm[TQ : 2 * TQ], held)
+    lanes = lax.broadcasted_iota(jnp.int32, (128, 128), 1)
+    held = norm_acc[...]
+    for lane, rows in norm_lanes(i):
+        held = jnp.where(lanes == lane, norm[rows], held)
+    norm_acc[...] = held
+
+
+def kept_norm(norm_acc, i):
+    lanes = lax.broadcasted_iota(jnp.int32, (128, 128), 1)
+    held = norm_acc[...]
+    return jnp.concatenate(
+        [
+            jnp.sum(jnp.where(lanes == lane, held, 0.0), axis=1, keepdims=True)
+            for lane, _ in norm_lanes(i)
+        ],
+        axis=0,
+    )
 
 
 def local_body(
     low_ref, ends_ref, qkv_ref, out_ref, norm_ref, part_ref, held_ref, kept_ref, s_ref, sems
 ):
-    norm_ref[...] = jnp.zeros((TQ, 128), jnp.float32)
+    norm_ref[...] = jnp.zeros((128, 128), jnp.float32)
     rows = lambda j: pl.ds(pl.multiple_of(j * TK - HALO, TK), TK)
     keys_at = lambda j: qkv_ref[rows(j), 256:384]
     values_at = lambda j: qkv_ref[rows(j), 384:512]
@@ -258,7 +272,7 @@
         out_specs=[any_space, vmem, any_space],
         out_shape=[
             jax.ShapeDtypeStruct((SPAN, 256), jnp.bfloat16),
-            jax.ShapeDtypeStruct((TQ, 128), jnp.float32),
+            jax.ShapeDtypeStruct((128, 128), jnp.float32),
             jax.ShapeDtypeStruct((HALO_BLOCKS, 2 * TQ, 128), jnp.float32),
         ],
         scratch_shapes=[
@@ -290,11 +304,6 @@
         j_low = low_ref[i] // TK
         count = HALO // TK - j_low
         row = lax.broadcasted_iota(jnp.int32, (TQ, TK), 0) + (HALO + first)
-        lanes = lax.broadcasted_iota(jnp.int32, (TQ, 128), 1)
-
-        @pl.when(count > 0)
-        def _():
-            part_copy(i, part_ref, kept_ref, sems).wait()
 
         for blocks in range(1, HALO // TK + 1):
 
@@ -304,17 +313,8 @@
                 top, total, acc = partial_softmax(
                     q, row, j_low, blocks, False, ends_ref, keys_at, values_at, s_ref
                 )
-                own = jnp.concatenate(
-                    [
-                        jnp.sum(
-                            jnp.where(lanes == norm_slot(i) + at, norm_acc[...], 0.0),
-                            axis=1,
-                            keepdims=True,
-                        )
-                        for at in (0, 2)
-                    ],
-                    axis=0,
-                )
+                own = kept_norm(norm_acc, i)
+                part_copy(i, part_ref, kept_ref, sems).wait()
                 top = top * SCALE
                 most = jnp.maximum(own, top)
                 own = jnp.exp(own - most)
@@ -358,8 +358,8 @@
             pltpu.VMEM((HALO_BLOCKS, TQ, 256), jnp.bfloat16),
             pltpu.VMEM((HALO_BLOCKS, 2 * TQ, 128), jnp.float32),
             pltpu.VMEM((HALO // TK, 2 * TQ, TK), jnp.float32),
-            pltpu.VMEM((TQ, 128), jnp.float32),
-            pltpu.VMEM((TQ, 128), jnp.float32),
+            pltpu.VMEM((128, 128), jnp.float32),
+            pltpu.VMEM((128, 128), jnp.float32),
             pltpu.SemaphoreType.DMA((2, HALO_BLOCKS)),
         ],
         input_output_aliases={4: 0},

time: 143 us -> 139 us (0.972)
  Pallas kernels: 19.9 us -> 17.5 us
  starting transfers between devices: 46.1 us -> 44.4 us
    all_to_all x1, starting transfers between devices: 13.1 us -> 11.2 us  [per_device(): back = lax.all_to_all(out.reshape(128, 16, 256), PLANE, 0, 0, tiled=True)]
    pallas_call x1, Pallas kernels: 10 us -> 8.42 us  [attend_local(): pl.pallas_call(local_body, in_specs=[pl.BlockSpec(memory_space=pltpu.SMEM...]
  transfers between devices with their start and end apart: 9 -> 9, of which waited for: 1 -> 1; matrix products, arithmetic and copies ran while one was open for 0% -> 0% of each run, Pallas kernels for 8% -> 7%
where the time goes in v6:
time: 139 us; the launch traced here: 138 us
  blocking collectives  70.4 us (51%)
  starting transfers between devices  44.4 us (32%)
  Pallas kernels  17.5 us (13%)
  local copies, waits for them, and re-layouts  2.95 us (2%)
  waiting for transfers between devices  2.21 us (2%)
    all_to_all x1, blocking collectives, per_device(): moved = lax.all_to_all(packed, PLANE, 0, 0, tiled=True)  70.4 us
    ppermute x7, starting transfers between devices, per_device(): lax.ppermute(pieces[d], 'z', [(i, (i + d) % 8) for i in range(8)])  29.9 us
    all_to_all x1, starting transfers between devices, per_device(): back = lax.all_to_all(out.reshape(128, 16, 256), PLANE, 0, 0, tiled=True)  11.2 us
    pallas_call x1, Pallas kernels, attend_local(): pl.pallas_call(local_body, in_specs=[pl.BlockSpec(memory_space=pltpu.SMEM...  8.42 us
    ppermute x1, starting transfers between devices, per_device(): lax.ppermute(qkv[SPAN - HALO:, 256:512], 'x', [(i, i + 1) for i in range(...  3.27 us
    pallas_call x1, Pallas kernels, pack(): pl.pallas_call(pack_body, in_specs=[pl.BlockSpec(memory_space=pl.ANY)] *...  2.94 us
    unnamed x4, local copies, waits for them, and re-layouts  2.92 us
    pallas_call x1, Pallas kernels, attend_halo(): pl.pallas_call(halo_body, in_specs=[pl.BlockSpec(memory_space=pltpu.SMEM)...  2.83 us
  transfers between devices with their start and end apart: 9, of which 1 were waited for; matrix products, arithmetic and copies ran while one was open for 0% of the time, Pallas kernels for 7%

profile of v6, /device:TPU:4, one launch (start us, length us, event | category | flops | bytes accessed | tf_op | source)
XLA Modules:
  0.0 138.4 jit_solution(11780339525538550925)
XLA Ops:
  0.6 2.9 %pack.1 = bf16[8,16,16,512]{3,2,1,0:T(8,128)(2,1)} custom-call(bf16[8,16,4096]{2,1,0:T(8,128)(2,1)} %q_ref.1, bf16[8,16,2048]{2,1,0:T(8,128)(2,1)} %k_ref.1, bf16[8,16,2048]{2,1,0:T(8,128)(2,1)} %v_ref.1), custom_call_target="tpu_custom_call" | custom-call | tf_op jit(solution)/shard_map/pack/pallas_call | solution.py:94
  3.6 70.4 %all_to_all.10 = bf16[128,16,512]{2,1,0:T(8,128)(2,1)S(1)} all-to-all(bf16[128,16,512]{2,1,0:T(8,128)(2,1)} %bitcast.10), channel_id=1, replica_groups=mesh['x'=4,'z'=8,'y'=8,'c'=2] {'z','y','c'}, dimensions={0} | all-to-all | bytes 4194304 | tf_op jit(solution)/shard_map/all_to_all | solution.py:374
  74.0 1.3 copy-done
  75.3 3.3 %collective-permute-start = (bf16[1024,256]{1,0:T(8,128)(2,1)S(1)}, bf16[1024,256]{1,0:T(8,128)(2,1)S(1)}, u32[]{:S(2)}, u32[]{:S(2)}) collective-permute-start(bf16[1024,256]{1,0:T(8,128)(2,1)S(1)} %slice.4), channel_id=1, source_target_pairs={{0,128},{128,256},{256,384},{1,129},{129,257},{257,385},{2,130},{1... | collective-permute-start | bytes 1572872 | tf_op jit(solution)/shard_map/ppermute | solution.py:377
  78.6 1.6 %doc_bounds.1 = (s32[9]{0:T(128)}, s32[12,256]{1,0:T(8,128)}) custom-call(s32[8,32]{1,0:T(8,128)} %lengths_ref.1, s32[1]{0:T(128)} %bitcast.row_ref, s32[1]{0:T(128)} %bitcast.1.base_ref), custom_call_target="tpu_custom_call" | custom-call | tf_op jit(solution)/shard_map/doc_bounds/pallas_call | solution.py:53
  80.2 1.6 %copy-done.1 = bf16[128,16,512]{2,1,0:T(8,128)(2,1)S(1)} copy-done((bf16[128,16,512]{2,1,0:T(8,128)(2,1)S(1)}, bf16[128,16,512]{2,1,0:T(8,128)(2,1)}, u32[]{:S(2)}) %copy-start.1) | copy-done | bytes 2097176
  81.8 8.4 %attend_local.1 = (bf16[2048,256]{1,0:T(8,128)(2,1)}, f32[128,128]{1,0:T(8,128)}, f32[4,512,128]{2,1,0:T(8,128)}) custom-call(s32[9]{0:T(128)} %get-tuple-element.16.low_ref, s32[12,256]{1,0:T(8,128)} %get-tuple-element.17.ends_ref, bf16[2048,512]{1,0:T(8,128)(2,1)S(1)} %bitcast.7), custom_call_target="tpu_custom_call" | custom-call | tf_op jit(solution)/shard_map/attend_local/pallas_call | solution.py:269
  90.2 0.0 collective-permute-done.halo_ref
  90.2 2.8 %attend_halo.1 = (bf16[2048,256]{1,0:T(8,128)(2,1)}, f32[8,128]{1,0:T(8,128)S(1)}, f32[8,128]{1,0:T(8,128)S(1)}, f32[8,128]{1,0:T(8,128)S(1)}, f32[8,128]{1,0:T(...) custom-call(s32[9]{0:T(128)} %get-tuple-element.16.low_ref, ...), custom_call_target="tpu_custom_call", output_to_operand_aliasing={{0}: (4, {})} | custom-call | tf_op jit(solution)/shard_map/attend_halo/pallas_call | solution.py:343
  93.1 11.2 %all-to-all-start.1 = ((bf16[128,16,256]{2,1,0:T(8,128)(2,1)}), bf16[128,16,256]{2,1,0:T(8,128)(2,1)S(1)}, u32[]{:S(2)}, u32[]{:S(2)}) async-start(bf16[128,16,256]{2,1,0:T(8,128)(2,1)} %bitcast.11), calls=%async_computation.1 | async-start | bytes 2097152 | tf_op jit(solution)/shard_map/all_to_all | solution.py:380
  104.3 3.0 %collective-permute-start.1 = (f32[8,128]{1,0:T(8,128)S(1)}, f32[8,128]{1,0:T(8,128)S(1)}, u32[]{:S(2)}, u32[]{:S(2)}) collective-permute-start(f32[8,128]{1,0:T(8,128)S(1)} %get-tuple-element.23), channel_id=1, source_target_pairs={{0,16},{16,32},{32,48},{48,64},{64,80},{80,96},{96,112},{112,0},{1... | collective-permute-start | bytes 12296 | tf_op jit(solution)/shard_map/ppermute | solution.py:382
  107.4 4.5 %collective-permute-start.2 = (f32[8,128]{1,0:T(8,128)S(1)}, f32[8,128]{1,0:T(8,128)S(1)}, u32[]{:S(2)}, u32[]{:S(2)}) collective-permute-start(f32[8,128]{1,0:T(8,128)S(1)} %get-tuple-element.24), channel_id=1, source_target_pairs={{0,32},{16,48},{32,64},{48,80},{64,96},{80,112},{96,0},{112,16},{1... | collective-permute-start | bytes 12296 | tf_op jit(solution)/shard_map/ppermute | solution.py:382
  111.8 4.9 %collective-permute-start.3 = (f32[8,128]{1,0:T(8,128)S(1)}, f32[8,128]{1,0:T(8,128)S(1)}, u32[]{:S(2)}, u32[]{:S(2)}) collective-permute-start(f32[8,128]{1,0:T(8,128)S(1)} %get-tuple-element.25), channel_id=1, source_target_pairs={{0,48},{16,64},{32,80},{48,96},{64,112},{80,0},{96,16},{112,32},{1... | collective-permute-start | bytes 12296 | tf_op jit(solution)/shard_map/ppermute | solution.py:382
  116.8 3.8 %collective-permute-start.4 = (f32[8,128]{1,0:T(8,128)S(1)}, f32[8,128]{1,0:T(8,128)S(1)}, u32[]{:S(2)}, u32[]{:S(2)}) collective-permute-start(f32[8,128]{1,0:T(8,128)S(1)} %get-tuple-element.26), channel_id=1, source_target_pairs={{0,64},{16,80},{32,96},{48,112},{64,0},{80,16},{96,32},{112,48},{1... | collective-permute-start | bytes 12296 | tf_op jit(solution)/shard_map/ppermute | solution.py:382
  120.6 5.1 %collective-permute-start.5 = (f32[8,128]{1,0:T(8,128)S(1)}, f32[8,128]{1,0:T(8,128)S(1)}, u32[]{:S(2)}, u32[]{:S(2)}) collective-permute-start(f32[8,128]{1,0:T(8,128)S(1)} %get-tuple-element.27), channel_id=1, source_target_pairs={{0,80},{16,96},{32,112},{48,0},{64,16},{80,32},{96,48},{112,64},{1... | collective-permute-start | bytes 12296 | tf_op jit(solution)/shard_map/ppermute | solution.py:382
  125.7 0.0 collective-permute-done.1.refs_1_
  125.7 5.3 %collective-permute-start.6 = (f32[8,128]{1,0:T(8,128)S(1)}, f32[8,128]{1,0:T(8,128)S(1)}, u32[]{:S(2)}, u32[]{:S(2)}) collective-permute-start(f32[8,128]{1,0:T(8,128)S(1)} %get-tuple-element.28), channel_id=1, source_target_pairs={{0,96},{16,112},{32,0},{48,16},{64,32},{80,48},{96,64},{112,80},{1... | collective-permute-start | bytes 12296 | tf_op jit(solution)/shard_map/ppermute | solution.py:382
  131.0 0.0 collective-permute-done.2.refs_2_
  131.0 3.3 %collective-permute-start.7 = (f32[8,128]{1,0:T(8,128)S(1)}, f32[8,128]{1,0:T(8,128)S(1)}, u32[]{:S(2)}, u32[]{:S(2)}) collective-permute-start(f32[8,128]{1,0:T(8,128)S(1)} %get-tuple-element.29), channel_id=1, source_target_pairs={{0,112},{16,0},{32,16},{48,32},{64,48},{80,64},{96,80},{112,96},{1... | collective-permute-start | bytes 12296 | tf_op jit(solution)/shard_map/ppermute | solution.py:382
  134.3 0.0 collective-permute-done.3.refs_3_
  134.3 0.0 collective-permute-done.4.refs_4_
  134.3 0.0 collective-permute-done.6.refs_6_
  134.3 2.2 %collective-permute-done.7.refs_7_ = f32[8,128]{1,0:T(8,128)S(1)} collective-permute-done((f32[8,128]{1,0:T(8,128)S(1)}, f32[8,128]{1,0:T(8,128)S(1)}, u32[]{:S(2)}, u32[]{:S(2)}) %collective-permute-start.7) | collective-permute-done | bytes 4128 | tf_op jit(solution)/shard_map/ppermute | solution.py:382
  136.5 1.7 %unpack.1 = (bf16[8,16,4096]{2,1,0:T(8,128)(2,1)}, f32[2,8,256]{2,1,0:T(8,128)}) custom-call(s32[1]{0:T(128)} %bitcast.row_ref, bf16[8,16,16,256]{3,2,1,0:T(8,128)(2,1)S(1)} %bitcast.9, f32[8,128]{1,0:T(8,128)S(1)} %get-tuple-element.22.refs_0_, f32[8,128]{1,0:T(8,128)S(1)} %collective-permute-done.1.refs_1_, f32[8,128]{1,0:T(8,128)S(1)} %collective-permute-done.2.refs_2_, ...), custom_call_target="tpu_custom_call" | custom-call | tf_op jit(solution)/shard_map/unpack/pallas_call | solution.py:131
  (5 shorter events, 0.0 us)
Async XLA Ops:
  74.0 1.3 copy-start
  75.3 14.9 %collective-permute-start = (bf16[1024,256]{1,0:T(8,128)(2,1)S(1)}, bf16[1024,256]{1,0:T(8,128)(2,1)S(1)}, u32[]{:S(2)}, u32[]{:S(2)}) collective-permute-start(bf16[1024,256]{1,0:T(8,128)(2,1)S(1)} %slice.4), channel_id=1, source_target_pairs={{0,128},{128,256},{256,384},{1,129},{129,257},{257,385},{2,130},{1... | collective-permute-start | bytes 1572872 | tf_op jit(solution)/shard_map/ppermute | solution.py:377
  80.2 1.6 %copy-start.1 = (bf16[128,16,512]{2,1,0:T(8,128)(2,1)S(1)}, bf16[128,16,512]{2,1,0:T(8,128)(2,1)}, u32[]{:S(2)}) copy-start(bf16[128,16,512]{2,1,0:T(8,128)(2,1)} %copy-done) | copy-start | bytes 6291460
  93.1 43.5 %all-to-all-start.1 = ((bf16[128,16,256]{2,1,0:T(8,128)(2,1)}), bf16[128,16,256]{2,1,0:T(8,128)(2,1)S(1)}, u32[]{:S(2)}, u32[]{:S(2)}) async-start(bf16[128,16,256]{2,1,0:T(8,128)(2,1)} %bitcast.11), calls=%async_computation.1 | async-start | bytes 2097152 | tf_op jit(solution)/shard_map/all_to_all | solution.py:380
  104.3 21.4 %collective-permute-start.1 = (f32[8,128]{1,0:T(8,128)S(1)}, f32[8,128]{1,0:T(8,128)S(1)}, u32[]{:S(2)}, u32[]{:S(2)}) collective-permute-start(f32[8,128]{1,0:T(8,128)S(1)} %get-tuple-element.23), channel_id=1, source_target_pairs={{0,16},{16,32},{32,48},{48,64},{64,80},{80,96},{96,112},{112,0},{1... | collective-permute-start | bytes 12296 | tf_op jit(solution)/shard_map/ppermute | solution.py:382
  107.4 23.7 %collective-permute-start.2 = (f32[8,128]{1,0:T(8,128)S(1)}, f32[8,128]{1,0:T(8,128)S(1)}, u32[]{:S(2)}, u32[]{:S(2)}) collective-permute-start(f32[8,128]{1,0:T(8,128)S(1)} %get-tuple-element.24), channel_id=1, source_target_pairs={{0,32},{16,48},{32,64},{48,80},{64,96},{80,112},{96,0},{112,16},{1... | collective-permute-start | bytes 12296 | tf_op jit(solution)/shard_map/ppermute | solution.py:382
  111.8 22.5 %collective-permute-start.3 = (f32[8,128]{1,0:T(8,128)S(1)}, f32[8,128]{1,0:T(8,128)S(1)}, u32[]{:S(2)}, u32[]{:S(2)}) collective-permute-start(f32[8,128]{1,0:T(8,128)S(1)} %get-tuple-element.25), channel_id=1, source_target_pairs={{0,48},{16,64},{32,80},{48,96},{64,112},{80,0},{96,16},{112,32},{1... | collective-permute-start | bytes 12296 | tf_op jit(solution)/shard_map/ppermute | solution.py:382
  116.8 17.5 %collective-permute-start.4 = (f32[8,128]{1,0:T(8,128)S(1)}, f32[8,128]{1,0:T(8,128)S(1)}, u32[]{:S(2)}, u32[]{:S(2)}) collective-permute-start(f32[8,128]{1,0:T(8,128)S(1)} %get-tuple-element.26), channel_id=1, source_target_pairs={{0,64},{16,80},{32,96},{48,112},{64,0},{80,16},{96,32},{112,48},{1... | collective-permute-start | bytes 12296 | tf_op jit(solution)/shard_map/ppermute | solution.py:382
  120.6 13.7 %collective-permute-start.5 = (f32[8,128]{1,0:T(8,128)S(1)}, f32[8,128]{1,0:T(8,128)S(1)}, u32[]{:S(2)}, u32[]{:S(2)}) collective-permute-start(f32[8,128]{1,0:T(8,128)S(1)} %get-tuple-element.27), channel_id=1, source_target_pairs={{0,80},{16,96},{32,112},{48,0},{64,16},{80,32},{96,48},{112,64},{1... | collective-permute-start | bytes 12296 | tf_op jit(solution)/shard_map/ppermute | solution.py:382
  125.7 8.6 %collective-permute-start.6 = (f32[8,128]{1,0:T(8,128)S(1)}, f32[8,128]{1,0:T(8,128)S(1)}, u32[]{:S(2)}, u32[]{:S(2)}) collective-permute-start(f32[8,128]{1,0:T(8,128)S(1)} %get-tuple-element.28), channel_id=1, source_target_pairs={{0,96},{16,112},{32,0},{48,16},{64,32},{80,48},{96,64},{112,80},{1... | collective-permute-start | bytes 12296 | tf_op jit(solution)/shard_map/ppermute | solution.py:382
  131.0 5.5 %collective-permute-start.7 = (f32[8,128]{1,0:T(8,128)S(1)}, f32[8,128]{1,0:T(8,128)S(1)}, u32[]{:S(2)}, u32[]{:S(2)}) collective-permute-start(f32[8,128]{1,0:T(8,128)S(1)} %get-tuple-element.29), channel_id=1, source_target_pairs={{0,112},{16,0},{32,16},{48,32},{64,48},{80,64},{96,80},{112,96},{1... | collective-permute-start | bytes 12296 | tf_op jit(solution)/shard_map/ppermute | solution.py:382

commit v7 on v6

--- a/solution.py
+++ b/solution.py
@@ -105,7 +105,7 @@
 
 
 def unpack_body(row_ref, in_ref, *refs):
-    *pieces, out_ref, norm_ref, sems = refs
+    *pieces, out_ref, norm_out, norm_ref, sems, norm_sem = refs
     copies = [
         pltpu.make_async_copy(
             in_ref.at[:, h], out_ref.at[:, :, pl.ds(h * 256, 256)], sems.at[h]
@@ -122,6 +122,9 @@
             for d in range(8):
                 held = jnp.where(rows == (row_ref[0] + 8 - d) % 8, pieces[d][at : at + 1], held)
             norm_ref[h, :, n * 128 : (n + 1) * 128] = held
+    norm_copy = pltpu.make_async_copy(norm_ref, norm_out, norm_sem)
+    norm_copy.start()
+    norm_copy.wait()
     for copy in copies:
         copy.wait()
 
@@ -131,48 +134,71 @@
     return pl.pallas_call(
         unpack_body,
         in_specs=[pl.BlockSpec(memory_space=pltpu.SMEM)] + [vmem] * 9,
-        out_specs=[pl.BlockSpec(memory_space=pl.ANY), vmem],
+        out_specs=[pl.BlockSpec(memory_space=pl.ANY)] * 2,
         out_shape=[
             jax.ShapeDtypeStruct((ROWS, 16, 4096), jnp.bfloat16),
             jax.ShapeDtypeStruct((2, ROWS, 256), jnp.float32),
         ],
-        scratch_shapes=[pltpu.SemaphoreType.DMA((KV_HEADS,))],
+        scratch_shapes=[
+            pltpu.VMEM((2, ROWS, 256), jnp.float32),
+            pltpu.SemaphoreType.DMA((KV_HEADS,)),
+            pltpu.SemaphoreType.DMA,
+        ],
         name="unpack",
     )(row, *in_vmem(parts, *pieces))
 
 
-def partial_softmax(q, row, j_low, blocks, diagonal, ends_ref, keys_at, values_at, s_ref):
-    both = jnp.concatenate((q[:, 0:128], q[:, 128:256]), axis=0)
-    top = None
-    for n in range(blocks):
-        s = lax.dot_general(
-            both,
-            keys_at(j_low + n),
-            (((1,), (1,)), ((), ())),
-            preferred_element_type=jnp.float32,
+def partial_softmax(parts, rows, j_low, blocks, diagonal, ends_ref, keys_at, values_at, s_ref):
+    tops, totals, accs = [], [], []
+    for p in range(len(parts)):
+        at, row, top = slice(p * TQ, (p + 1) * TQ), rows[p // 2], None
+        for n in range(blocks):
+            s = lax.dot_general(
+                parts[p],
+                keys_at(j_low + n),
+                (((1,), (1,)), ((), ())),
+                preferred_element_type=jnp.float32,
+            )
+            seen = row < ends_ref[pl.ds(j_low + n, 1), :]
+            if diagonal and n == blocks - 1:
+                key = lax.broadcasted_iota(jnp.int32, (TQ, TK), 1) + (j_low + n) * TK
+                seen = seen & (key <= row)
+            s = jnp.where(seen, s, -1e30)
+            s_ref[n, at] = s
+            here = jnp.maximum(s[:, 0:128], s[:, 128:256])
+            top = here if top is None else jnp.maximum(top, here)
+        tops.append(jnp.broadcast_to(jnp.max(top, axis=1, keepdims=True), top.shape))
+    for p in range(len(parts)):
+        at, total, acc = slice(p * TQ, (p + 1) * TQ), None, None
+        top = jnp.concatenate((tops[p], tops[p]), axis=1)
+        for n in range(blocks):
+            w = jnp.exp2((s_ref[n, at] - top) * (SCALE * LOG2E))
+            part = w[:, 0:128] + w[:, 128:256]
+            o = jnp.dot(
+                w.astype(jnp.bfloat16), values_at(j_low + n), preferred_element_type=jnp.float32
+            )
+            total = part if total is None else total + part
+            acc = o if acc is None else acc + o
+        lead = total.astype(jnp.bfloat16)
+        trail = (total - lead.astype(jnp.float32)).astype(jnp.bfloat16)
+        totals.append(
+            jnp.dot(
+                jnp.concatenate((lead, trail), axis=1),
+                jnp.ones((256, 128), jnp.bfloat16),
+                preferred_element_type=jnp.float32,
+            )
         )
-        seen = row < ends_ref[pl.ds(j_low + n, 1), :]
-        if diagonal and n == blocks - 1:
-            key = lax.broadcasted_iota(jnp.int32, (TQ, TK), 1) + (j_low + n) * TK
-            seen = seen & (key <= row)
-        halves = []
-        for h in range(2):
-            part = jnp.where(seen, s[h * TQ : (h + 1) * TQ], -1e30)
-            s_ref[n, h * TQ : (h + 1) * TQ] = part
-            halves.append(jnp.maximum(part[:, 0:128], part[:, 128:256]))
-        here = jnp.concatenate(halves, axis=0)
-        top = here if top is None else jnp.maximum(top, here)
-    top = jnp.max(top, axis=1, keepdims=True)
-    total = acc = None
-    for n in range(blocks):
-        w = jnp.exp2((s_ref[n] - top) * (SCALE * LOG2E))
-        part = w[:, 0:128] + w[:, 128:256]
-        o = jnp.dot(
-            w.astype(jnp.bfloat16), values_at(j_low + n), preferred_element_type=jnp.float32
-        )
-        total = part if total is None else total + part
-        acc = o if acc is None else acc + o
-    return top, jnp.sum(total, axis=1, keepdims=True), acc
+        accs.append(acc)
+    return tuple(jnp.concatenate(v, axis=0) for v in (tops, totals, accs))
+
+
+def head_parts(qkv_ref, i):
+    q = qkv_ref[pl.ds(pl.multiple_of(i * TQ, TQ), TQ), 0:256]
+    return [q[:, 0:128], q[:, 128:256]]
+
+
+def positions(i):
+    return lax.broadcasted_iota(jnp.int32, (TQ, TK), 0) + (HALO + i * TQ)
 
 
 def out_copy(i, held_ref, out_ref, sems):
@@ -199,18 +225,6 @@
     for lane, rows in norm_lanes(i):
         held = jnp.where(lanes == lane, norm[rows], held)
     norm_acc[...] = held
-
-
-def kept_norm(norm_acc, i):
-    lanes = lax.broadcasted_iota(jnp.int32, (128, 128), 1)
-    held = norm_acc[...]
-    return jnp.concatenate(
-        [
-            jnp.sum(jnp.where(lanes == lane, held, 0.0), axis=1, keepdims=True)
-            for lane, _ in norm_lanes(i)
-        ],
-        axis=0,
-    )
 
 
 def local_body(
@@ -225,25 +239,28 @@
         first = pl.multiple_of(i * TQ, TQ)
         j_low = jnp.maximum(low_ref[i], HALO) // TK
         count = (HALO + first) // TK + 1 - j_low
-        row = lax.broadcasted_iota(jnp.int32, (TQ, TK), 0) + (HALO + first)
+        parts, row = head_parts(qkv_ref, i), positions(i)
         for blocks in range(1, MOST_BLOCKS + 1):
 
             @pl.when(count == blocks)
             def _():
-                q = qkv_ref[pl.ds(first, TQ), 0:256]
                 top, total, acc = partial_softmax(
-                    q, row, j_low, blocks, True, ends_ref, keys_at, values_at, s_ref
+                    parts, [row], j_low, blocks, True, ends_ref, keys_at, values_at, s_ref
                 )
                 result = acc / total
-                kept_ref[i] = result
+                norm = top * SCALE + jnp.log(total)
+                kept_ref[i, 0] = result
+                kept_ref[i, 1] = norm
                 keep(held_ref, i, result)
-                keep_norm(norm_ref, i, top * SCALE + jnp.log(total))
-
-        @pl.when(low_ref[i] >= HALO)
+                keep_norm(norm_ref, i, norm)
+
+        pair_low = low_ref[i // 2 * 2]
+
+        @pl.when(pair_low >= HALO)
         def _():
             out_copy(i, held_ref, out_ref, sems).start()
 
-        @pl.when(low_ref[i] < HALO)
+        @pl.when(pair_low < HALO)
         def _():
             part_copy(i, kept_ref, part_ref, sems).start()
 
@@ -252,13 +269,13 @@
     lax.fori_loop(0, BLOCKS, block, 0)
     for i in range(BLOCKS):
 
-        @pl.when(low_ref[i] >= HALO)
+        @pl.when(low_ref[i // 2 * 2] >= HALO)
         def _():
             out_copy(i, held_ref, out_ref, sems).wait()
 
         if i < HALO_BLOCKS:
 
-            @pl.when(low_ref[i] < HALO)
+            @pl.when(low_ref[i // 2 * 2] < HALO)
             def _():
                 part_copy(i, kept_ref, part_ref, sems).wait()
 
@@ -273,11 +290,11 @@
         out_shape=[
             jax.ShapeDtypeStruct((SPAN, 256), jnp.bfloat16),
             jax.ShapeDtypeStruct((128, 128), jnp.float32),
-            jax.ShapeDtypeStruct((HALO_BLOCKS, 2 * TQ, 128), jnp.float32),
+            jax.ShapeDtypeStruct((HALO_BLOCKS, 2, 2 * TQ, 128), jnp.float32),
         ],
         scratch_shapes=[
             pltpu.VMEM((BLOCKS, TQ, 256), jnp.bfloat16),
-            pltpu.VMEM((BLOCKS, 2 * TQ, 128), jnp.float32),
+            pltpu.VMEM((BLOCKS, 2, 2 * TQ, 128), jnp.float32),
             pltpu.VMEM((MOST_BLOCKS, 2 * TQ, TK), jnp.float32),
             pltpu.SemaphoreType.DMA((2, BLOCKS)),
         ],
@@ -290,7 +307,7 @@
     held_ref, kept_ref, s_ref, norm_acc, norm_t, sems = refs[9:]
     for i in range(HALO_BLOCKS):
 
-        @pl.when(low_ref[i] < HALO)
+        @pl.when(low_ref[i // 2 * 2] < HALO)
         def _():
             part_copy(i, part_ref, kept_ref, sems).start()
 
@@ -299,40 +316,46 @@
     keys_at = lambda j: halo_ref[rows(j), 0:128]
     values_at = lambda j: halo_ref[rows(j), 128:256]
 
-    def block(i, carry):
-        first = pl.multiple_of(i * TQ, TQ)
-        j_low = low_ref[i] // TK
+    def pair(p, carry):
+        pair_blocks = (2 * p, 2 * p + 1)
+        j_low = low_ref[2 * p] // TK
         count = HALO // TK - j_low
-        row = lax.broadcasted_iota(jnp.int32, (TQ, TK), 0) + (HALO + first)
-
         for blocks in range(1, HALO // TK + 1):
 
             @pl.when(count == blocks)
             def _():
-                q = qkv_ref[pl.ds(first, TQ), 0:256]
                 top, total, acc = partial_softmax(
-                    q, row, j_low, blocks, False, ends_ref, keys_at, values_at, s_ref
+                    [part for i in pair_blocks for part in head_parts(qkv_ref, i)],
+                    [positions(i) for i in pair_blocks],
+                    j_low,
+                    blocks,
+                    False,
+                    ends_ref,
+                    keys_at,
+                    values_at,
+                    s_ref,
                 )
-                own = kept_norm(norm_acc, i)
-                part_copy(i, part_ref, kept_ref, sems).wait()
-                top = top * SCALE
-                most = jnp.maximum(own, top)
-                own = jnp.exp(own - most)
-                here = jnp.exp(top - most)
-                total = own + total * here
-                keep(held_ref, i, (kept_ref[i] * own + acc * here) / total)
-                keep_norm(norm_acc, i, most + jnp.log(total))
-                out_copy(i, held_ref, out_ref, sems).start()
+                for i in pair_blocks:
+                    part_copy(i, part_ref, kept_ref, sems).wait()
+                for n, i in enumerate(pair_blocks):
+                    at = slice(2 * n * TQ, 2 * (n + 1) * TQ)
+                    own, these = kept_ref[i, 1], top[at] * SCALE
+                    most = jnp.maximum(own, these)
+                    own, these = jnp.exp(own - most), jnp.exp(these - most)
+                    whole = own + total[at] * these
+                    keep(held_ref, i, (kept_ref[i, 0] * own + acc[at] * these) / whole)
+                    out_copy(i, held_ref, out_ref, sems).start()
+                    keep_norm(norm_acc, i, most + jnp.log(whole))
 
         return carry
 
-    lax.fori_loop(0, HALO_BLOCKS, block, 0)
+    lax.fori_loop(0, HALO_BLOCKS // 2, pair, 0)
     norm_t[...] = jnp.transpose(norm_acc[...])
     for d in range(8):
         norm_refs[d][...] = norm_t[pl.ds(pl.multiple_of(((low_ref[BLOCKS] + d) % 8) * 8, 8), 8)]
     for i in range(HALO_BLOCKS):
 
-        @pl.when(low_ref[i] < HALO)
+        @pl.when(low_ref[i // 2 * 2] < HALO)
         def _():
             out_copy(i, held_ref, out_ref, sems).wait()
 
@@ -356,8 +379,8 @@
         + [pltpu.VMEM((8, 128), jnp.float32)] * 8,
         scratch_shapes=[
             pltpu.VMEM((HALO_BLOCKS, TQ, 256), jnp.bfloat16),
-            pltpu.VMEM((HALO_BLOCKS, 2 * TQ, 128), jnp.float32),
-            pltpu.VMEM((HALO // TK, 2 * TQ, TK), jnp.float32),
+            pltpu.VMEM((HALO_BLOCKS, 2, 2 * TQ, 128), jnp.float32),
+            pltpu.VMEM((HALO // TK, 4 * TQ, TK), jnp.float32),
             pltpu.VMEM((128, 128), jnp.float32),
             pltpu.VMEM((128, 128), jnp.float32),
             pltpu.SemaphoreType.DMA((2, HALO_BLOCKS)),

time: 139 us -> 137 us (0.986)
  the two profiles are of different devices: /device:TPU:4 before, /device:TPU:6 now
where the time goes in v7:
time: 137 us; the launch traced here: 136 us
  blocking collectives  70.4 us (51%)
  starting transfers between devices  41.2 us (30%)
  Pallas kernels  17.8 us (13%)
  local copies, waits for them, and re-layouts  2.95 us (2%)
  waiting for transfers between devices  2.68 us (2%)
    all_to_all x1, blocking collectives, per_device(): moved = lax.all_to_all(packed, PLANE, 0, 0, tiled=True)  70.4 us
    ppermute x7, starting transfers between devices, per_device(): lax.ppermute(pieces[d], 'z', [(i, (i + d) % 8) for i in range(8)])  29.9 us
    all_to_all x1, starting transfers between devices, per_device(): back = lax.all_to_all(out.reshape(128, 16, 256), PLANE, 0, 0, tiled=True)  9.84 us
    pallas_call x1, Pallas kernels, attend_local(): pl.pallas_call(local_body, in_specs=[pl.BlockSpec(memory_space=pltpu.SMEM...  8.92 us
    pallas_call x1, Pallas kernels, attend_halo(): pl.pallas_call(halo_body, in_specs=[pl.BlockSpec(memory_space=pltpu.SMEM)...  3.22 us
    pallas_call x1, Pallas kernels, pack(): pl.pallas_call(pack_body, in_specs=[pl.BlockSpec(memory_space=pl.ANY)] *...  2.94 us
    unnamed x4, local copies, waits for them, and re-layouts  2.92 us
  transfers between devices with their start and end apart: 9, of which 2 were waited for; matrix products, arithmetic and copies ran while one was open for 0% of the time, Pallas kernels for 8%

profile of v7, /device:TPU:6, one launch (start us, length us, event | category | flops | bytes accessed | tf_op | source)
XLA Modules:
  0.0 136.0 jit_solution(4557687621364149051)
XLA Ops:
  0.6 2.9 %pack.1 = bf16[8,16,16,512]{3,2,1,0:T(8,128)(2,1)} custom-call(bf16[8,16,4096]{2,1,0:T(8,128)(2,1)} %q_ref.1, bf16[8,16,2048]{2,1,0:T(8,128)(2,1)} %k_ref.1, bf16[8,16,2048]{2,1,0:T(8,128)(2,1)} %v_ref.1), custom_call_target="tpu_custom_call" | custom-call | tf_op jit(solution)/shard_map/pack/pallas_call | solution.py:94
  3.6 70.4 %all_to_all.10 = bf16[128,16,512]{2,1,0:T(8,128)(2,1)S(1)} all-to-all(bf16[128,16,512]{2,1,0:T(8,128)(2,1)} %bitcast.10), channel_id=1, replica_groups=mesh['x'=4,'z'=8,'y'=8,'c'=2] {'z','y','c'}, dimensions={0} | all-to-all | bytes 4194304 | tf_op jit(solution)/shard_map/all_to_all | solution.py:397
  74.0 1.3 copy-done
  75.3 1.5 %collective-permute-start = (bf16[1024,256]{1,0:T(8,128)(2,1)S(1)}, bf16[1024,256]{1,0:T(8,128)(2,1)S(1)}, u32[]{:S(2)}, u32[]{:S(2)}) collective-permute-start(bf16[1024,256]{1,0:T(8,128)(2,1)S(1)} %slice.4), channel_id=1, source_target_pairs={{0,128},{128,256},{256,384},{1,129},{129,257},{257,385},{2,130},{1... | collective-permute-start | bytes 1572872 | tf_op jit(solution)/shard_map/ppermute | solution.py:400
  76.8 1.6 %doc_bounds.1 = (s32[9]{0:T(128)}, s32[12,256]{1,0:T(8,128)}) custom-call(s32[8,32]{1,0:T(8,128)} %lengths_ref.1, s32[1]{0:T(128)} %bitcast.row_ref, s32[1]{0:T(128)} %bitcast.1.base_ref), custom_call_target="tpu_custom_call" | custom-call | tf_op jit(solution)/shard_map/doc_bounds/pallas_call | solution.py:53
  78.4 1.6 %copy-done.1 = bf16[128,16,512]{2,1,0:T(8,128)(2,1)S(1)} copy-done((bf16[128,16,512]{2,1,0:T(8,128)(2,1)S(1)}, bf16[128,16,512]{2,1,0:T(8,128)(2,1)}, u32[]{:S(2)}) %copy-start.1) | copy-done | bytes 2097176
  80.0 8.9 %attend_local.1 = (bf16[2048,256]{1,0:T(8,128)(2,1)}, f32[128,128]{1,0:T(8,128)}, f32[4,2,512,128]{3,2,1,0:T(8,128)}) custom-call(s32[9]{0:T(128)} %get-tuple-element.16.low_ref, s32[12,256]{1,0:T(8,128)} %get-tuple-element.17.ends_ref, bf16[2048,512]{1,0:T(8,128)(2,1)S(1)} %bitcast.7), custom_call_target="tpu_custom_call" | custom-call | tf_op jit(solution)/shard_map/attend_local/pallas_call | solution.py:286
  88.9 0.5 collective-permute-done.halo_ref
  89.4 3.2 %attend_halo.1 = (bf16[2048,256]{1,0:T(8,128)(2,1)}, f32[8,128]{1,0:T(8,128)S(1)}, f32[8,128]{1,0:T(8,128)S(1)}, f32[8,128]{1,0:T(8,128)S(1)}, f32[8,128]{1,0:T(...) custom-call(s32[9]{0:T(128)} %get-tuple-element.16.low_ref, ...), custom_call_target="tpu_custom_call", output_to_operand_aliasing={{0}: (4, {})} | custom-call | tf_op jit(solution)/shard_map/attend_halo/pallas_call | solution.py:366
  92.6 9.8 %all-to-all-start.1 = ((bf16[128,16,256]{2,1,0:T(8,128)(2,1)}), bf16[128,16,256]{2,1,0:T(8,128)(2,1)S(1)}, u32[]{:S(2)}, u32[]{:S(2)}) async-start(bf16[128,16,256]{2,1,0:T(8,128)(2,1)} %bitcast.11), calls=%async_computation.1 | async-start | bytes 2097152 | tf_op jit(solution)/shard_map/all_to_all | solution.py:403
  102.5 3.0 %collective-permute-start.1 = (f32[8,128]{1,0:T(8,128)S(1)}, f32[8,128]{1,0:T(8,128)S(1)}, u32[]{:S(2)}, u32[]{:S(2)}) collective-permute-start(f32[8,128]{1,0:T(8,128)S(1)} %get-tuple-element.23), channel_id=1, source_target_pairs={{0,16},{16,32},{32,48},{48,64},{64,80},{80,96},{96,112},{112,0},{1... | collective-permute-start | bytes 12296 | tf_op jit(solution)/shard_map/ppermute | solution.py:405
  105.5 4.5 %collective-permute-start.2 = (f32[8,128]{1,0:T(8,128)S(1)}, f32[8,128]{1,0:T(8,128)S(1)}, u32[]{:S(2)}, u32[]{:S(2)}) collective-permute-start(f32[8,128]{1,0:T(8,128)S(1)} %get-tuple-element.24), channel_id=1, source_target_pairs={{0,32},{16,48},{32,64},{48,80},{64,96},{80,112},{96,0},{112,16},{1... | collective-permute-start | bytes 12296 | tf_op jit(solution)/shard_map/ppermute | solution.py:405
  110.0 4.9 %collective-permute-start.3 = (f32[8,128]{1,0:T(8,128)S(1)}, f32[8,128]{1,0:T(8,128)S(1)}, u32[]{:S(2)}, u32[]{:S(2)}) collective-permute-start(f32[8,128]{1,0:T(8,128)S(1)} %get-tuple-element.25), channel_id=1, source_target_pairs={{0,48},{16,64},{32,80},{48,96},{64,112},{80,0},{96,16},{112,32},{1... | collective-permute-start | bytes 12296 | tf_op jit(solution)/shard_map/ppermute | solution.py:405
  114.9 3.8 %collective-permute-start.4 = (f32[8,128]{1,0:T(8,128)S(1)}, f32[8,128]{1,0:T(8,128)S(1)}, u32[]{:S(2)}, u32[]{:S(2)}) collective-permute-start(f32[8,128]{1,0:T(8,128)S(1)} %get-tuple-element.26), channel_id=1, source_target_pairs={{0,64},{16,80},{32,96},{48,112},{64,0},{80,16},{96,32},{112,48},{1... | collective-permute-start | bytes 12296 | tf_op jit(solution)/shard_map/ppermute | solution.py:405
  118.8 5.1 %collective-permute-start.5 = (f32[8,128]{1,0:T(8,128)S(1)}, f32[8,128]{1,0:T(8,128)S(1)}, u32[]{:S(2)}, u32[]{:S(2)}) collective-permute-start(f32[8,128]{1,0:T(8,128)S(1)} %get-tuple-element.27), channel_id=1, source_target_pairs={{0,80},{16,96},{32,112},{48,0},{64,16},{80,32},{96,48},{112,64},{1... | collective-permute-start | bytes 12296 | tf_op jit(solution)/shard_map/ppermute | solution.py:405
  123.9 0.0 collective-permute-done.1.refs_1_
  123.9 5.3 %collective-permute-start.6 = (f32[8,128]{1,0:T(8,128)S(1)}, f32[8,128]{1,0:T(8,128)S(1)}, u32[]{:S(2)}, u32[]{:S(2)}) collective-permute-start(f32[8,128]{1,0:T(8,128)S(1)} %get-tuple-element.28), channel_id=1, source_target_pairs={{0,96},{16,112},{32,0},{48,16},{64,32},{80,48},{96,64},{112,80},{1... | collective-permute-start | bytes 12296 | tf_op jit(solution)/shard_map/ppermute | solution.py:405
  129.2 0.0 collective-permute-done.2.refs_2_
  129.2 3.3 %collective-permute-start.7 = (f32[8,128]{1,0:T(8,128)S(1)}, f32[8,128]{1,0:T(8,128)S(1)}, u32[]{:S(2)}, u32[]{:S(2)}) collective-permute-start(f32[8,128]{1,0:T(8,128)S(1)} %get-tuple-element.29), channel_id=1, source_target_pairs={{0,112},{16,0},{32,16},{48,32},{64,48},{80,64},{96,80},{112,96},{1... | collective-permute-start | bytes 12296 | tf_op jit(solution)/shard_map/ppermute | solution.py:405
  132.4 0.0 collective-permute-done.3.refs_3_
  132.5 0.0 collective-permute-done.4.refs_4_
  132.5 0.0 collective-permute-done.6.refs_6_
  132.5 2.2 %collective-permute-done.7.refs_7_ = f32[8,128]{1,0:T(8,128)S(1)} collective-permute-done((f32[8,128]{1,0:T(8,128)S(1)}, f32[8,128]{1,0:T(8,128)S(1)}, u32[]{:S(2)}, u32[]{:S(2)}) %collective-permute-start.7) | collective-permute-done | bytes 4128 | tf_op jit(solution)/shard_map/ppermute | solution.py:405
  134.7 1.1 unpack.1
  (5 shorter events, 0.0 us)
Async XLA Ops:
  74.0 1.3 copy-start
  75.3 14.0 %collective-permute-start = (bf16[1024,256]{1,0:T(8,128)(2,1)S(1)}, bf16[1024,256]{1,0:T(8,128)(2,1)S(1)}, u32[]{:S(2)}, u32[]{:S(2)}) collective-permute-start(bf16[1024,256]{1,0:T(8,128)(2,1)S(1)} %slice.4), channel_id=1, source_target_pairs={{0,128},{128,256},{256,384},{1,129},{129,257},{257,385},{2,130},{1... | collective-permute-start | bytes 1572872 | tf_op jit(solution)/shard_map/ppermute | solution.py:400
  78.4 1.6 %copy-start.1 = (bf16[128,16,512]{2,1,0:T(8,128)(2,1)S(1)}, bf16[128,16,512]{2,1,0:T(8,128)(2,1)}, u32[]{:S(2)}) copy-start(bf16[128,16,512]{2,1,0:T(8,128)(2,1)} %copy-done) | copy-start | bytes 6291460
  92.6 42.1 %all-to-all-start.1 = ((bf16[128,16,256]{2,1,0:T(8,128)(2,1)}), bf16[128,16,256]{2,1,0:T(8,128)(2,1)S(1)}, u32[]{:S(2)}, u32[]{:S(2)}) async-start(bf16[128,16,256]{2,1,0:T(8,128)(2,1)} %bitcast.11), calls=%async_computation.1 | async-start | bytes 2097152 | tf_op jit(solution)/shard_map/all_to_all | solution.py:403
  102.5 21.4 %collective-permute-start.1 = (f32[8,128]{1,0:T(8,128)S(1)}, f32[8,128]{1,0:T(8,128)S(1)}, u32[]{:S(2)}, u32[]{:S(2)}) collective-permute-start(f32[8,128]{1,0:T(8,128)S(1)} %get-tuple-element.23), channel_id=1, source_target_pairs={{0,16},{16,32},{32,48},{48,64},{64,80},{80,96},{96,112},{112,0},{1... | collective-permute-start | bytes 12296 | tf_op jit(solution)/shard_map/ppermute | solution.py:405
  105.5 23.7 %collective-permute-start.2 = (f32[8,128]{1,0:T(8,128)S(1)}, f32[8,128]{1,0:T(8,128)S(1)}, u32[]{:S(2)}, u32[]{:S(2)}) collective-permute-start(f32[8,128]{1,0:T(8,128)S(1)} %get-tuple-element.24), channel_id=1, source_target_pairs={{0,32},{16,48},{32,64},{48,80},{64,96},{80,112},{96,0},{112,16},{1... | collective-permute-start | bytes 12296 | tf_op jit(solution)/shard_map/ppermute | solution.py:405
  110.0 22.5 %collective-permute-start.3 = (f32[8,128]{1,0:T(8,128)S(1)}, f32[8,128]{1,0:T(8,128)S(1)}, u32[]{:S(2)}, u32[]{:S(2)}) collective-permute-start(f32[8,128]{1,0:T(8,128)S(1)} %get-tuple-element.25), channel_id=1, source_target_pairs={{0,48},{16,64},{32,80},{48,96},{64,112},{80,0},{96,16},{112,32},{1... | collective-permute-start | bytes 12296 | tf_op jit(solution)/shard_map/ppermute | solution.py:405
  114.9 17.5 %collective-permute-start.4 = (f32[8,128]{1,0:T(8,128)S(1)}, f32[8,128]{1,0:T(8,128)S(1)}, u32[]{:S(2)}, u32[]{:S(2)}) collective-permute-start(f32[8,128]{1,0:T(8,128)S(1)} %get-tuple-element.26), channel_id=1, source_target_pairs={{0,64},{16,80},{32,96},{48,112},{64,0},{80,16},{96,32},{112,48},{1... | collective-permute-start | bytes 12296 | tf_op jit(solution)/shard_map/ppermute | solution.py:405
  118.8 13.7 %collective-permute-start.5 = (f32[8,128]{1,0:T(8,128)S(1)}, f32[8,128]{1,0:T(8,128)S(1)}, u32[]{:S(2)}, u32[]{:S(2)}) collective-permute-start(f32[8,128]{1,0:T(8,128)S(1)} %get-tuple-element.27), channel_id=1, source_target_pairs={{0,80},{16,96},{32,112},{48,0},{64,16},{80,32},{96,48},{112,64},{1... | collective-permute-start | bytes 12296 | tf_op jit(solution)/shard_map/ppermute | solution.py:405
  123.9 8.6 %collective-permute-start.6 = (f32[8,128]{1,0:T(8,128)S(1)}, f32[8,128]{1,0:T(8,128)S(1)}, u32[]{:S(2)}, u32[]{:S(2)}) collective-permute-start(f32[8,128]{1,0:T(8,128)S(1)} %get-tuple-element.28), channel_id=1, source_target_pairs={{0,96},{16,112},{32,0},{48,16},{64,32},{80,48},{96,64},{112,80},{1... | collective-permute-start | bytes 12296 | tf_op jit(solution)/shard_map/ppermute | solution.py:405
  129.2 5.5 %collective-permute-start.7 = (f32[8,128]{1,0:T(8,128)S(1)}, f32[8,128]{1,0:T(8,128)S(1)}, u32[]{:S(2)}, u32[]{:S(2)}) collective-permute-start(f32[8,128]{1,0:T(8,128)S(1)} %get-tuple-element.29), channel_id=1, source_target_pairs={{0,112},{16,0},{32,16},{48,32},{64,48},{80,64},{96,80},{112,96},{1... | collective-permute-start | bytes 12296 | tf_op jit(solution)/shard_map/ppermute | solution.py:405

commit v8 on v7

--- a/solution.py
+++ b/solution.py
@@ -120,7 +120,7 @@
             at = 2 * h + n
             held = jnp.zeros((8, 128), jnp.float32)
             for d in range(8):
-                held = jnp.where(rows == (row_ref[0] + 8 - d) % 8, pieces[d][at : at + 1], held)
+                held = jnp.where(rows == (row_ref[0] + 8 - d) % 8, pieces[d % 4][d // 4, at : at + 1], held)
             norm_ref[h, :, n * 128 : (n + 1) * 128] = held
     norm_copy = pltpu.make_async_copy(norm_ref, norm_out, norm_sem)
     norm_copy.start()
@@ -129,11 +129,11 @@
         copy.wait()
 
 
-def unpack(row, parts, pieces):
+def unpack(row, parts, pairs):
     vmem = pl.BlockSpec(memory_space=pltpu.VMEM)
     return pl.pallas_call(
         unpack_body,
-        in_specs=[pl.BlockSpec(memory_space=pltpu.SMEM)] + [vmem] * 9,
+        in_specs=[pl.BlockSpec(memory_space=pltpu.SMEM)] + [vmem] * 5,
         out_specs=[pl.BlockSpec(memory_space=pl.ANY)] * 2,
         out_shape=[
             jax.ShapeDtypeStruct((ROWS, 16, 4096), jnp.bfloat16),
@@ -145,7 +145,7 @@
             pltpu.SemaphoreType.DMA,
         ],
         name="unpack",
-    )(row, *in_vmem(parts, *pieces))
+    )(row, *in_vmem(parts, *pairs))
 
 
 def partial_softmax(parts, rows, j_low, blocks, diagonal, ends_ref, keys_at, values_at, s_ref):
@@ -303,8 +303,8 @@
 
 
 def halo_body(low_ref, ends_ref, qkv_ref, halo_ref, prev_ref, prev_norm, part_ref, *refs):
-    out_ref, *norm_refs = refs[:9]
-    held_ref, kept_ref, s_ref, norm_acc, norm_t, sems = refs[9:]
+    out_ref, *norm_refs = refs[:3]
+    held_ref, kept_ref, s_ref, norm_acc, norm_t, sems = refs[3:]
     for i in range(HALO_BLOCKS):
 
         @pl.when(low_ref[i // 2 * 2] < HALO)
@@ -352,7 +352,7 @@
     lax.fori_loop(0, HALO_BLOCKS // 2, pair, 0)
     norm_t[...] = jnp.transpose(norm_acc[...])
     for d in range(8):
-        norm_refs[d][...] = norm_t[pl.ds(pl.multiple_of(((low_ref[BLOCKS] + d) % 8) * 8, 8), 8)]
+        norm_refs[d // 4][d % 4] = norm_t[pl.ds(pl.multiple_of(((low_ref[BLOCKS] + d) % 8) * 8, 8), 8)]
     for i in range(HALO_BLOCKS):
 
         @pl.when(low_ref[i // 2 * 2] < HALO)
@@ -374,9 +374,9 @@
             vmem,
             any_space,
         ],
-        out_specs=[any_space] + [vmem] * 8,
+        out_specs=[any_space] + [vmem] * 2,
         out_shape=[jax.ShapeDtypeStruct((SPAN, 256), jnp.bfloat16)]
-        + [pltpu.VMEM((8, 128), jnp.float32)] * 8,
+        + [pltpu.VMEM((4, 8, 128), jnp.float32)] * 2,
         scratch_shapes=[
             pltpu.VMEM((HALO_BLOCKS, TQ, 256), jnp.bfloat16),
             pltpu.VMEM((HALO_BLOCKS, 2, 2 * TQ, 128), jnp.float32),
@@ -399,11 +399,13 @@
     qkv = moved.reshape(SPAN, 512)
     halo = lax.ppermute(qkv[SPAN - HALO :, 256:512], "x", [(i, i + 1) for i in range(3)])
     out, norm, part = attend_local(low, ends, qkv)
-    out, *pieces = attend_halo(low, ends, qkv, halo, out, norm, part)
+    out, near, far = attend_halo(low, ends, qkv, halo, out, norm, part)
     back = lax.all_to_all(out.reshape(128, 16, 256), PLANE, 0, 0, tiled=True)
-    for d in range(1, 8):
-        pieces[d] = lax.ppermute(pieces[d], "z", [(i, (i + d) % 8) for i in range(8)])
-    attended, log_norm = unpack(row[None], back.reshape(ROWS, KV_HEADS, 16, 256), pieces)
+    far = lax.ppermute(far, "z", [(i, (i + 4) % 8) for i in range(8)])
+    pairs = [jnp.stack((near[d], far[d])) for d in range(4)]
+    for d in range(1, 4):
+        pairs[d] = lax.ppermute(pairs[d], "z", [(i, (i + d) % 8) for i in range(8)])
+    attended, log_norm = unpack(row[None], back.reshape(ROWS, KV_HEADS, 16, 256), pairs)
     return attended, log_norm
 
 

time: 137 us -> 146 us (1.066)
  the two profiles are of different devices: /device:TPU:6 before, /device:TPU:38 now
where the time goes in v8:
time: 146 us; the launch traced here: 145 us
  blocking collectives  67.5 us (46%)
  starting transfers between devices  31 us (21%)
  waiting for transfers between devices  25.1 us (17%)
  Pallas kernels  17.7 us (12%)
  local copies, waits for them, and re-layouts  2.94 us (2%)
    all_to_all x1, blocking collectives, per_device(): moved = lax.all_to_all(packed, PLANE, 0, 0, tiled=True)  67.5 us
    ppermute x1, waiting for transfers between devices, per_device(): far = lax.ppermute(far, 'z', [(i, (i + 4) % 8) for i in range(8)])  19.4 us
    ppermute x3, starting transfers between devices, per_device(): pairs[d] = lax.ppermute(pairs[d], 'z', [(i, (i + d) % 8) for i in range(8)])  11.2 us
    all_to_all x1, starting transfers between devices, per_device(): back = lax.all_to_all(out.reshape(128, 16, 256), PLANE, 0, 0, tiled=True)  10.7 us
    pallas_call x1, Pallas kernels, attend_local(): pl.pallas_call(local_body, in_specs=[pl.BlockSpec(memory_space=pltpu.SMEM...  8.91 us
    ppermute x1, starting transfers between devices, per_device(): far = lax.ppermute(far, 'z', [(i, (i + 4) % 8) for i in range(8)])  7.65 us
    ppermute x3, waiting for transfers between devices, per_device(): pairs[d] = lax.ppermute(pairs[d], 'z', [(i, (i + d) % 8) for i in range(8)])  3.98 us
    pallas_call x1, Pallas kernels, attend_halo(): pl.pallas_call(halo_body, in_specs=[pl.BlockSpec(memory_space=pltpu.SMEM)...  3.22 us
  transfers between devices with their start and end apart: 6, of which 4 were waited for; matrix products, arithmetic and copies ran while one was open for 0% of the time, Pallas kernels for 7%

profile of v8, /device:TPU:38, one launch (start us, length us, event | category | flops | bytes accessed | tf_op | source)
XLA Modules:
  0.0 145.2 jit_solution(6467587745088007361)
XLA Ops:
  0.6 2.9 %pack.1 = bf16[8,16,16,512]{3,2,1,0:T(8,128)(2,1)} custom-call(bf16[8,16,4096]{2,1,0:T(8,128)(2,1)} %q_ref.1, bf16[8,16,2048]{2,1,0:T(8,128)(2,1)} %k_ref.1, bf16[8,16,2048]{2,1,0:T(8,128)(2,1)} %v_ref.1), custom_call_target="tpu_custom_call" | custom-call | tf_op jit(solution)/shard_map/pack/pallas_call | solution.py:94
  3.5 67.5 %all_to_all.10 = bf16[128,16,512]{2,1,0:T(8,128)(2,1)S(1)} all-to-all(bf16[128,16,512]{2,1,0:T(8,128)(2,1)} %bitcast.10), channel_id=1, replica_groups=mesh['x'=4,'z'=8,'y'=8,'c'=2] {'z','y','c'}, dimensions={0} | all-to-all | bytes 4194304 | tf_op jit(solution)/shard_map/all_to_all | solution.py:397
  71.1 0.0 copy-start
  71.1 1.3 copy-done
  72.4 1.5 %collective-permute-start = (bf16[1024,256]{1,0:T(8,128)(2,1)S(1)}, bf16[1024,256]{1,0:T(8,128)(2,1)S(1)}, u32[]{:S(2)}, u32[]{:S(2)}) collective-permute-start(bf16[1024,256]{1,0:T(8,128)(2,1)S(1)} %slice.36), channel_id=1, source_target_pairs={{0,128},{128,256},{256,384},{1,129},{129,257},{257,385},{2,130},{1... | collective-permute-start | bytes 1572872 | tf_op jit(solution)/shard_map/ppermute | solution.py:400
  73.9 1.6 %doc_bounds.1 = (s32[9]{0:T(128)}, s32[12,256]{1,0:T(8,128)}) custom-call(s32[8,32]{1,0:T(8,128)} %lengths_ref.1, s32[1]{0:T(128)} %bitcast.row_ref, s32[1]{0:T(128)} %bitcast.1.base_ref), custom_call_target="tpu_custom_call" | custom-call | tf_op jit(solution)/shard_map/doc_bounds/pallas_call | solution.py:53
  75.4 0.0 copy-start.1
  75.4 1.6 %copy-done.1 = bf16[128,16,512]{2,1,0:T(8,128)(2,1)S(1)} copy-done((bf16[128,16,512]{2,1,0:T(8,128)(2,1)S(1)}, bf16[128,16,512]{2,1,0:T(8,128)(2,1)}, u32[]{:S(2)}) %copy-start.1) | copy-done | bytes 2097176
  77.0 8.9 %attend_local.1 = (bf16[2048,256]{1,0:T(8,128)(2,1)}, f32[128,128]{1,0:T(8,128)}, f32[4,2,512,128]{3,2,1,0:T(8,128)}) custom-call(s32[9]{0:T(128)} %get-tuple-element.10.low_ref, s32[12,256]{1,0:T(8,128)} %get-tuple-element.11.ends_ref, bf16[2048,512]{1,0:T(8,128)(2,1)S(1)} %bitcast.7), custom_call_target="tpu_custom_call" | custom-call | tf_op jit(solution)/shard_map/attend_local/pallas_call | solution.py:286
  86.0 1.7 %collective-permute-done.halo_ref = bf16[1024,256]{1,0:T(8,128)(2,1)S(1)} collective-permute-done((bf16[1024,256]{1,0:T(8,128)(2,1)S(1)}, bf16[1024,256]{1,0:T(8,128)(2,1)S(1)}, u32[]{:S(2)}, u32[]{:S(2)}) %collective-permute-start) | collective-permute-done | bytes 524320 | tf_op jit(solution)/shard_map/ppermute | solution.py:400
  87.7 3.2 %attend_halo.1 = (bf16[2048,256]{1,0:T(8,128)(2,1)}, f32[4,8,128]{2,1,0:T(8,128)S(1)}, f32[4,8,128]{2,1,0:T(8,128)S(1)}) custom-call(s32[9]{0:T(128)} %get-tuple-element.10.low_ref, s32[12,256]{1,0:T(8,128)} %get-tuple-element.11.ends_ref, bf16[2048,512]{1,0:T(8,128)(2,1)S(1)} %bitcast.8, ...), custom_call_target="tpu_custom_call", output_to_operand_aliasing={{0}: (4, {})} | custom-call | tf_op jit(solution)/shard_map/attend_halo/pallas_call | solution.py:366
  90.9 10.7 %all-to-all-start.1 = ((bf16[128,16,256]{2,1,0:T(8,128)(2,1)}), bf16[128,16,256]{2,1,0:T(8,128)(2,1)S(1)}, u32[]{:S(2)}, u32[]{:S(2)}) async-start(bf16[128,16,256]{2,1,0:T(8,128)(2,1)} %bitcast.11), calls=%async_computation.1 | async-start | bytes 2097152 | tf_op jit(solution)/shard_map/all_to_all | solution.py:403
  101.6 7.6 %collective-permute-start.1 = (f32[4,8,128]{2,1,0:T(8,128)S(1)}, f32[4,8,128]{2,1,0:T(8,128)S(1)}, u32[]{:S(2)}, u32[]{:S(2)}) collective-permute-start(f32[4,8,128]{2,1,0:T(8,128)S(1)} %get-tuple-element.17), channel_id=1, source_target_pairs={{0,64},{16,80},{32,96},{48,112},{64,0},{80,16},{96,32},{112,48},{1... | collective-permute-start | bytes 49160 | tf_op jit(solution)/shard_map/ppermute | solution.py:404
  109.3 19.4 %collective-permute-done.1 = f32[4,8,128]{2,1,0:T(8,128)S(1)} collective-permute-done((f32[4,8,128]{2,1,0:T(8,128)S(1)}, f32[4,8,128]{2,1,0:T(8,128)S(1)}, u32[]{:S(2)}, u32[]{:S(2)}) %collective-permute-start.1) | collective-permute-done | bytes 16416 | tf_op jit(solution)/shard_map/ppermute | solution.py:404
  128.6 4.8 %collective-permute-start.2 = (f32[2,8,128]{2,1,0:T(8,128)S(1)}, f32[2,8,128]{2,1,0:T(8,128)S(1)}, u32[]{:S(2)}, u32[]{:S(2)}) collective-permute-start(f32[2,8,128]{2,1,0:T(8,128)S(1)} %pad_maximum_fusion.1), channel_id=1, source_target_pairs={{0,16},{16,32},{32,48},{48,64},{64,80},{80,96},{96,112},{112,0},{1... | collective-permute-start | bytes 24584 | tf_op jit(solution)/shard_map/ppermute | solution.py:407
  133.4 1.9 %collective-permute-start.3 = (f32[2,8,128]{2,1,0:T(8,128)S(1)}, f32[2,8,128]{2,1,0:T(8,128)S(1)}, u32[]{:S(2)}, u32[]{:S(2)}) collective-permute-start(f32[2,8,128]{2,1,0:T(8,128)S(1)} %pad_maximum_fusion.2), channel_id=1, source_target_pairs={{0,32},{16,48},{32,64},{48,80},{64,96},{80,112},{96,0},{112,16},{1... | collective-permute-start | bytes 24584 | tf_op jit(solution)/shard_map/ppermute | solution.py:407
  135.4 4.5 %collective-permute-start.4 = (f32[2,8,128]{2,1,0:T(8,128)S(1)}, f32[2,8,128]{2,1,0:T(8,128)S(1)}, u32[]{:S(2)}, u32[]{:S(2)}) collective-permute-start(f32[2,8,128]{2,1,0:T(8,128)S(1)} %pad_maximum_fusion.3), channel_id=1, source_target_pairs={{0,48},{16,64},{32,80},{48,96},{64,112},{80,0},{96,16},{112,32},{1... | collective-permute-start | bytes 24584 | tf_op jit(solution)/shard_map/ppermute | solution.py:407
  139.9 0.0 collective-permute-done.2.refs_1_
  139.9 1.1 collective-permute-done.3.refs_2_
  141.1 2.8 %collective-permute-done.4.refs_3_ = f32[2,8,128]{2,1,0:T(8,128)S(1)} collective-permute-done((f32[2,8,128]{2,1,0:T(8,128)S(1)}, f32[2,8,128]{2,1,0:T(8,128)S(1)}, u32[]{:S(2)}, u32[]{:S(2)}) %collective-permute-start.4) | collective-permute-done | bytes 8224 | tf_op jit(solution)/shard_map/ppermute | solution.py:407
  143.9 0.0 all-to-all-done.1
  143.9 1.1 unpack.1
  (7 shorter events, 0.1 us)
Async XLA Ops:
  71.1 1.3 copy-start
  72.4 15.3 %collective-permute-start = (bf16[1024,256]{1,0:T(8,128)(2,1)S(1)}, bf16[1024,256]{1,0:T(8,128)(2,1)S(1)}, u32[]{:S(2)}, u32[]{:S(2)}) collective-permute-start(bf16[1024,256]{1,0:T(8,128)(2,1)S(1)} %slice.36), channel_id=1, source_target_pairs={{0,128},{128,256},{256,384},{1,129},{129,257},{257,385},{2,130},{1... | collective-permute-start | bytes 1572872 | tf_op jit(solution)/shard_map/ppermute | solution.py:400
  75.4 1.6 %copy-start.1 = (bf16[128,16,512]{2,1,0:T(8,128)(2,1)S(1)}, bf16[128,16,512]{2,1,0:T(8,128)(2,1)}, u32[]{:S(2)}) copy-start(bf16[128,16,512]{2,1,0:T(8,128)(2,1)} %copy-done) | copy-start | bytes 6291460
  90.9 53.0 %all-to-all-start.1 = ((bf16[128,16,256]{2,1,0:T(8,128)(2,1)}), bf16[128,16,256]{2,1,0:T(8,128)(2,1)S(1)}, u32[]{:S(2)}, u32[]{:S(2)}) async-start(bf16[128,16,256]{2,1,0:T(8,128)(2,1)} %bitcast.11), calls=%async_computation.1 | async-start | bytes 2097152 | tf_op jit(solution)/shard_map/all_to_all | solution.py:403
  101.6 27.0 %collective-permute-start.1 = (f32[4,8,128]{2,1,0:T(8,128)S(1)}, f32[4,8,128]{2,1,0:T(8,128)S(1)}, u32[]{:S(2)}, u32[]{:S(2)}) collective-permute-start(f32[4,8,128]{2,1,0:T(8,128)S(1)} %get-tuple-element.17), channel_id=1, source_target_pairs={{0,64},{16,80},{32,96},{48,112},{64,0},{80,16},{96,32},{112,48},{1... | collective-permute-start | bytes 49160 | tf_op jit(solution)/shard_map/ppermute | solution.py:404
  128.6 11.3 %collective-permute-start.2 = (f32[2,8,128]{2,1,0:T(8,128)S(1)}, f32[2,8,128]{2,1,0:T(8,128)S(1)}, u32[]{:S(2)}, u32[]{:S(2)}) collective-permute-start(f32[2,8,128]{2,1,0:T(8,128)S(1)} %pad_maximum_fusion.1), channel_id=1, source_target_pairs={{0,16},{16,32},{32,48},{48,64},{64,80},{80,96},{96,112},{112,0},{1... | collective-permute-start | bytes 24584 | tf_op jit(solution)/shard_map/ppermute | solution.py:407
  133.4 7.7 %collective-permute-start.3 = (f32[2,8,128]{2,1,0:T(8,128)S(1)}, f32[2,8,128]{2,1,0:T(8,128)S(1)}, u32[]{:S(2)}, u32[]{:S(2)}) collective-permute-start(f32[2,8,128]{2,1,0:T(8,128)S(1)} %pad_maximum_fusion.2), channel_id=1, source_target_pairs={{0,32},{16,48},{32,64},{48,80},{64,96},{80,112},{96,0},{112,16},{1... | collective-permute-start | bytes 24584 | tf_op jit(solution)/shard_map/ppermute | solution.py:407
  135.4 8.6 %collective-permute-start.4 = (f32[2,8,128]{2,1,0:T(8,128)S(1)}, f32[2,8,128]{2,1,0:T(8,128)S(1)}, u32[]{:S(2)}, u32[]{:S(2)}) collective-permute-start(f32[2,8,128]{2,1,0:T(8,128)S(1)} %pad_maximum_fusion.3), channel_id=1, source_target_pairs={{0,48},{16,64},{32,80},{48,96},{64,112},{80,0},{96,16},{112,32},{1... | collective-permute-start | bytes 24584 | tf_op jit(solution)/shard_map/ppermute | solution.py:407

commit v9 on v7

--- a/solution.py
+++ b/solution.py
@@ -56,7 +56,7 @@
         out_specs=[smem, pl.BlockSpec(memory_space=pltpu.VMEM)],
         out_shape=[
             jax.ShapeDtypeStruct((BLOCKS + 1,), jnp.int32),
-            jax.ShapeDtypeStruct((12, TK), jnp.int32),
+            pltpu.VMEM((12, TK), jnp.int32),
         ],
         name="doc_bounds",
     )(lengths, row, base)
@@ -205,10 +205,6 @@
     return pltpu.make_async_copy(held_ref.at[i], out_ref.at[pl.ds(i * TQ, TQ)], sems.at[0, i])
 
 
-def part_copy(i, src_ref, dst_ref, sems):
-    return pltpu.make_async_copy(src_ref.at[i], dst_ref.at[i], sems.at[1, i])
-
-
 def keep(held_ref, i, result):
     result = result.astype(jnp.bfloat16)
     held_ref[i, :, 0:128] = result[0:TQ]
@@ -228,7 +224,7 @@
 
 
 def local_body(
-    low_ref, ends_ref, qkv_ref, out_ref, norm_ref, part_ref, held_ref, kept_ref, s_ref, sems
+    low_ref, ends_ref, qkv_ref, out_ref, norm_ref, part_ref, held_ref, s_ref, sems
 ):
     norm_ref[...] = jnp.zeros((128, 128), jnp.float32)
     rows = lambda j: pl.ds(pl.multiple_of(j * TK - HALO, TK), TK)
@@ -249,8 +245,12 @@
                 )
                 result = acc / total
                 norm = top * SCALE + jnp.log(total)
-                kept_ref[i, 0] = result
-                kept_ref[i, 1] = norm
+
+                @pl.when(i < HALO_BLOCKS)
+                def _():
+                    part_ref[i, 0] = result
+                    part_ref[i, 1] = norm
+
                 keep(held_ref, i, result)
                 keep_norm(norm_ref, i, norm)
 
@@ -260,10 +260,6 @@
         def _():
             out_copy(i, held_ref, out_ref, sems).start()
 
-        @pl.when(pair_low < HALO)
-        def _():
-            part_copy(i, kept_ref, part_ref, sems).start()
-
         return carry
 
     lax.fori_loop(0, BLOCKS, block, 0)
@@ -272,12 +268,6 @@
         @pl.when(low_ref[i // 2 * 2] >= HALO)
         def _():
             out_copy(i, held_ref, out_ref, sems).wait()
-
-        if i < HALO_BLOCKS:
-
-            @pl.when(low_ref[i // 2 * 2] < HALO)
-            def _():
-                part_copy(i, kept_ref, part_ref, sems).wait()
 
 
 def attend_local(low, ends, qkv):
@@ -286,35 +276,38 @@
     return pl.pallas_call(
         local_body,
         in_specs=[pl.BlockSpec(memory_space=pltpu.SMEM), vmem, vmem],
-        out_specs=[any_space, vmem, any_space],
+        out_specs=[any_space, vmem, vmem],
         out_shape=[
             jax.ShapeDtypeStruct((SPAN, 256), jnp.bfloat16),
-            jax.ShapeDtypeStruct((128, 128), jnp.float32),
-            jax.ShapeDtypeStruct((HALO_BLOCKS, 2, 2 * TQ, 128), jnp.float32),
+            pltpu.VMEM((128, 128), jnp.float32),
+            pltpu.VMEM((HALO_BLOCKS, 2, 2 * TQ, 128), jnp.float32),
         ],
         scratch_shapes=[
             pltpu.VMEM((BLOCKS, TQ, 256), jnp.bfloat16),
-            pltpu.VMEM((BLOCKS, 2, 2 * TQ, 128), jnp.float32),
             pltpu.VMEM((MOST_BLOCKS, 2 * TQ, TK), jnp.float32),
-            pltpu.SemaphoreType.DMA((2, BLOCKS)),
+            pltpu.SemaphoreType.DMA((1, BLOCKS)),
         ],
         name="attend_local",
-    )(low, ends, *in_vmem(qkv))
+    )(low, *in_vmem(ends), qkv)
 
 
 def halo_body(low_ref, ends_ref, qkv_ref, halo_ref, prev_ref, prev_norm, part_ref, *refs):
     out_ref, *norm_refs = refs[:9]
-    held_ref, kept_ref, s_ref, norm_acc, norm_t, sems = refs[9:]
-    for i in range(HALO_BLOCKS):
-
-        @pl.when(low_ref[i // 2 * 2] < HALO)
-        def _():
-            part_copy(i, part_ref, kept_ref, sems).start()
+    held_ref, q_ref, s_ref, norm_acc, norm_t, sems, q_sem = refs[9:]
+    q_copy = pltpu.make_async_copy(qkv_ref.at[pl.ds(0, HALO), pl.ds(0, 256)], q_ref, q_sem)
+
+    @pl.when(low_ref[0] < HALO)
+    def _():
+        q_copy.start()
 
     norm_acc[...] = prev_norm[...]
     rows = lambda j: pl.ds(pl.multiple_of(j * TK, TK), TK)
     keys_at = lambda j: halo_ref[rows(j), 0:128]
     values_at = lambda j: halo_ref[rows(j), 128:256]
+
+    @pl.when(low_ref[0] < HALO)
+    def _():
+        q_copy.wait()
 
     def pair(p, carry):
         pair_blocks = (2 * p, 2 * p + 1)
@@ -325,7 +318,7 @@
             @pl.when(count == blocks)
             def _():
                 top, total, acc = partial_softmax(
-                    [part for i in pair_blocks for part in head_parts(qkv_ref, i)],
+                    [part for i in pair_blocks for part in head_parts(q_ref, i)],
                     [positions(i) for i in pair_blocks],
                     j_low,
                     blocks,
@@ -335,15 +328,13 @@
                     values_at,
                     s_ref,
                 )
-                for i in pair_blocks:
-                    part_copy(i, part_ref, kept_ref, sems).wait()
                 for n, i in enumerate(pair_blocks):
                     at = slice(2 * n * TQ, 2 * (n + 1) * TQ)
-                    own, these = kept_ref[i, 1], top[at] * SCALE
+                    own, these = part_ref[i, 1], top[at] * SCALE
                     most = jnp.maximum(own, these)
                     own, these = jnp.exp(own - most), jnp.exp(these - most)
                     whole = own + total[at] * these
-                    keep(held_ref, i, (kept_ref[i, 0] * own + acc[at] * these) / whole)
+                    keep(held_ref, i, (part_ref[i, 0] * own + acc[at] * these) / whole)
                     out_copy(i, held_ref, out_ref, sems).start()
                     keep_norm(norm_acc, i, most + jnp.log(whole))
 
@@ -368,26 +359,27 @@
         in_specs=[
             pl.BlockSpec(memory_space=pltpu.SMEM),
             vmem,
-            vmem,
+            any_space,
             vmem,
             any_space,
             vmem,
-            any_space,
+            vmem,
         ],
         out_specs=[any_space] + [vmem] * 8,
         out_shape=[jax.ShapeDtypeStruct((SPAN, 256), jnp.bfloat16)]
         + [pltpu.VMEM((8, 128), jnp.float32)] * 8,
         scratch_shapes=[
             pltpu.VMEM((HALO_BLOCKS, TQ, 256), jnp.bfloat16),
-            pltpu.VMEM((HALO_BLOCKS, 2, 2 * TQ, 128), jnp.float32),
+            pltpu.VMEM((HALO, 256), jnp.bfloat16),
             pltpu.VMEM((HALO // TK, 4 * TQ, TK), jnp.float32),
             pltpu.VMEM((128, 128), jnp.float32),
             pltpu.VMEM((128, 128), jnp.float32),
-            pltpu.SemaphoreType.DMA((2, HALO_BLOCKS)),
+            pltpu.SemaphoreType.DMA((1, HALO_BLOCKS)),
+            pltpu.SemaphoreType.DMA,
         ],
         input_output_aliases={4: 0},
         name="attend_halo",
-    )(low, ends, *in_vmem(qkv, halo), out, norm, part)
+    )(low, *in_vmem(ends), qkv, *in_vmem(halo), out, *in_vmem(norm, part))
 
 
 def per_device(queries, keys, values, lengths):

time: 137 us -> 138 us (level)
  waiting for transfers between devices: 2.68 us -> 4.16 us
    unnamed x4 -> x2, local copies, waits for them, and re-layouts: 2.92 us -> 1.33 us
    ppermute x1, waiting for transfers between devices: 0.48 us -> 1.95 us  [per_device(): lax.ppermute(qkv[SPAN - HALO:, 256:512], 'x', [(i, i + 1) for i in range(...]
where the time goes in v9:
time: 138 us; the launch traced here: 137 us
  blocking collectives  70.4 us (51%)
  starting transfers between devices  41.3 us (30%)
  Pallas kernels  18.1 us (13%)
  waiting for transfers between devices  4.16 us (3%)
  local copies, waits for them, and re-layouts  2.16 us (2%)
    all_to_all x1, blocking collectives, per_device(): moved = lax.all_to_all(packed, PLANE, 0, 0, tiled=True)  70.4 us
    ppermute x7, starting transfers between devices, per_device(): lax.ppermute(pieces[d], 'z', [(i, (i + d) % 8) for i in range(8)])  29.9 us
    all_to_all x1, starting transfers between devices, per_device(): back = lax.all_to_all(out.reshape(128, 16, 256), PLANE, 0, 0, tiled=True)  9.97 us
    pallas_call x1, Pallas kernels, attend_local(): pl.pallas_call(local_body, in_specs=[pl.BlockSpec(memory_space=pltpu.SMEM...  9.34 us
    pallas_call x1, Pallas kernels, attend_halo(): pl.pallas_call(halo_body, in_specs=[pl.BlockSpec(memory_space=pltpu.SMEM)...  3.31 us
    pallas_call x1, Pallas kernels, pack(): pl.pallas_call(pack_body, in_specs=[pl.BlockSpec(memory_space=pl.ANY)] *...  2.9 us
  transfers between devices with their start and end apart: 9, of which 2 were waited for; matrix products, arithmetic and copies ran while one was open for 0% of the time, Pallas kernels for 8%

profile of v9, /device:TPU:6, one launch (start us, length us, event | category | flops | bytes accessed | tf_op | source)
XLA Modules:
  0.0 137.1 jit_solution(4406460532002032892)
XLA Ops:
  0.6 2.9 %pack.1 = bf16[8,16,16,512]{3,2,1,0:T(8,128)(2,1)} custom-call(bf16[8,16,4096]{2,1,0:T(8,128)(2,1)} %q_ref.1, bf16[8,16,2048]{2,1,0:T(8,128)(2,1)} %k_ref.1, bf16[8,16,2048]{2,1,0:T(8,128)(2,1)} %v_ref.1), custom_call_target="tpu_custom_call" | custom-call | tf_op jit(solution)/shard_map/pack/pallas_call | solution.py:94
  3.5 70.4 %all_to_all.10 = bf16[128,16,512]{2,1,0:T(8,128)(2,1)S(1)} all-to-all(bf16[128,16,512]{2,1,0:T(8,128)(2,1)} %bitcast.10), channel_id=1, replica_groups=mesh['x'=4,'z'=8,'y'=8,'c'=2] {'z','y','c'}, dimensions={0} | all-to-all | bytes 4194304 | tf_op jit(solution)/shard_map/all_to_all | solution.py:389
  73.9 1.3 copy-done
  75.2 0.8 slice.4
  76.1 1.5 %collective-permute-start = (bf16[1024,256]{1,0:T(8,128)(2,1)}, bf16[1024,256]{1,0:T(8,128)(2,1)S(1)}, u32[]{:S(2)}, u32[]{:S(2)}) collective-permute-start(bf16[1024,256]{1,0:T(8,128)(2,1)} %slice.4), channel_id=1, source_target_pairs={{0,128},{128,256},{256,384},{1,129},{129,257},{257,385},{2,130},{1... | collective-permute-start | bytes 1572872 | tf_op jit(solution)/shard_map/ppermute | solution.py:392
  77.5 1.5 %doc_bounds.1 = (s32[9]{0:T(128)}, s32[12,256]{1,0:T(8,128)S(1)}) custom-call(s32[8,32]{1,0:T(8,128)} %lengths_ref.1, s32[1]{0:T(128)} %bitcast.row_ref, s32[1]{0:T(128)} %bitcast.1.base_ref), custom_call_target="tpu_custom_call" | custom-call | tf_op jit(solution)/shard_map/doc_bounds/pallas_call | solution.py:53
  79.0 9.3 %attend_local.1 = (bf16[2048,256]{1,0:T(8,128)(2,1)}, f32[128,128]{1,0:T(8,128)S(1)}, f32[4,2,512,128]{3,2,1,0:T(8,128)S(1)}) custom-call(s32[9]{0:T(128)} %get-tuple-element.16.low_ref, s32[12,256]{1,0:T(8,128)S(1)} %get-tuple-element.17.ends_ref, bf16[2048,512]{1,0:T(8,128)(2,1)} %bitcast.8), custom_call_target="tpu_custom_call" | custom-call | tf_op jit(solution)/shard_map/attend_local/pallas_call | solution.py:276
  88.4 2.0 %collective-permute-done.halo_ref = bf16[1024,256]{1,0:T(8,128)(2,1)S(1)} collective-permute-done((bf16[1024,256]{1,0:T(8,128)(2,1)}, bf16[1024,256]{1,0:T(8,128)(2,1)S(1)}, u32[]{:S(2)}, u32[]{:S(2)}) %collective-permute-start) | collective-permute-done | bytes 524320 | tf_op jit(solution)/shard_map/ppermute | solution.py:392
  90.3 3.3 %attend_halo.1 = (bf16[2048,256]{1,0:T(8,128)(2,1)}, f32[8,128]{1,0:T(8,128)S(1)}, f32[8,128]{1,0:T(8,128)S(1)}, f32[8,128]{1,0:T(8,128)S(1)}, f32[8,128]{1,0:T(...) custom-call(s32[9]{0:T(128)} %get-tuple-element.16.low_ref, ...), custom_call_target="tpu_custom_call", output_to_operand_aliasing={{0}: (4, {})} | custom-call | tf_op jit(solution)/shard_map/attend_halo/pallas_call | solution.py:357
  93.6 10.0 %all-to-all-start.1 = ((bf16[128,16,256]{2,1,0:T(8,128)(2,1)}), bf16[128,16,256]{2,1,0:T(8,128)(2,1)S(1)}, u32[]{:S(2)}, u32[]{:S(2)}) async-start(bf16[128,16,256]{2,1,0:T(8,128)(2,1)} %bitcast.11), calls=%async_computation.1 | async-start | bytes 2097152 | tf_op jit(solution)/shard_map/all_to_all | solution.py:395
  103.6 3.0 %collective-permute-start.1 = (f32[8,128]{1,0:T(8,128)S(1)}, f32[8,128]{1,0:T(8,128)S(1)}, u32[]{:S(2)}, u32[]{:S(2)}) collective-permute-start(f32[8,128]{1,0:T(8,128)S(1)} %get-tuple-element.23), channel_id=1, source_target_pairs={{0,16},{16,32},{32,48},{48,64},{64,80},{80,96},{96,112},{112,0},{1... | collective-permute-start | bytes 12296 | tf_op jit(solution)/shard_map/ppermute | solution.py:397
  106.7 4.5 %collective-permute-start.2 = (f32[8,128]{1,0:T(8,128)S(1)}, f32[8,128]{1,0:T(8,128)S(1)}, u32[]{:S(2)}, u32[]{:S(2)}) collective-permute-start(f32[8,128]{1,0:T(8,128)S(1)} %get-tuple-element.24), channel_id=1, source_target_pairs={{0,32},{16,48},{32,64},{48,80},{64,96},{80,112},{96,0},{112,16},{1... | collective-permute-start | bytes 12296 | tf_op jit(solution)/shard_map/ppermute | solution.py:397
  111.2 4.9 %collective-permute-start.3 = (f32[8,128]{1,0:T(8,128)S(1)}, f32[8,128]{1,0:T(8,128)S(1)}, u32[]{:S(2)}, u32[]{:S(2)}) collective-permute-start(f32[8,128]{1,0:T(8,128)S(1)} %get-tuple-element.25), channel_id=1, source_target_pairs={{0,48},{16,64},{32,80},{48,96},{64,112},{80,0},{96,16},{112,32},{1... | collective-permute-start | bytes 12296 | tf_op jit(solution)/shard_map/ppermute | solution.py:397
  116.1 3.8 %collective-permute-start.4 = (f32[8,128]{1,0:T(8,128)S(1)}, f32[8,128]{1,0:T(8,128)S(1)}, u32[]{:S(2)}, u32[]{:S(2)}) collective-permute-start(f32[8,128]{1,0:T(8,128)S(1)} %get-tuple-element.26), channel_id=1, source_target_pairs={{0,64},{16,80},{32,96},{48,112},{64,0},{80,16},{96,32},{112,48},{1... | collective-permute-start | bytes 12296 | tf_op jit(solution)/shard_map/ppermute | solution.py:397
  119.9 5.1 %collective-permute-start.5 = (f32[8,128]{1,0:T(8,128)S(1)}, f32[8,128]{1,0:T(8,128)S(1)}, u32[]{:S(2)}, u32[]{:S(2)}) collective-permute-start(f32[8,128]{1,0:T(8,128)S(1)} %get-tuple-element.27), channel_id=1, source_target_pairs={{0,80},{16,96},{32,112},{48,0},{64,16},{80,32},{96,48},{112,64},{1... | collective-permute-start | bytes 12296 | tf_op jit(solution)/shard_map/ppermute | solution.py:397
  125.0 0.0 collective-permute-done.1.refs_1_
  125.1 5.3 %collective-permute-start.6 = (f32[8,128]{1,0:T(8,128)S(1)}, f32[8,128]{1,0:T(8,128)S(1)}, u32[]{:S(2)}, u32[]{:S(2)}) collective-permute-start(f32[8,128]{1,0:T(8,128)S(1)} %get-tuple-element.28), channel_id=1, source_target_pairs={{0,96},{16,112},{32,0},{48,16},{64,32},{80,48},{96,64},{112,80},{1... | collective-permute-start | bytes 12296 | tf_op jit(solution)/shard_map/ppermute | solution.py:397
  130.3 0.0 collective-permute-done.2.refs_2_
  130.3 3.3 %collective-permute-start.7 = (f32[8,128]{1,0:T(8,128)S(1)}, f32[8,128]{1,0:T(8,128)S(1)}, u32[]{:S(2)}, u32[]{:S(2)}) collective-permute-start(f32[8,128]{1,0:T(8,128)S(1)} %get-tuple-element.29), channel_id=1, source_target_pairs={{0,112},{16,0},{32,16},{48,32},{64,48},{80,64},{96,80},{112,96},{1... | collective-permute-start | bytes 12296 | tf_op jit(solution)/shard_map/ppermute | solution.py:397
  133.6 0.0 collective-permute-done.3.refs_3_
  133.6 0.0 collective-permute-done.4.refs_4_
  133.7 2.2 %collective-permute-done.7.refs_7_ = f32[8,128]{1,0:T(8,128)S(1)} collective-permute-done((f32[8,128]{1,0:T(8,128)S(1)}, f32[8,128]{1,0:T(8,128)S(1)}, u32[]{:S(2)}, u32[]{:S(2)}) %collective-permute-start.7) | collective-permute-done | bytes 4128 | tf_op jit(solution)/shard_map/ppermute | solution.py:397
  135.8 0.0 all-to-all-done.1
  135.8 1.1 unpack.1
  (3 shorter events, 0.0 us)
Async XLA Ops:
  73.9 1.3 copy-start
  76.1 14.2 %collective-permute-start = (bf16[1024,256]{1,0:T(8,128)(2,1)}, bf16[1024,256]{1,0:T(8,128)(2,1)S(1)}, u32[]{:S(2)}, u32[]{:S(2)}) collective-permute-start(bf16[1024,256]{1,0:T(8,128)(2,1)} %slice.4), channel_id=1, source_target_pairs={{0,128},{128,256},{256,384},{1,129},{129,257},{257,385},{2,130},{1... | collective-permute-start | bytes 1572872 | tf_op jit(solution)/shard_map/ppermute | solution.py:392
  93.6 42.2 %all-to-all-start.1 = ((bf16[128,16,256]{2,1,0:T(8,128)(2,1)}), bf16[128,16,256]{2,1,0:T(8,128)(2,1)S(1)}, u32[]{:S(2)}, u32[]{:S(2)}) async-start(bf16[128,16,256]{2,1,0:T(8,128)(2,1)} %bitcast.11), calls=%async_computation.1 | async-start | bytes 2097152 | tf_op jit(solution)/shard_map/all_to_all | solution.py:395
  103.6 21.4 %collective-permute-start.1 = (f32[8,128]{1,0:T(8,128)S(1)}, f32[8,128]{1,0:T(8,128)S(1)}, u32[]{:S(2)}, u32[]{:S(2)}) collective-permute-start(f32[8,128]{1,0:T(8,128)S(1)} %get-tuple-element.23), channel_id=1, source_target_pairs={{0,16},{16,32},{32,48},{48,64},{64,80},{80,96},{96,112},{112,0},{1... | collective-permute-start | bytes 12296 | tf_op jit(solution)/shard_map/ppermute | solution.py:397
  106.7 23.7 %collective-permute-start.2 = (f32[8,128]{1,0:T(8,128)S(1)}, f32[8,128]{1,0:T(8,128)S(1)}, u32[]{:S(2)}, u32[]{:S(2)}) collective-permute-start(f32[8,128]{1,0:T(8,128)S(1)} %get-tuple-element.24), channel_id=1, source_target_pairs={{0,32},{16,48},{32,64},{48,80},{64,96},{80,112},{96,0},{112,16},{1... | collective-permute-start | bytes 12296 | tf_op jit(solution)/shard_map/ppermute | solution.py:397
  111.2 22.5 %collective-permute-start.3 = (f32[8,128]{1,0:T(8,128)S(1)}, f32[8,128]{1,0:T(8,128)S(1)}, u32[]{:S(2)}, u32[]{:S(2)}) collective-permute-start(f32[8,128]{1,0:T(8,128)S(1)} %get-tuple-element.25), channel_id=1, source_target_pairs={{0,48},{16,64},{32,80},{48,96},{64,112},{80,0},{96,16},{112,32},{1... | collective-permute-start | bytes 12296 | tf_op jit(solution)/shard_map/ppermute | solution.py:397
  116.1 17.5 %collective-permute-start.4 = (f32[8,128]{1,0:T(8,128)S(1)}, f32[8,128]{1,0:T(8,128)S(1)}, u32[]{:S(2)}, u32[]{:S(2)}) collective-permute-start(f32[8,128]{1,0:T(8,128)S(1)} %get-tuple-element.26), channel_id=1, source_target_pairs={{0,64},{16,80},{32,96},{48,112},{64,0},{80,16},{96,32},{112,48},{1... | collective-permute-start | bytes 12296 | tf_op jit(solution)/shard_map/ppermute | solution.py:397
  119.9 13.7 %collective-permute-start.5 = (f32[8,128]{1,0:T(8,128)S(1)}, f32[8,128]{1,0:T(8,128)S(1)}, u32[]{:S(2)}, u32[]{:S(2)}) collective-permute-start(f32[8,128]{1,0:T(8,128)S(1)} %get-tuple-element.27), channel_id=1, source_target_pairs={{0,80},{16,96},{32,112},{48,0},{64,16},{80,32},{96,48},{112,64},{1... | collective-permute-start | bytes 12296 | tf_op jit(solution)/shard_map/ppermute | solution.py:397
  125.1 8.6 %collective-permute-start.6 = (f32[8,128]{1,0:T(8,128)S(1)}, f32[8,128]{1,0:T(8,128)S(1)}, u32[]{:S(2)}, u32[]{:S(2)}) collective-permute-start(f32[8,128]{1,0:T(8,128)S(1)} %get-tuple-element.28), channel_id=1, source_target_pairs={{0,96},{16,112},{32,0},{48,16},{64,32},{80,48},{96,64},{112,80},{1... | collective-permute-start | bytes 12296 | tf_op jit(solution)/shard_map/ppermute | solution.py:397
  130.3 5.5 %collective-permute-start.7 = (f32[8,128]{1,0:T(8,128)S(1)}, f32[8,128]{1,0:T(8,128)S(1)}, u32[]{:S(2)}, u32[]{:S(2)}) collective-permute-start(f32[8,128]{1,0:T(8,128)S(1)} %get-tuple-element.29), channel_id=1, source_target_pairs={{0,112},{16,0},{32,16},{48,32},{64,48},{80,64},{96,80},{112,96},{1... | collective-permute-start | bytes 12296 | tf_op jit(solution)/shard_map/ppermute | solution.py:397
